TPU v7x, 32 devices: a whole 2x2x4 slice. The times are simulated.
32 devices in a mesh: gx: 2 (over y), gy: 16 (over z, x, core).
Axes of the slice: x: 2, y: 2, z: 4, core: 2. Of those that a mesh axis runs over, the one named last changes fastest.
Arguments:
- density: float32 [2, 512, 4096], P(None, 'gx', 'gy'), may hold values from -6 to 6
- observed: float32 [512, 4096], P('gx', 'gy'), may hold values from -6 to 6
- stations: int32 [512, 4096], P('gx', 'gy'), may hold values 0 or 1
- layer_index: int32 [2], replicated, may hold values from 0 to 511
Outputs:
- predicted: float32 [512, 4096], P('gx', 'gy')
- residual: float32 [512, 4096], P('gx', 'gy')
- gradient: float32 [2, 512, 4096], P(None, 'gx', 'gy')
All inputs are finite; a program needn't handle non-finite values. No bound on the sum of `stations` on one device may be relied on, other than what follows from the above.
Results may differ from a plain program's by a relative error of at most 0.00016.
Values sent between devices are 32-bit elements; how exact they have to be, the bound alone decides.
No kernel may reach another device: no remote copies, remote signals or barrier semaphores. Data moves between devices by JAX's collectives and lax.ppermute only.
A program may use at most 64 MiB of HBM per device.

v0:
```python
import functools
import math

import jax
import jax.numpy as jnp
import ml_dtypes
import numpy as np
from jax import lax
from jax.experimental import pallas as pl
from jax.experimental.pallas import tpu as pltpu
from jax.sharding import PartitionSpec as P

RADIUS = 128
LAYERS_ALL = 512

F32 = jnp.float32
BF16 = jnp.bfloat16


def halves(table):
    table = table.astype(np.float32)
    high = table.astype(ml_dtypes.bfloat16)
    low = (table - high.astype(np.float32)).astype(ml_dtypes.bfloat16)
    return [high, low]


@functools.lru_cache(maxsize=None)
def tables(tile):
    length = 2 * tile
    half = tile // 2
    ticks = np.arange(tile)
    even = 2 * np.arange(half)
    odd = even + 1

    def angles(freqs):
        return (freqs[:, None] * ticks[None, :] % length) * (2.0 * math.pi / length)

    middle = even.copy()
    middle[0] = tile
    even_sin = np.sin(angles(even))
    even_sin[0] = np.cos(angles(middle))[0]
    basis = np.concatenate([np.cos(angles(even)), even_sin, np.cos(angles(odd)), np.sin(angles(odd))])
    fold = np.where(ticks == 0, 1.0, 2.0) * (ticks <= RADIUS)
    freqs = np.concatenate([even, middle, odd])
    weights = np.where((freqs == 0) | (freqs == tile), 1.0, 2.0) / length
    sides = np.cos(angles(freqs)) * fold[None, :] * weights[:, None]
    return halves(basis) + halves(basis.T) + halves(sides) + halves(sides.T)


def parts(value):
    high = value.astype(BF16)
    return high, (value - high.astype(F32)).astype(BF16)


def product(left, right):
    def dot(a, b):
        return jnp.dot(a, b, preferred_element_type=F32)

    return dot(left[0], right[0]) + (dot(left[0], right[1]) + dot(left[1], right[0]))


def pair(refs, *index):
    return refs[0][index], refs[1][index]


def spectrum(index, sides, sides_t, tile):
    rows = lax.broadcasted_iota(jnp.int32, (tile, tile), 0)
    cols = lax.broadcasted_iota(jnp.int32, (tile, tile), 1)
    depth = RADIUS * (0.375 + index.astype(F32) / LAYERS_ALL)
    depth2 = depth * depth
    square = (rows * rows + cols * cols).astype(F32) + depth2
    value = depth2 / (square * jnp.sqrt(square))
    first = product(parts(value), pair(sides_t, slice(None), slice(None)))
    return product(pair(sides, slice(None), slice(None)), parts(first))


def group(block, half):
    return slice(min(block, 2) * half, (min(block, 2) + 1) * half)


def forward_kernel(phases, tile, layers, scalars, density, *refs):
    basis, basis_t, sides, sides_t = refs[0:2], refs[2:4], refs[4:6], refs[6:8]
    spectra, own = refs[8:10]
    sends = refs[10:-3]
    total, spill_rows, spill_both = refs[-3:]
    half = tile // 2
    everything = slice(None)
    for layer in range(layers):
        spec = spectrum(scalars[2 + layer], sides, sides_t, tile)
        spectra[layer] = spec
        first = product(parts(density[layer]), pair(basis_t, everything, everything))
        field = product(pair(basis, everything, everything), parts(first))
        for a in range(4):
            for b in range(4):
                rows, cols = slice(a * half, (a + 1) * half), slice(b * half, (b + 1) * half)
                term = spec[group(a, half), group(b, half)] * field[rows, cols]
                total[rows, cols] = term if layer == 0 else total[rows, cols] + term
    low, high = slice(0, tile), slice(tile, 2 * tile)
    even = product(pair(basis_t, everything, low), parts(total[low, :]))
    odd = product(pair(basis_t, everything, high), parts(total[high, :]))
    plus, minus = even + odd, even - odd

    def columns(value):
        first = product(parts(value[:, low]), pair(basis, low, everything))
        second = product(parts(value[:, high]), pair(basis, high, everything))
        return first + second, first - second

    own_value, spill_cols_value = columns(plus)
    own[...] = own_value
    total[low, low] = spill_cols_value
    spill_rows[...], spill_both[...] = columns(minus)
    for ref, (px, py) in zip(sends, phases):
        if py is None:
            ref[...] = spill_rows[pl.ds(pl.multiple_of(scalars_off(scalars, 0, px), RADIUS), RADIUS), :]
        elif px is None:
            ref[...] = total[low, pl.ds(pl.multiple_of(scalars_off(scalars, 1, py), RADIUS), RADIUS)]
        else:
            ref[...] = spill_both[
                pl.ds(pl.multiple_of(scalars_off(scalars, 0, px), RADIUS), RADIUS),
                pl.ds(pl.multiple_of(scalars_off(scalars, 1, py), RADIUS), RADIUS),
            ]


def scalars_off(scalars, axis, phase):
    return jnp.where(scalars[axis] == phase, 0, RADIUS)


def own_slice(scalars, axis, phase):
    return pl.ds(pl.multiple_of(RADIUS - scalars_off(scalars, axis, phase), RADIUS), RADIUS)


def halo_slice(scalars, axis, phase):
    return pl.ds(pl.multiple_of(scalars_off(scalars, axis, phase), RADIUS), RADIUS)


def residual_kernel(phases, scalars, own, observed, stations, *refs):
    count = len(phases)
    received, (predicted, residual), sends = refs[:count], refs[count : count + 2], refs[count + 2 :]
    predicted[...] = own[...]

    def at(px, py):
        rows = slice(None) if px is None else own_slice(scalars, 0, px)
        cols = slice(None) if py is None else own_slice(scalars, 1, py)
        return rows, cols

    for ref, (px, py) in zip(received, phases):
        index = at(px, py)
        predicted[index] += ref[...]
    residual[...] = stations[...].astype(F32) * (predicted[...] - observed[...])
    for ref, (px, py) in zip(sends, phases):
        ref[...] = residual[at(px, py)]


def adjoint_kernel(phases, tile, layers, scalars, residual, spectra, *refs):
    count = len(phases)
    received = refs[:count]
    basis, basis_t = refs[count : count + 2], refs[count + 2 : count + 4]
    gradient, x01, x10, x11, held = refs[count + 4 :]
    half = tile // 2
    everything = slice(None)
    if len(phases) < 8:
        x01[...] = jnp.zeros_like(x01)
        x10[...] = jnp.zeros_like(x10)
        x11[...] = jnp.zeros_like(x11)
    for ref, (px, py) in zip(received, phases):
        if py is None:
            x10[halo_slice(scalars, 0, px), :] = ref[...]
        elif px is None:
            x01[:, halo_slice(scalars, 1, py)] = ref[...]
        else:
            x11[halo_slice(scalars, 0, px), halo_slice(scalars, 1, py)] = ref[...]
    low, high = slice(0, tile), slice(tile, 2 * tile)
    up_even, up_odd = residual[...] + x01[...], residual[...] - x01[...]
    down_even, down_odd = x10[...] + x11[...], x10[...] - x11[...]

    def rows_of(even, odd, which):
        first = product(parts(even), pair(basis_t, everything, low))
        second = product(parts(odd), pair(basis_t, everything, high))
        held[which, low] = product(pair(basis, which, everything), parts(first))
        held[which, high] = product(pair(basis, which, everything), parts(second))

    rows_of(up_even + down_even, up_odd + down_odd, low)
    rows_of(up_even - down_even, up_odd - down_odd, high)
    for layer in range(layers):

        def scaled(a):
            rows = slice(a * half, (a + 1) * half)
            return jnp.concatenate(
                [
                    spectra[layer, group(a, half), group(b, half)] * held[rows, b * half : (b + 1) * half]
                    for b in range(4)
                ],
                axis=1,
            )

        even = jnp.concatenate([scaled(0), scaled(1)], axis=0)
        odd = jnp.concatenate([scaled(2), scaled(3)], axis=0)
        mid = product(pair(basis_t, everything, low), parts(even)) + product(
            pair(basis_t, everything, high), parts(odd)
        )
        gradient[layer] = product(parts(mid[:, low]), pair(basis, low, everything)) + product(
            parts(mid[:, high]), pair(basis, high, everything)
        )


def partner(index, phase):
    return index + 1 if index % 2 == phase else index - 1


def exchange(values, phases):
    nx, ny = lax.axis_size("gx"), lax.axis_size("gy")
    received = []
    for value, (px, py) in zip(values, phases):
        links = []
        for i in range(nx):
            for j in range(ny):
                x = i if px is None else partner(i, px)
                y = j if py is None else partner(j, py)
                if 0 <= x < nx and 0 <= y < ny:
                    links.append((i * ny + j, x * ny + y))
        received.append(lax.ppermute(value, ("gx", "gy"), links))
    return received


def body(density, observed, stations, layer_index):
    layers, tile = density.shape[0], density.shape[1]
    nx, ny = lax.axis_size("gx"), lax.axis_size("gy")
    xs = [phase for phase in range(2) if nx > 1 + phase]
    ys = [phase for phase in range(2) if ny > 1 + phase]
    phases = [(px, None) for px in xs] + [(None, py) for py in ys] + [(px, py) for px in xs for py in ys]

    def strip(px, py):
        shape = (tile if px is None else RADIUS, tile if py is None else RADIUS)
        return jax.ShapeDtypeStruct(shape, F32)

    strips = [strip(*phase) for phase in phases]
    consts = [jnp.asarray(table) for table in tables(tile)]
    scalars = jnp.concatenate(
        [jnp.stack([lax.axis_index("gx") % 2, lax.axis_index("gy") % 2]).astype(jnp.int32), layer_index]
    )
    smem = pl.BlockSpec(memory_space=pltpu.SMEM)
    vmem = pl.BlockSpec(memory_space=pltpu.VMEM)
    square = jax.ShapeDtypeStruct((tile, tile), F32)
    groups = 3 * (tile // 2)

    out = pl.pallas_call(
        functools.partial(forward_kernel, phases, tile, layers),
        out_shape=[jax.ShapeDtypeStruct((layers, groups, groups), F32), square] + strips,
        in_specs=[smem] + [vmem] * (1 + len(consts)),
        out_specs=[vmem] * (2 + len(strips)),
        scratch_shapes=[
            pltpu.VMEM((2 * tile, 2 * tile), F32),
            pltpu.VMEM((tile, tile), F32),
            pltpu.VMEM((tile, tile), F32),
        ],
        name="forward",
    )(scalars, density, *consts)
    spectra, own, sends = out[0], out[1], out[2:]
    received = exchange(sends, phases)
    out = pl.pallas_call(
        functools.partial(residual_kernel, phases),
        out_shape=[square, square] + strips,
        in_specs=[smem] + [vmem] * (3 + len(strips)),
        out_specs=[vmem] * (2 + len(strips)),
        name="residual",
    )(scalars, own, observed, stations, *received)
    predicted, residual, sends = out[0], out[1], out[2:]
    received = exchange(sends, phases)
    gradient = pl.pallas_call(
        functools.partial(adjoint_kernel, phases, tile, layers),
        out_shape=jax.ShapeDtypeStruct((layers, tile, tile), F32),
        in_specs=[smem] + [vmem] * (2 + len(strips) + 4),
        out_specs=vmem,
        scratch_shapes=[
            pltpu.VMEM((tile, tile), F32),
            pltpu.VMEM((tile, tile), F32),
            pltpu.VMEM((tile, tile), F32),
            pltpu.VMEM((2 * tile, 2 * tile), F32),
        ],
        name="adjoint",
    )(scalars, residual, spectra, *received, *consts[:4])
    return predicted, residual, gradient


def solution(mesh):
    in_specs = (P(None, "gx", "gy"), P("gx", "gy"), P("gx", "gy"), P())
    out_specs = (P("gx", "gy"), P("gx", "gy"), P(None, "gx", "gy"))
    return jax.shard_map(body, mesh=mesh, in_specs=in_specs, out_specs=out_specs, check_vma=False)
```

profile of v0, /device:TPU:17, one launch (start us, length us, event | category | flops | bytes accessed | tf_op | source)
XLA Modules:
  0.0 43.7 jit_solution(11805425590159626272)
XLA Ops:
  0.6 1.2 %pad_add_fusion.scalars = s32[4]{0:T(128)} fusion(s32[2]{0:T(128)} %param.15, s32[1]{0:T(128)} %bitcast.1, s32[1]{0:T(128)} %bitcast), kind=kLoop, calls=%fused_computation | loop fusion | flops 8 | bytes 32 | tf_op jit(solution)/shard_map/concatenate | solution.py:238
  1.9 6.8 %forward.1 = (f32[2,384,384]{2,1,0:T(8,128)}, f32[256,256]{1,0:T(8,128)}, f32[128,256]{1,0:T(8,128)}, f32[256,128]{1,0:T(8,128)}, f32[256,128]{1,0:T(8,128)}, /*index=5*/f32[128,128]{1,0:T(8,128)}, f32[128,128]{1,0:T(8,128)}) custom-call(s32[4]{0:T(128)} %pad_add_fusion.scalars, f32[2,256,256]{2,1,0:T(8,128)} %density.1, ...), custom_call_target="tpu_custom_call" | custom-call | tf_op jit(solution)/shard_map/forward/pallas_call | solution.py:246
  8.6 1.2 %collective-permute-start = (f32[128,256]{1,0:T(8,128)}, f32[128,256]{1,0:T(8,128)S(1)}, u32[]{:S(2)}, u32[]{:S(2)}) collective-permute-start(f32[128,256]{1,0:T(8,128)} %get-tuple-element.18), channel_id=1, source_target_pairs={{0,16},{1,17},{2,18},{3,19},{4,20},{5,21},{6,22},{7,23},{8,24},{9,... | collective-permute-start | bytes 393224 | tf_op jit(solution)/shard_map/ppermute | solution.py:221
  9.9 0.9 %collective-permute-start.1 = (f32[256,128]{1,0:T(8,128)}, f32[256,128]{1,0:T(8,128)S(1)}, u32[]{:S(2)}, u32[]{:S(2)}) collective-permute-start(f32[256,128]{1,0:T(8,128)} %get-tuple-element.19), channel_id=1, source_target_pairs={{0,1},{1,0},{2,3},{3,2},{4,5},{5,4},{6,7},{7,6},{8,9},{9,8},{10,11... | collective-permute-start | bytes 393224 | tf_op jit(solution)/shard_map/ppermute | solution.py:221
  10.8 3.0 %collective-permute-start.2 = (f32[256,128]{1,0:T(8,128)}, f32[256,128]{1,0:T(8,128)S(1)}, u32[]{:S(2)}, u32[]{:S(2)}) collective-permute-start(f32[256,128]{1,0:T(8,128)} %get-tuple-element.20), channel_id=1, source_target_pairs={{1,2},{2,1},{3,4},{4,3},{5,6},{6,5},{7,8},{8,7},{9,10},{10,9},{11,... | collective-permute-start | bytes 393224 | tf_op jit(solution)/shard_map/ppermute | solution.py:221
  13.8 0.6 %collective-permute-start.3 = (f32[128,128]{1,0:T(8,128)}, f32[128,128]{1,0:T(8,128)S(1)}, u32[]{:S(2)}, u32[]{:S(2)}) collective-permute-start(f32[128,128]{1,0:T(8,128)} %get-tuple-element.21), channel_id=1, source_target_pairs={{0,17},{1,16},{2,19},{3,18},{4,21},{5,20},{6,23},{7,22},{8,25},{9,... | collective-permute-start | bytes 196616 | tf_op jit(solution)/shard_map/ppermute | solution.py:221
  14.4 4.1 %collective-permute-start.4 = (f32[128,128]{1,0:T(8,128)}, f32[128,128]{1,0:T(8,128)S(1)}, u32[]{:S(2)}, u32[]{:S(2)}) collective-permute-start(f32[128,128]{1,0:T(8,128)} %get-tuple-element.22), channel_id=1, source_target_pairs={{1,18},{2,17},{3,20},{4,19},{5,22},{6,21},{7,24},{8,23},{9,26},{10... | collective-permute-start | bytes 196616 | tf_op jit(solution)/shard_map/ppermute | solution.py:221
  18.5 0.0 collective-permute-done.3.refs_3_
  18.5 0.0 copy-start.6
  18.6 3.2 %collective-permute-done.4.refs_4_ = f32[128,128]{1,0:T(8,128)S(1)} collective-permute-done((f32[128,128]{1,0:T(8,128)}, f32[128,128]{1,0:T(8,128)S(1)}, u32[]{:S(2)}, u32[]{:S(2)}) %collective-permute-start.4) | collective-permute-done | bytes 65568 | tf_op jit(solution)/shard_map/ppermute | solution.py:221
  21.8 0.0 copy-start.7
  21.8 0.0 collective-permute-done.refs_0_
  21.8 0.0 copy-start
  21.8 0.0 collective-permute-done.1.refs_1_
  21.8 0.0 copy-start.1
  21.8 0.0 collective-permute-done.2.refs_2_
  21.8 0.0 copy-start.2
  21.8 0.0 copy-done.6
  21.9 0.6 %copy-done.7 = f32[128,128]{1,0:T(8,128)} copy-done((f32[128,128]{1,0:T(8,128)}, f32[128,128]{1,0:T(8,128)S(1)}, u32[]{:S(2)}) %copy-start.7) | copy-done | bytes 65560
  22.4 0.1 copy-done
  22.5 0.1 copy-done.1
  22.5 0.1 copy-done.2
  22.6 2.3 %residual.1 = (f32[256,256]{1,0:T(8,128)}, f32[256,256]{1,0:T(8,128)}, f32[128,256]{1,0:T(8,128)}, f32[256,128]{1,0:T(8,128)}, f32[256,128]{1,0:T(8,128)}, /*index=5*/f32[128,128]{1,0:T(8,128)}, f32[128,128]{1,0:T(8,128)}) custom-call(s32[4]{0:T(128)} %pad_add_fusion.scalars, f32[256,256]{1,0:T(8,128)} %get-tuple-element.17.own, f32[256,256]{1,0:T(8,128)} %observed.1, ...), custom_call_target="tpu_custom_call" | custom-call | tf_op jit(solution)/shard_map/residual/pallas_call | solution.py:260
  24.9 1.2 %collective-permute-start.5 = (f32[128,256]{1,0:T(8,128)}, f32[128,256]{1,0:T(8,128)S(1)}, u32[]{:S(2)}, u32[]{:S(2)}) collective-permute-start(f32[128,256]{1,0:T(8,128)} %get-tuple-element.26), channel_id=1, source_target_pairs={{0,16},{1,17},{2,18},{3,19},{4,20},{5,21},{6,22},{7,23},{8,24},{9,... | collective-permute-start | bytes 393224 | tf_op jit(solution)/shard_map/ppermute | solution.py:221
  26.1 0.7 %collective-permute-start.6 = (f32[256,128]{1,0:T(8,128)}, f32[256,128]{1,0:T(8,128)S(1)}, u32[]{:S(2)}, u32[]{:S(2)}) collective-permute-start(f32[256,128]{1,0:T(8,128)} %get-tuple-element.27), channel_id=1, source_target_pairs={{0,1},{1,0},{2,3},{3,2},{4,5},{5,4},{6,7},{7,6},{8,9},{9,8},{10,11... | collective-permute-start | bytes 393224 | tf_op jit(solution)/shard_map/ppermute | solution.py:221
  26.8 2.7 %collective-permute-start.7 = (f32[256,128]{1,0:T(8,128)}, f32[256,128]{1,0:T(8,128)S(1)}, u32[]{:S(2)}, u32[]{:S(2)}) collective-permute-start(f32[256,128]{1,0:T(8,128)} %get-tuple-element.28), channel_id=1, source_target_pairs={{1,2},{2,1},{3,4},{4,3},{5,6},{6,5},{7,8},{8,7},{9,10},{10,9},{11,... | collective-permute-start | bytes 393224 | tf_op jit(solution)/shard_map/ppermute | solution.py:221
  29.6 0.1 collective-permute-start.8
  29.7 4.8 %collective-permute-start.9 = (f32[128,128]{1,0:T(8,128)}, f32[128,128]{1,0:T(8,128)S(1)}, u32[]{:S(2)}, u32[]{:S(2)}) collective-permute-start(f32[128,128]{1,0:T(8,128)} %get-tuple-element.30), channel_id=1, source_target_pairs={{1,18},{2,17},{3,20},{4,19},{5,22},{6,21},{7,24},{8,23},{9,26},{10... | collective-permute-start | bytes 196616 | tf_op jit(solution)/shard_map/ppermute | solution.py:221
  34.5 0.0 collective-permute-done.8.refs_3_
  34.5 0.0 copy-start.8
  34.5 2.8 %collective-permute-done.9.refs_4_ = f32[128,128]{1,0:T(8,128)S(1)} collective-permute-done((f32[128,128]{1,0:T(8,128)}, f32[128,128]{1,0:T(8,128)S(1)}, u32[]{:S(2)}, u32[]{:S(2)}) %collective-permute-start.9) | collective-permute-done | bytes 65568 | tf_op jit(solution)/shard_map/ppermute | solution.py:221
  37.4 0.0 copy-start.9
  37.4 0.0 collective-permute-done.5.refs_0_
  37.4 0.0 copy-start.3
  37.4 0.0 collective-permute-done.6.refs_1_
  37.4 0.0 copy-start.4
  37.4 0.0 collective-permute-done.7.refs_2_
  37.4 0.0 copy-start.5
  37.4 0.0 copy-done.8
  37.4 0.6 %copy-done.9 = f32[128,128]{1,0:T(8,128)} copy-done((f32[128,128]{1,0:T(8,128)}, f32[128,128]{1,0:T(8,128)S(1)}, u32[]{:S(2)}) %copy-start.9) | copy-done | bytes 65560
  38.0 0.1 copy-done.3
  38.0 0.0 copy-done.4
  38.1 0.1 copy-done.5
  38.1 5.6 %adjoint.1 = f32[2,256,256]{2,1,0:T(8,128)} custom-call(s32[4]{0:T(128)} %pad_add_fusion.scalars, f32[256,256]{1,0:T(8,128)} %get-tuple-element.15.residual, f32[2,384,384]{2,1,0:T(8,128)} %get-tuple-element.25.spectra, f32[128,256]{1,0:T(8,128)} %copy-done.3, f32[256,128]{1,0:T(8,128)} %copy-done.4, f32[256,128]{1,0:T(8,128)} %copy-done.5, ...), custom_call_target="tpu_custom_call" | custom-call | tf_op jit(solution)/shard_map/adjoint/pallas_call | solution.py:269
Async XLA Ops:
  8.6 13.2 %collective-permute-start = (f32[128,256]{1,0:T(8,128)}, f32[128,256]{1,0:T(8,128)S(1)}, u32[]{:S(2)}, u32[]{:S(2)}) collective-permute-start(f32[128,256]{1,0:T(8,128)} %get-tuple-element.18), channel_id=1, source_target_pairs={{0,16},{1,17},{2,18},{3,19},{4,20},{5,21},{6,22},{7,23},{8,24},{9,... | collective-permute-start | bytes 393224 | tf_op jit(solution)/shard_map/ppermute | solution.py:221
  9.9 11.9 %collective-permute-start.1 = (f32[256,128]{1,0:T(8,128)}, f32[256,128]{1,0:T(8,128)S(1)}, u32[]{:S(2)}, u32[]{:S(2)}) collective-permute-start(f32[256,128]{1,0:T(8,128)} %get-tuple-element.19), channel_id=1, source_target_pairs={{0,1},{1,0},{2,3},{3,2},{4,5},{5,4},{6,7},{7,6},{8,9},{9,8},{10,11... | collective-permute-start | bytes 393224 | tf_op jit(solution)/shard_map/ppermute | solution.py:221
  10.8 11.0 %collective-permute-start.2 = (f32[256,128]{1,0:T(8,128)}, f32[256,128]{1,0:T(8,128)S(1)}, u32[]{:S(2)}, u32[]{:S(2)}) collective-permute-start(f32[256,128]{1,0:T(8,128)} %get-tuple-element.20), channel_id=1, source_target_pairs={{1,2},{2,1},{3,4},{4,3},{5,6},{6,5},{7,8},{8,7},{9,10},{10,9},{11,... | collective-permute-start | bytes 393224 | tf_op jit(solution)/shard_map/ppermute | solution.py:221
  13.8 4.7 %collective-permute-start.3 = (f32[128,128]{1,0:T(8,128)}, f32[128,128]{1,0:T(8,128)S(1)}, u32[]{:S(2)}, u32[]{:S(2)}) collective-permute-start(f32[128,128]{1,0:T(8,128)} %get-tuple-element.21), channel_id=1, source_target_pairs={{0,17},{1,16},{2,19},{3,18},{4,21},{5,20},{6,23},{7,22},{8,25},{9,... | collective-permute-start | bytes 196616 | tf_op jit(solution)/shard_map/ppermute | solution.py:221
  14.4 7.4 %collective-permute-start.4 = (f32[128,128]{1,0:T(8,128)}, f32[128,128]{1,0:T(8,128)S(1)}, u32[]{:S(2)}, u32[]{:S(2)}) collective-permute-start(f32[128,128]{1,0:T(8,128)} %get-tuple-element.22), channel_id=1, source_target_pairs={{1,18},{2,17},{3,20},{4,19},{5,22},{6,21},{7,24},{8,23},{9,26},{10... | collective-permute-start | bytes 196616 | tf_op jit(solution)/shard_map/ppermute | solution.py:221
  18.5 3.3 %copy-start.6 = (f32[128,128]{1,0:T(8,128)}, f32[128,128]{1,0:T(8,128)S(1)}, u32[]{:S(2)}) copy-start(f32[128,128]{1,0:T(8,128)S(1)} %collective-permute-done.3.refs_3_) | copy-start | bytes 196612
  21.8 0.6 %copy-start.7 = (f32[128,128]{1,0:T(8,128)}, f32[128,128]{1,0:T(8,128)S(1)}, u32[]{:S(2)}) copy-start(f32[128,128]{1,0:T(8,128)S(1)} %collective-permute-done.4.refs_4_) | copy-start | bytes 196612
  21.8 0.7 %copy-start = (f32[128,256]{1,0:T(8,128)}, f32[128,256]{1,0:T(8,128)S(1)}, u32[]{:S(2)}) copy-start(f32[128,256]{1,0:T(8,128)S(1)} %collective-permute-done.refs_0_) | copy-start | bytes 393220
  21.8 0.7 %copy-start.1 = (f32[256,128]{1,0:T(8,128)}, f32[256,128]{1,0:T(8,128)S(1)}, u32[]{:S(2)}) copy-start(f32[256,128]{1,0:T(8,128)S(1)} %collective-permute-done.1.refs_1_) | copy-start | bytes 393220
  21.8 0.8 %copy-start.2 = (f32[256,128]{1,0:T(8,128)}, f32[256,128]{1,0:T(8,128)S(1)}, u32[]{:S(2)}) copy-start(f32[256,128]{1,0:T(8,128)S(1)} %collective-permute-done.2.refs_2_) | copy-start | bytes 393220
  24.9 12.5 %collective-permute-start.5 = (f32[128,256]{1,0:T(8,128)}, f32[128,256]{1,0:T(8,128)S(1)}, u32[]{:S(2)}, u32[]{:S(2)}) collective-permute-start(f32[128,256]{1,0:T(8,128)} %get-tuple-element.26), channel_id=1, source_target_pairs={{0,16},{1,17},{2,18},{3,19},{4,20},{5,21},{6,22},{7,23},{8,24},{9,... | collective-permute-start | bytes 393224 | tf_op jit(solution)/shard_map/ppermute | solution.py:221
  26.1 11.3 %collective-permute-start.6 = (f32[256,128]{1,0:T(8,128)}, f32[256,128]{1,0:T(8,128)S(1)}, u32[]{:S(2)}, u32[]{:S(2)}) collective-permute-start(f32[256,128]{1,0:T(8,128)} %get-tuple-element.27), channel_id=1, source_target_pairs={{0,1},{1,0},{2,3},{3,2},{4,5},{5,4},{6,7},{7,6},{8,9},{9,8},{10,11... | collective-permute-start | bytes 393224 | tf_op jit(solution)/shard_map/ppermute | solution.py:221
  26.8 10.6 %collective-permute-start.7 = (f32[256,128]{1,0:T(8,128)}, f32[256,128]{1,0:T(8,128)S(1)}, u32[]{:S(2)}, u32[]{:S(2)}) collective-permute-start(f32[256,128]{1,0:T(8,128)} %get-tuple-element.28), channel_id=1, source_target_pairs={{1,2},{2,1},{3,4},{4,3},{5,6},{6,5},{7,8},{8,7},{9,10},{10,9},{11,... | collective-permute-start | bytes 393224 | tf_op jit(solution)/shard_map/ppermute | solution.py:221
  29.6 4.9 %collective-permute-start.8 = (f32[128,128]{1,0:T(8,128)}, f32[128,128]{1,0:T(8,128)S(1)}, u32[]{:S(2)}, u32[]{:S(2)}) collective-permute-start(f32[128,128]{1,0:T(8,128)} %get-tuple-element.29), channel_id=1, source_target_pairs={{0,17},{1,16},{2,19},{3,18},{4,21},{5,20},{6,23},{7,22},{8,25},{9,... | collective-permute-start | bytes 196616 | tf_op jit(solution)/shard_map/ppermute | solution.py:221
  29.7 7.7 %collective-permute-start.9 = (f32[128,128]{1,0:T(8,128)}, f32[128,128]{1,0:T(8,128)S(1)}, u32[]{:S(2)}, u32[]{:S(2)}) collective-permute-start(f32[128,128]{1,0:T(8,128)} %get-tuple-element.30), channel_id=1, source_target_pairs={{1,18},{2,17},{3,20},{4,19},{5,22},{6,21},{7,24},{8,23},{9,26},{10... | collective-permute-start | bytes 196616 | tf_op jit(solution)/shard_map/ppermute | solution.py:221
  34.5 2.9 %copy-start.8 = (f32[128,128]{1,0:T(8,128)}, f32[128,128]{1,0:T(8,128)S(1)}, u32[]{:S(2)}) copy-start(f32[128,128]{1,0:T(8,128)S(1)} %collective-permute-done.8.refs_3_) | copy-start | bytes 196612
  37.4 0.6 %copy-start.9 = (f32[128,128]{1,0:T(8,128)}, f32[128,128]{1,0:T(8,128)S(1)}, u32[]{:S(2)}) copy-start(f32[128,128]{1,0:T(8,128)S(1)} %collective-permute-done.9.refs_4_) | copy-start | bytes 196612
  37.4 0.7 %copy-start.3 = (f32[128,256]{1,0:T(8,128)}, f32[128,256]{1,0:T(8,128)S(1)}, u32[]{:S(2)}) copy-start(f32[128,256]{1,0:T(8,128)S(1)} %collective-permute-done.5.refs_0_) | copy-start | bytes 393220
  37.4 0.7 %copy-start.4 = (f32[256,128]{1,0:T(8,128)}, f32[256,128]{1,0:T(8,128)S(1)}, u32[]{:S(2)}) copy-start(f32[256,128]{1,0:T(8,128)S(1)} %collective-permute-done.6.refs_1_) | copy-start | bytes 393220
  37.4 0.7 %copy-start.5 = (f32[256,128]{1,0:T(8,128)}, f32[256,128]{1,0:T(8,128)S(1)}, u32[]{:S(2)}) copy-start(f32[256,128]{1,0:T(8,128)S(1)} %collective-permute-done.7.refs_2_) | copy-start | bytes 393220
where the time goes:
time: 44.2 us; the launch traced here: 43.7 us
  starting transfers between devices  19.5 us (44%)
  Pallas kernels  14.6 us (33%)
  waiting for transfers between devices  6.09 us (14%)
  local copies, waits for them, and re-layouts  1.47 us (3%)
  other arithmetic  1.24 us (3%)
  between operations  0.79 us (2%)
    ppermute x10, starting transfers between devices, exchange(): received.append(lax.ppermute(value, ('gx', 'gy'), links))  19.5 us
    pallas_call x1, Pallas kernels, body(): pl.pallas_call(functools.partial(forward_kernel, phases, tile, layers), o...  6.76 us
    ppermute x10, waiting for transfers between devices, exchange(): received.append(lax.ppermute(value, ('gx', 'gy'), links))  6.09 us
    pallas_call x1, Pallas kernels, body(): pl.pallas_call(functools.partial(adjoint_kernel, phases, tile, layers), o...  5.57 us
    pallas_call x1, Pallas kernels, body(): pl.pallas_call(functools.partial(residual_kernel, phases), out_shape=[squ...  2.31 us
    unnamed x20, local copies, waits for them, and re-layouts  1.47 us
    concatenate x1, other arithmetic, body(): jnp.concatenate([jnp.stack([lax.axis_index('gx') % 2, lax.axis_index('gy'...  1.24 us
  transfers between devices with their start and end apart: 10, of which 2 were waited for; matrix products, arithmetic and copies ran while one was open for 0% of the time, Pallas kernels for 0%

commit v1 on v0

v1 whole, which is shorter than its diff:
```python
import functools
import math

import jax
import jax.numpy as jnp
import ml_dtypes
import numpy as np
from jax import lax
from jax.experimental import pallas as pl
from jax.experimental.pallas import tpu as pltpu
from jax.sharding import PartitionSpec as P

RADIUS = 128
LAYERS_ALL = 512

F32 = jnp.float32
BF16 = jnp.bfloat16
PARAMS = pltpu.CompilerParams(vmem_limit_bytes=24 * 2**20)


def halves(table):
    table = table.astype(np.float32)
    high = table.astype(ml_dtypes.bfloat16)
    low = (table - high.astype(np.float32)).astype(ml_dtypes.bfloat16)
    return [high, low]


@functools.lru_cache(maxsize=None)
def tables(tile):
    length = 2 * tile
    half = tile // 2
    ticks = np.arange(tile)
    even = 2 * np.arange(half)
    odd = even + 1

    def angles(freqs):
        return (freqs[:, None] * ticks[None, :] % length) * (2.0 * math.pi / length)

    middle = even.copy()
    middle[0] = tile
    even_sin = np.sin(angles(even))
    even_sin[0] = np.cos(angles(middle))[0]
    basis = np.concatenate([np.cos(angles(even)), even_sin, np.cos(angles(odd)), np.sin(angles(odd))])
    fold = np.where(ticks == 0, 1.0, 2.0) * (ticks <= RADIUS)
    freqs = np.concatenate([even, middle, odd])
    weights = np.where((freqs == 0) | (freqs == tile), 1.0, 2.0) / length
    sides = np.cos(angles(freqs)) * fold[None, :] * weights[:, None]
    return halves(basis) + halves(basis.T) + halves(sides) + halves(sides.T)


def parts(value):
    high = value.astype(BF16)
    return high, (value - high.astype(F32)).astype(BF16)


def product(left, right):
    def dot(a, b):
        return jnp.dot(a, b, preferred_element_type=F32)

    return dot(left[0], right[0]) + (dot(left[0], right[1]) + dot(left[1], right[0]))


def pair(refs, *index):
    return refs[0][index], refs[1][index]


def side(axis, phase):
    return jnp.where((lax.axis_index(axis) & 1) == phase, 0, RADIUS)


def halo(axis, phase):
    return pl.ds(pl.multiple_of(side(axis, phase), RADIUS), RADIUS)


def edge(axis, phase):
    return pl.ds(pl.multiple_of(RADIUS - side(axis, phase), RADIUS), RADIUS)


def group(block, half):
    return slice(min(block, 2) * half, (min(block, 2) + 1) * half)


ALL = slice(None)


def spectrum_kernel(tile, layers, index_source, *refs):
    sources, spectra, held, index, sems = refs[:4], refs[4], refs[5:9], refs[9], refs[10]
    copies = [pltpu.make_async_copy(sources[k], held[k], sems.at[k]) for k in range(4)]
    copies.append(pltpu.make_async_copy(index_source, index, sems.at[4]))
    for copy in reversed(copies):
        copy.start()
    span = RADIUS + 8
    rows = lax.broadcasted_iota(jnp.int32, (span, tile), 0)
    cols = lax.broadcasted_iota(jnp.int32, (span, tile), 1)
    offsets = (rows * rows + cols * cols).astype(F32)
    copies[4].wait()
    values = []
    for layer in range(layers):
        depth = RADIUS * (0.375 + index[layer].astype(F32) / LAYERS_ALL)
        square = offsets + depth * depth
        values.append(depth * depth / (square * jnp.sqrt(square)))
    copies[2].wait()
    copies[3].wait()
    first = product(parts(jnp.concatenate(values, axis=0)), pair(held[2:], ALL, ALL))
    copies[0].wait()
    copies[1].wait()
    rest = jnp.zeros((tile - span, first.shape[1]), F32)
    for layer in range(layers):
        own = jnp.concatenate([first[layer * span : (layer + 1) * span], rest], axis=0)
        spectra[layer] = product(pair(held[:2], ALL, ALL), parts(own))


def forward_kernel(xs, ys, tile, layers, density, spectra, *refs):
    count = len(ys)
    received, basis, basis_t = refs[:count], refs[count : count + 2], refs[count + 2 : count + 4]
    own, spill = refs[count + 4 : count + 6]
    sends, (wrapped, total) = refs[count + 6 : -2], refs[-2:]
    half = tile // 2
    low, high = slice(0, tile), slice(tile, 2 * tile)
    if count < 2:
        wrapped[...] = jnp.zeros_like(wrapped)
    for ref, phase in zip(received, ys):
        for layer in range(layers):
            wrapped[layer * tile : (layer + 1) * tile, halo("gy", phase)] = ref[layer]
    field = jnp.concatenate([density[layer] for layer in range(layers)], axis=0)
    behind = wrapped[...]
    even = product(parts(field + behind), pair(basis_t, ALL, low))
    odd = product(parts(field - behind), pair(basis_t, ALL, high))
    for layer in range(layers):
        rows = slice(layer * tile, (layer + 1) * tile)
        both = jnp.concatenate([even[rows], odd[rows]], axis=1)
        value = product(pair(basis, ALL, ALL), parts(both))
        for a in range(4):
            for b in range(4):
                place = slice(a * half, (a + 1) * half), slice(b * half, (b + 1) * half)
                term = spectra[layer, group(a, half), group(b, half)] * value[place]
                total[place] = term if layer == 0 else total[place] + term
    mixed = product(parts(total[:, low]), pair(basis, low, ALL)) + product(
        parts(total[:, high]), pair(basis, high, ALL)
    )
    even = product(pair(basis_t, ALL, low), parts(mixed[low]))
    odd = product(pair(basis_t, ALL, high), parts(mixed[high]))
    own[...] = even + odd
    spill[...] = even - odd
    for ref, phase in zip(sends, xs):
        ref[:RADIUS] = own[edge("gx", phase)]
        ref[RADIUS:] = spill[halo("gx", phase)]


def residual_kernel(xs, ys, tile, own, spill, observed, stations, *refs):
    count = len(xs)
    received, strips = refs[:count], refs[count : 2 * count]
    predicted, residual, behind = refs[2 * count : 2 * count + 3]
    sends = refs[2 * count + 3 :]
    predicted[...] = own[...]
    if count < 2:
        behind[...] = jnp.zeros_like(behind)
    for ref, strip, phase in zip(received, strips, xs):
        predicted[edge("gx", phase)] += ref[RADIUS:]
        rows = halo("gx", phase)
        behind[rows] = strip[1] * (spill[rows] + ref[:RADIUS] - strip[0])
    residual[...] = stations[...].astype(F32) * (predicted[...] - observed[...])
    for ref, phase in zip(sends, ys):
        cols = edge("gy", phase)
        ref[:tile] = residual[:, cols]
        for k, other in enumerate(xs):
            start = tile + k * RADIUS
            ref[start : start + RADIUS] = behind[halo("gx", other), cols]


def adjoint_kernel(xs, ys, tile, layers, predicted, residual, behind, spectra, *refs):
    count = len(ys)
    received, basis, basis_t = refs[:count], refs[count : count + 2], refs[count + 2 : count + 4]
    predicted_out, residual_out, gradient = refs[count + 4 : count + 7]
    across, corner, held, result, sems = refs[count + 7 :]
    half = tile // 2
    low, high = slice(0, tile), slice(tile, 2 * tile)
    copies = [
        pltpu.make_async_copy(predicted, predicted_out, sems.at[0]),
        pltpu.make_async_copy(residual, residual_out, sems.at[1]),
    ]
    for copy in copies:
        copy.start()
    if count < 2:
        across[...] = jnp.zeros_like(across)
    if count < 2 or len(xs) < 2:
        corner[...] = jnp.zeros_like(corner)
    for ref, phase in zip(received, ys):
        cols = halo("gy", phase)
        across[:, cols] = ref[:tile]
        for k, other in enumerate(xs):
            start = tile + k * RADIUS
            corner[halo("gx", other), cols] = ref[start : start + RADIUS]
    up_even, up_odd = residual[...] + across[...], residual[...] - across[...]
    down_even, down_odd = behind[...] + corner[...], behind[...] - corner[...]
    even = jnp.concatenate([up_even + down_even, up_even - down_even], axis=0)
    odd = jnp.concatenate([up_odd + down_odd, up_odd - down_odd], axis=0)
    even = product(parts(even), pair(basis_t, ALL, low))
    odd = product(parts(odd), pair(basis_t, ALL, high))
    for rows in (low, high):
        both = jnp.concatenate([even[rows], odd[rows]], axis=1)
        held[rows] = product(pair(basis, rows, ALL), parts(both))
    for layer in range(layers):

        def scaled(a):
            rows = slice(a * half, (a + 1) * half)
            return jnp.concatenate(
                [
                    spectra[layer, group(a, half), group(b, half)] * held[rows, b * half : (b + 1) * half]
                    for b in range(4)
                ],
                axis=1,
            )

        scaled_rows = [scaled(a) for a in range(4)]
        whole = jnp.concatenate(scaled_rows, axis=0)
        mixed = product(parts(whole[:, low]), pair(basis, low, ALL)) + product(
            parts(whole[:, high]), pair(basis, high, ALL)
        )
        result[layer] = product(pair(basis_t, ALL, low), parts(mixed[low])) + product(
            pair(basis_t, ALL, high), parts(mixed[high])
        )
        copies.append(pltpu.make_async_copy(result.at[layer], gradient.at[layer], sems.at[2 + layer]))
        copies[-1].start()
    for copy in copies:
        copy.wait()


def partner(index, phase):
    return index + 1 if index % 2 == phase else index - 1


def swap(value, axis, phase):
    count = lax.axis_size(axis)
    links = [(i, partner(i, phase)) for i in range(count)]
    return lax.ppermute(value, axis, [link for link in links if 0 <= link[1] < count])


def in_hbm(value):
    return pltpu.with_memory_space_constraint(value, pltpu.HBM)


def phases(axis):
    return [phase for phase in (1, 0) if lax.axis_size(axis) > 1 + phase]


def cost(units, tile):
    flops = int(units * 6 * tile**3)
    return pl.CostEstimate(flops=flops, bytes_accessed=tile * tile * 16, transcendentals=0)


def body(density, observed, stations, layer_index):
    layers, tile = density.shape[0], density.shape[1]
    xs, ys = phases("gx"), phases("gy")
    groups = 3 * (tile // 2)
    consts = [jnp.asarray(table) for table in tables(tile)]
    basis, sides = consts[:4], consts[4:]
    vmem = pl.BlockSpec(memory_space=pltpu.VMEM)
    hbm = pl.BlockSpec(memory_space=pltpu.HBM)

    def array(*shape):
        return jax.ShapeDtypeStruct(shape, F32)

    def cols_of(phase):
        upper = (lax.axis_index("gy") & 1) == phase
        return jnp.where(upper, density[..., tile - RADIUS :], density[..., :RADIUS])

    def rows_of(phase):
        upper = (lax.axis_index("gx") & 1) == phase
        both = jnp.stack([observed, stations.astype(F32)])
        return jnp.where(upper, both[:, tile - RADIUS :], both[:, :RADIUS])

    density_halos = [swap(cols_of(phase), "gy", phase) for phase in ys]
    strips = [swap(rows_of(phase), "gx", phase) for phase in xs]
    spectra = pl.pallas_call(
        functools.partial(spectrum_kernel, tile, layers),
        out_shape=array(layers, groups, groups),
        in_specs=[hbm] * 5,
        out_specs=vmem,
        scratch_shapes=[pltpu.VMEM(table.shape, BF16) for table in sides]
        + [pltpu.SMEM((layers,), jnp.int32), pltpu.SemaphoreType.DMA((5,))],
        compiler_params=PARAMS,
        cost_estimate=cost(8, tile),
        name="spectrum",
    )(*[in_hbm(value) for value in (layer_index, *sides)])
    out = pl.pallas_call(
        functools.partial(forward_kernel, xs, ys, tile, layers),
        out_shape=[array(tile, tile)] * (2 + len(xs)),
        in_specs=[vmem] * (6 + len(ys)),
        out_specs=[vmem] * (2 + len(xs)),
        scratch_shapes=[pltpu.VMEM((layers * tile, tile), F32), pltpu.VMEM((2 * tile, 2 * tile), F32)],
        compiler_params=PARAMS,
        cost_estimate=cost(18, tile),
        name="forward",
    )(density, spectra, *density_halos, *basis)
    own, spill, sends = out[0], out[1], out[2:]
    received = [swap(value, "gx", phase) for value, phase in zip(sends, xs)]
    tall = tile + RADIUS * len(xs)
    out = pl.pallas_call(
        functools.partial(residual_kernel, xs, ys, tile),
        out_shape=[array(tile, tile)] * 3 + [array(tall, RADIUS)] * len(ys),
        in_specs=[vmem] * (4 + 2 * len(xs)),
        out_specs=[vmem] * (3 + len(ys)),
        compiler_params=PARAMS,
        cost_estimate=cost(1, tile),
        name="residual",
    )(own, spill, observed, stations, *received, *strips)
    predicted, residual, behind, sends = out[0], out[1], out[2], out[3:]
    received = [swap(value, "gy", phase) for value, phase in zip(sends, ys)]
    return pl.pallas_call(
        functools.partial(adjoint_kernel, xs, ys, tile, layers),
        out_shape=[array(tile, tile), array(tile, tile), array(layers, tile, tile)],
        in_specs=[vmem] * (8 + len(ys)),
        out_specs=[hbm] * 3,
        scratch_shapes=[
            pltpu.VMEM((tile, tile), F32),
            pltpu.VMEM((tile, tile), F32),
            pltpu.VMEM((2 * tile, 2 * tile), F32),
            pltpu.VMEM((layers, tile, tile), F32),
            pltpu.SemaphoreType.DMA((2 + layers,)),
        ],
        compiler_params=PARAMS,
        cost_estimate=cost(20, tile),
        name="adjoint",
    )(predicted, residual, behind, spectra, *received, *basis)


def solution(mesh):
    in_specs = (P(None, "gx", "gy"), P("gx", "gy"), P("gx", "gy"), P())
    out_specs = (P("gx", "gy"), P("gx", "gy"), P(None, "gx", "gy"))
    return jax.shard_map(body, mesh=mesh, in_specs=in_specs, out_specs=out_specs, check_vma=False)
```

time: 44.2 us -> 35.5 us (0.80)
  starting transfers between devices: 19.5 us -> 9.64 us
  waiting for transfers between devices: 6.09 us -> 14.3 us
  Pallas kernels: 14.6 us -> 9.39 us
  local copies, waits for them, and re-layouts: 1.47 us -> 0.04 us
    ppermute x10 -> x6, starting transfers between devices: 19.5 us -> 9.64 us  [swap(): lax.ppermute(value, axis, [link for link in links if 0 <= link[1] < count])]
    ppermute x10 -> x6, waiting for transfers between devices: 6.09 us -> 14.3 us  [swap(): lax.ppermute(value, axis, [link for link in links if 0 <= link[1] < count])]
    pallas_call x3 -> x4, Pallas kernels: 14.6 us -> 9.39 us  [the longest x1 4.4 us: body(): pl.pallas_call(functools.partial(adjoint_kernel, xs, ys, tile, layers), o...]
    unnamed x20 -> x14, local copies, waits for them, and re-layouts: 1.47 us -> 0.04 us
    concatenate x1 -> x0, other arithmetic: 1.24 us -> none  [body(): jnp.concatenate([jnp.stack([lax.axis_index('gx') % 2, lax.axis_index('gy'...]
    select_n x0 -> x2, other arithmetic: none -> 1.16 us  [the longest x1 1.12 us: cols_of(): return jnp.where(upper, density[..., tile - RADIUS:], density[..., :RADIUS])]
  transfers between devices with their start and end apart: 10 -> 6, of which waited for: 2 -> 3; matrix products, arithmetic and copies ran while one was open for 0% -> 0% of each run, Pallas kernels for 0% -> 14%
where the time goes in v1:
time: 35.5 us; the launch traced here: 35.4 us
  waiting for transfers between devices  14.3 us (40%)
  starting transfers between devices  9.64 us (27%)
  Pallas kernels  9.39 us (26%)
  other arithmetic  1.18 us (3%)
  between operations  0.8 us (2%)
    ppermute x6, waiting for transfers between devices, swap(): lax.ppermute(value, axis, [link for link in links if 0 <= link[1] < count])  14.3 us
    ppermute x6, starting transfers between devices, swap(): lax.ppermute(value, axis, [link for link in links if 0 <= link[1] < count])  9.64 us
    pallas_call x1, Pallas kernels, body(): pl.pallas_call(functools.partial(adjoint_kernel, xs, ys, tile, layers), o...  4.4 us
    pallas_call x1, Pallas kernels, body(): pl.pallas_call(functools.partial(forward_kernel, xs, ys, tile, layers), o...  2.6 us
    pallas_call x1, Pallas kernels, body(): pl.pallas_call(functools.partial(spectrum_kernel, tile, layers), out_shap...  2.21 us
    select_n x1, other arithmetic, cols_of(): return jnp.where(upper, density[..., tile - RADIUS:], density[..., :RADIUS])  1.12 us
  transfers between devices with their start and end apart: 6, of which 3 were waited for; matrix products, arithmetic and copies ran while one was open for 0% of the time, Pallas kernels for 14%

profile of v1, /device:TPU:17, one launch (start us, length us, event | category | flops | bytes accessed | tf_op | source)
XLA Modules:
  0.0 35.4 jit_solution(1607135851007627428)
XLA Ops:
  0.6 0.0 copy-start
  0.6 0.0 copy-start.1
  0.7 1.1 %slice_select_fusion = (f32[2,256,128]{2,1,0:T(8,128)S(1)}, f32[2,256,128]{2,1,0:T(8,128)S(1)}) fusion(f32[2,256,256]{2,1,0:T(8,128)} %density.1, pred[]{:T(512)S(6)} %eq.10, pred[]{:T(512)S(6)} %eq.9), kind=kLoop, calls=%fused_computation.6 | loop fusion | flops 131072 | bytes 1048578 | tf_op jit(solution)/shard_map/jit(_where)/select_n | solution.py:266
  1.8 0.7 %collective-permute-start.1 = (f32[2,256,128]{2,1,0:T(8,128)S(1)}, f32[2,256,128]{2,1,0:T(8,128)S(1)}, u32[]{:S(2)}, u32[]{:S(2)}) collective-permute-start(f32[2,256,128]{2,1,0:T(8,128)S(1)} %get-tuple-element.19), channel_id=1, source_target_pairs={{0,1},{1,0},{2,3},{3,2},{4,5},{5,4},{6,7},{7,6},{8,9},{9,8},{10,11... | collective-permute-start | bytes 786440 | tf_op jit(solution)/shard_map/ppermute | solution.py:236
  2.5 3.0 %collective-permute-start = (f32[2,256,128]{2,1,0:T(8,128)S(1)}, f32[2,256,128]{2,1,0:T(8,128)S(1)}, u32[]{:S(2)}, u32[]{:S(2)}) collective-permute-start(f32[2,256,128]{2,1,0:T(8,128)S(1)} %get-tuple-element.20), channel_id=1, source_target_pairs={{1,2},{2,1},{3,4},{4,3},{5,6},{6,5},{7,8},{8,7},{9,10},{10,9},{11,... | collective-permute-start | bytes 786440 | tf_op jit(solution)/shard_map/ppermute | solution.py:236
  5.5 0.0 copy-done
  5.6 0.0 copy-done.1
  5.6 0.0 copy-start.2
  5.7 0.0 copy-start.3
  5.7 0.0 copy-start.4
  5.7 0.0 copy-start.5
  5.7 0.0 copy-start.6
  5.7 1.3 %collective-permute-start.3 = (f32[2,128,256]{2,1,0:T(8,128)S(1)}, f32[2,128,256]{2,1,0:T(8,128)S(1)}, u32[]{:S(2)}, u32[]{:S(2)}) collective-permute-start(f32[2,128,256]{2,1,0:T(8,128)S(1)} %fusion.1), channel_id=1, source_target_pairs={{0,16},{16,0},{1,17},{17,1},{2,18},{18,2},{3,19},{19,3},{4,20},{20... | collective-permute-start | bytes 786440 | tf_op jit(solution)/shard_map/ppermute | solution.py:236
  7.0 2.2 %spectrum.1.spectra = f32[2,384,384]{2,1,0:T(8,128)S(1)} custom-call(s32[2]{0:T(128)} %index_source.1, bf16[384,256]{1,0:T(8,128)(2,1)} %constant.33.clone.refs_0_, bf16[384,256]{1,0:T(8,128)(2,1)} %constant.34.clone.refs_1_, bf16[256,384]{1,0:T(8,128)(2,1)} %constant.35.clone.refs_2_, bf16[256,384]{1,0:T(8,128)(2,1)} %constant.36.clone.refs_3_), custom_call_target="tpu_custom_call" | custom-call | flops 805306368 | bytes 1048576 | tf_op jit(solution)/shard_map/spectrum/pallas_call | solution.py:275
  9.2 0.0 collective-permute-done.1.refs_1_
  9.2 4.1 %collective-permute-done.refs_0_ = f32[2,256,128]{2,1,0:T(8,128)S(1)} collective-permute-done((f32[2,256,128]{2,1,0:T(8,128)S(1)}, f32[2,256,128]{2,1,0:T(8,128)S(1)}, u32[]{:S(2)}, u32[]{:S(2)}) %collective-permute-start) | collective-permute-done | bytes 262176 | tf_op jit(solution)/shard_map/ppermute | solution.py:236
  13.3 0.0 copy-done.2
  13.3 0.0 copy-done.3
  13.3 0.0 copy-done.4
  13.3 0.0 copy-done.5
  13.3 0.0 copy-done.6
  13.3 2.6 %forward.1 = (f32[256,256]{1,0:T(8,128)S(1)}, f32[256,256]{1,0:T(8,128)S(1)}, f32[256,256]{1,0:T(8,128)S(1)}) custom-call(f32[2,256,256]{2,1,0:T(8,128)S(1)} %copy-done.2, f32[2,384,384]{2,1,0:T(8,128)S(1)} %spectrum.1.spectra, f32[2,256,128]{2,1,0:T(8,128)S(1)} %collective-permute-done.refs_0_, f32[2,256,128]{2,1,0:T(8,128)S(1)} %collective-permute-done.1.refs_1_, ...), custom_call_target="tpu_custom_call" | custom-call | flops 1811939328 | bytes 1048576 | tf_op jit(solution)/shard_map/forward/pallas_call | solution.py:286
  15.9 1.3 %collective-permute-start.2 = (f32[256,256]{1,0:T(8,128)S(1)}, f32[256,256]{1,0:T(8,128)S(1)}, u32[]{:S(2)}, u32[]{:S(2)}) collective-permute-start(f32[256,256]{1,0:T(8,128)S(1)} %get-tuple-element.13), channel_id=1, source_target_pairs={{0,16},{16,0},{1,17},{17,1},{2,18},{18,2},{3,19},{19,3},{4,20},{20... | collective-permute-start | bytes 786440 | tf_op jit(solution)/shard_map/ppermute | solution.py:236
  17.2 0.0 collective-permute-done.3.refs_1_
  17.2 5.2 %collective-permute-done.2.refs_0_ = f32[256,256]{1,0:T(8,128)S(1)} collective-permute-done((f32[256,256]{1,0:T(8,128)S(1)}, f32[256,256]{1,0:T(8,128)S(1)}, u32[]{:S(2)}, u32[]{:S(2)}) %collective-permute-start.2) | collective-permute-done | bytes 262176 | tf_op jit(solution)/shard_map/ppermute | solution.py:236
  22.4 0.2 residual.1
  22.6 3.2 %collective-permute-start.4 = (f32[384,128]{1,0:T(8,128)S(1)}, f32[384,128]{1,0:T(8,128)S(1)}, u32[]{:S(2)}, u32[]{:S(2)}) collective-permute-start(f32[384,128]{1,0:T(8,128)S(1)} %get-tuple-element.17), channel_id=1, source_target_pairs={{1,2},{2,1},{3,4},{4,3},{5,6},{6,5},{7,8},{8,7},{9,10},{10,9},{11,... | collective-permute-start | bytes 589832 | tf_op jit(solution)/shard_map/ppermute | solution.py:236
  25.8 0.1 collective-permute-start.5
  25.9 5.1 %collective-permute-done.4.refs_0_ = f32[384,128]{1,0:T(8,128)S(1)} collective-permute-done((f32[384,128]{1,0:T(8,128)S(1)}, f32[384,128]{1,0:T(8,128)S(1)}, u32[]{:S(2)}, u32[]{:S(2)}) %collective-permute-start.4) | collective-permute-done | bytes 196640 | tf_op jit(solution)/shard_map/ppermute | solution.py:236
  31.0 0.0 collective-permute-done.5.refs_1_
  31.0 4.4 %adjoint.1 = (f32[256,256]{1,0:T(8,128)}, f32[256,256]{1,0:T(8,128)}, f32[2,256,256]{2,1,0:T(8,128)}) custom-call(f32[256,256]{1,0:T(8,128)S(1)} %get-tuple-element.14.predicted, f32[256,256]{1,0:T(8,128)S(1)} %get-tuple-element.15.residual, f32[256,256]{1,0:T(8,128)S(1)} %get-tuple-element.16.behind, f32[2,384,384]{2,1,0:T(8,128)S(1)} %spectrum.1.spectra, ...), custom_call_target="tpu_custom_call" | custom-call | flops 2013265920 | bytes 1048576 | tf_op jit(solution)/shard_map/adjoint/pallas_call | solution.py:310
  (2 shorter events, 0.1 us)
Async XLA Ops:
  0.6 4.9 %copy-start = (s32[256,256]{1,0:T(8,128)S(1)}, s32[256,256]{1,0:T(8,128)}, u32[]{:S(2)}) copy-start(s32[256,256]{1,0:T(8,128)} %stations.1) | copy-start | bytes 786436
  0.6 5.0 %copy-start.1 = (f32[256,256]{1,0:T(8,128)S(1)}, f32[256,256]{1,0:T(8,128)}, u32[]{:S(2)}) copy-start(f32[256,256]{1,0:T(8,128)} %observed.1) | copy-start | bytes 786436
  1.8 7.5 %collective-permute-start.1 = (f32[2,256,128]{2,1,0:T(8,128)S(1)}, f32[2,256,128]{2,1,0:T(8,128)S(1)}, u32[]{:S(2)}, u32[]{:S(2)}) collective-permute-start(f32[2,256,128]{2,1,0:T(8,128)S(1)} %get-tuple-element.19), channel_id=1, source_target_pairs={{0,1},{1,0},{2,3},{3,2},{4,5},{5,4},{6,7},{7,6},{8,9},{9,8},{10,11... | collective-permute-start | bytes 786440 | tf_op jit(solution)/shard_map/ppermute | solution.py:236
  2.5 10.8 %collective-permute-start = (f32[2,256,128]{2,1,0:T(8,128)S(1)}, f32[2,256,128]{2,1,0:T(8,128)S(1)}, u32[]{:S(2)}, u32[]{:S(2)}) collective-permute-start(f32[2,256,128]{2,1,0:T(8,128)S(1)} %get-tuple-element.20), channel_id=1, source_target_pairs={{1,2},{2,1},{3,4},{4,3},{5,6},{6,5},{7,8},{8,7},{9,10},{10,9},{11,... | collective-permute-start | bytes 786440 | tf_op jit(solution)/shard_map/ppermute | solution.py:236
  5.6 7.7 %copy-start.2 = (f32[2,256,256]{2,1,0:T(8,128)S(1)}, f32[2,256,256]{2,1,0:T(8,128)}, u32[]{:S(2)}) copy-start(f32[2,256,256]{2,1,0:T(8,128)} %density.1) | copy-start | bytes 1572868
  5.7 7.7 %copy-start.3 = (bf16[256,512]{1,0:T(8,128)(2,1)S(1)}, bf16[256,512]{1,0:T(8,128)(2,1)}, u32[]{:S(2)}) copy-start(bf16[256,512]{1,0:T(8,128)(2,1)} %constant.32.clone.refs_5_) | copy-start | bytes 786436
  5.7 7.6 %copy-start.4 = (bf16[256,512]{1,0:T(8,128)(2,1)S(1)}, bf16[256,512]{1,0:T(8,128)(2,1)}, u32[]{:S(2)}) copy-start(bf16[256,512]{1,0:T(8,128)(2,1)} %constant.31.clone.refs_4_) | copy-start | bytes 786436
  5.7 7.6 %copy-start.5 = (bf16[512,256]{1,0:T(8,128)(2,1)S(1)}, bf16[512,256]{1,0:T(8,128)(2,1)}, u32[]{:S(2)}) copy-start(bf16[512,256]{1,0:T(8,128)(2,1)} %constant.30.clone.refs_3_) | copy-start | bytes 786436
  5.7 7.6 %copy-start.6 = (bf16[512,256]{1,0:T(8,128)(2,1)S(1)}, bf16[512,256]{1,0:T(8,128)(2,1)}, u32[]{:S(2)}) copy-start(bf16[512,256]{1,0:T(8,128)(2,1)} %constant.29.clone.refs_2_) | copy-start | bytes 786436
  5.7 11.5 %collective-permute-start.3 = (f32[2,128,256]{2,1,0:T(8,128)S(1)}, f32[2,128,256]{2,1,0:T(8,128)S(1)}, u32[]{:S(2)}, u32[]{:S(2)}) collective-permute-start(f32[2,128,256]{2,1,0:T(8,128)S(1)} %fusion.1), channel_id=1, source_target_pairs={{0,16},{16,0},{1,17},{17,1},{2,18},{18,2},{3,19},{19,3},{4,20},{20... | collective-permute-start | bytes 786440 | tf_op jit(solution)/shard_map/ppermute | solution.py:236
  15.9 6.5 %collective-permute-start.2 = (f32[256,256]{1,0:T(8,128)S(1)}, f32[256,256]{1,0:T(8,128)S(1)}, u32[]{:S(2)}, u32[]{:S(2)}) collective-permute-start(f32[256,256]{1,0:T(8,128)S(1)} %get-tuple-element.13), channel_id=1, source_target_pairs={{0,16},{16,0},{1,17},{17,1},{2,18},{18,2},{3,19},{19,3},{4,20},{20... | collective-permute-start | bytes 786440 | tf_op jit(solution)/shard_map/ppermute | solution.py:236
  22.6 8.4 %collective-permute-start.4 = (f32[384,128]{1,0:T(8,128)S(1)}, f32[384,128]{1,0:T(8,128)S(1)}, u32[]{:S(2)}, u32[]{:S(2)}) collective-permute-start(f32[384,128]{1,0:T(8,128)S(1)} %get-tuple-element.17), channel_id=1, source_target_pairs={{1,2},{2,1},{3,4},{4,3},{5,6},{6,5},{7,8},{8,7},{9,10},{10,9},{11,... | collective-permute-start | bytes 589832 | tf_op jit(solution)/shard_map/ppermute | solution.py:236
  25.8 5.2 %collective-permute-start.5 = (f32[384,128]{1,0:T(8,128)S(1)}, f32[384,128]{1,0:T(8,128)S(1)}, u32[]{:S(2)}, u32[]{:S(2)}) collective-permute-start(f32[384,128]{1,0:T(8,128)S(1)} %get-tuple-element.18), channel_id=1, source_target_pairs={{0,1},{1,0},{2,3},{3,2},{4,5},{5,4},{6,7},{7,6},{8,9},{9,8},{10,11... | collective-permute-start | bytes 589832 | tf_op jit(solution)/shard_map/ppermute | solution.py:236

commit v2 on v1

--- a/solution.py
+++ b/solution.py
@@ -1,4 +1,5 @@
 import functools
+import itertools
 import math
 
 import jax
@@ -9,6 +10,7 @@
 from jax.experimental import pallas as pl
 from jax.experimental.pallas import tpu as pltpu
 from jax.sharding import PartitionSpec as P
+
 
 RADIUS = 128
 LAYERS_ALL = 512
@@ -110,14 +112,13 @@
         spectra[layer] = product(pair(held[:2], ALL, ALL), parts(own))
 
 
-def forward_kernel(xs, ys, tile, layers, density, spectra, *refs):
-    count = len(ys)
-    received, basis, basis_t = refs[:count], refs[count : count + 2], refs[count + 2 : count + 4]
-    own, spill = refs[count + 4 : count + 6]
-    sends, (wrapped, total) = refs[count + 6 : -2], refs[-2:]
+def forward_kernel(xs, ys, early, tile, layers, density, spectra, observed, stations, *refs):
+    received, refs = refs[: len(ys)], refs[len(ys) :]
+    basis, basis_t, (own, spill), refs = refs[:2], refs[2:4], refs[4:6], refs[6:]
+    sends, firsts, (wrapped, total) = refs[: 2 * len(xs)], refs[2 * len(xs) : -2], refs[-2:]
     half = tile // 2
     low, high = slice(0, tile), slice(tile, 2 * tile)
-    if count < 2:
+    if len(ys) < 2:
         wrapped[...] = jnp.zeros_like(wrapped)
     for ref, phase in zip(received, ys):
         for layer in range(layers):
@@ -142,54 +143,67 @@
     odd = product(pair(basis_t, ALL, high), parts(mixed[high]))
     own[...] = even + odd
     spill[...] = even - odd
-    for ref, phase in zip(sends, xs):
-        ref[:RADIUS] = own[edge("gx", phase)]
-        ref[RADIUS:] = spill[halo("gx", phase)]
-
-
-def residual_kernel(xs, ys, tile, own, spill, observed, stations, *refs):
+    for k, (phase, other) in enumerate(itertools.product(xs, (1, 0))):
+        sends[k][:RADIUS] = spill[halo("gx", phase), edge("gy", other)]
+        sends[k][RADIUS:] = own[edge("gx", phase), edge("gy", other)]
+    if early:
+        place = halo("gx", xs[0]), edge("gy", 1)
+        firsts[0][...] = stations[place].astype(F32) * (own[place] - observed[place])
+
+
+def side_kernel(xs, early, other, tile, own, spill, observed, stations, *refs):
     count = len(xs)
-    received, strips = refs[:count], refs[count : 2 * count]
-    predicted, residual, behind = refs[2 * count : 2 * count + 3]
-    sends = refs[2 * count + 3 :]
-    predicted[...] = own[...]
+    received, strips, refs = refs[:count], refs[count : 2 * count], refs[2 * count :]
+    (predicted, residual, behind), sends = refs[:3], refs[3:]
+    cols = edge("gy", other)
+    predicted[...] = own[:, cols]
     if count < 2:
         behind[...] = jnp.zeros_like(behind)
     for ref, strip, phase in zip(received, strips, xs):
-        predicted[edge("gx", phase)] += ref[RADIUS:]
+        predicted[edge("gx", phase)] += ref[:RADIUS]
         rows = halo("gx", phase)
-        behind[rows] = strip[1] * (spill[rows] + ref[:RADIUS] - strip[0])
-    residual[...] = stations[...].astype(F32) * (predicted[...] - observed[...])
-    for ref, phase in zip(sends, ys):
-        cols = edge("gy", phase)
-        ref[:tile] = residual[:, cols]
-        for k, other in enumerate(xs):
-            start = tile + k * RADIUS
-            ref[start : start + RADIUS] = behind[halo("gx", other), cols]
-
-
-def adjoint_kernel(xs, ys, tile, layers, predicted, residual, behind, spectra, *refs):
-    count = len(ys)
-    received, basis, basis_t = refs[:count], refs[count : count + 2], refs[count + 2 : count + 4]
-    predicted_out, residual_out, gradient = refs[count + 4 : count + 7]
-    across, corner, held, result, sems = refs[count + 7 :]
+        behind[rows] = strip[1, :, cols] * (spill[rows, cols] + ref[RADIUS:] - strip[0, :, cols])
+    residual[...] = stations[:, cols].astype(F32) * (predicted[...] - observed[:, cols])
+    for ref in sends:
+        if early and other:
+            ref[:RADIUS] = residual[edge("gx", xs[0])]
+        else:
+            ref[:tile] = residual[...]
+        for k, phase in enumerate(xs):
+            start = ref.shape[0] + (k - count) * RADIUS
+            ref[start : start + RADIUS] = behind[halo("gx", phase)]
+
+
+def adjoint_kernel(xs, ys, early, tile, layers, spectra, *refs):
+    halves, firsts, refs = (refs[:3], refs[3:6]), refs[6 : 6 + early], refs[6 + early :]
+    strips, basis, basis_t, refs = refs[: len(ys)], refs[len(ys) :][:2], refs[len(ys) :][2:4], refs[len(ys) + 4 :]
+    predicted_out, residual_out, gradient = refs[:3]
+    residual, behind, across, corner, held, result, sems = refs[3:]
     half = tile // 2
     low, high = slice(0, tile), slice(tile, 2 * tile)
-    copies = [
-        pltpu.make_async_copy(predicted, predicted_out, sems.at[0]),
-        pltpu.make_async_copy(residual, residual_out, sems.at[1]),
-    ]
+    copies = []
+    for k, other in enumerate((1, 0)):
+        cols = edge("gy", other)
+        copies.append(pltpu.make_async_copy(halves[k][0], predicted_out.at[:, cols], sems.at[2 * k]))
+        copies.append(pltpu.make_async_copy(halves[k][1], residual_out.at[:, cols], sems.at[2 * k + 1]))
     for copy in copies:
         copy.start()
-    if count < 2:
+    for k, other in enumerate((1, 0)):
+        residual[:, edge("gy", other)] = halves[k][1][...]
+        behind[:, edge("gy", other)] = halves[k][2][...]
+    if len(ys) < 2:
         across[...] = jnp.zeros_like(across)
-    if count < 2 or len(xs) < 2:
+    if len(ys) < 2 or len(xs) < 2:
         corner[...] = jnp.zeros_like(corner)
-    for ref, phase in zip(received, ys):
+    for ref, phase in zip(strips, ys):
         cols = halo("gy", phase)
-        across[:, cols] = ref[:tile]
+        if early and phase:
+            across[halo("gx", xs[0]), cols] = firsts[0][...]
+            across[edge("gx", xs[0]), cols] = ref[:RADIUS]
+        else:
+            across[:, cols] = ref[:tile]
         for k, other in enumerate(xs):
-            start = tile + k * RADIUS
+            start = ref.shape[0] + (k - len(xs)) * RADIUS
             corner[halo("gx", other), cols] = ref[start : start + RADIUS]
     up_even, up_odd = residual[...] + across[...], residual[...] - across[...]
     down_even, down_odd = behind[...] + corner[...], behind[...] - corner[...]
@@ -217,11 +231,18 @@
         mixed = product(parts(whole[:, low]), pair(basis, low, ALL)) + product(
             parts(whole[:, high]), pair(basis, high, ALL)
         )
-        result[layer] = product(pair(basis_t, ALL, low), parts(mixed[low])) + product(
-            pair(basis_t, ALL, high), parts(mixed[high])
-        )
-        copies.append(pltpu.make_async_copy(result.at[layer], gradient.at[layer], sems.at[2 + layer]))
-        copies[-1].start()
+        upper, lower = parts(mixed[low]), parts(mixed[high])
+        for k in range(2):
+            rows = slice(k * half, (k + 1) * half)
+            result[layer, rows] = product(pair(basis_t, rows, low), upper) + product(
+                pair(basis_t, rows, high), lower
+            )
+            copies.append(
+                pltpu.make_async_copy(
+                    result.at[layer, rows], gradient.at[layer, rows], sems.at[4 + 2 * layer + k]
+                )
+            )
+            copies[-1].start()
     for copy in copies:
         copy.wait()
 
@@ -283,46 +304,56 @@
         cost_estimate=cost(8, tile),
         name="spectrum",
     )(*[in_hbm(value) for value in (layer_index, *sides)])
+    early = int(len(xs) == 1 and 1 in ys)
+    operands = [density, spectra, observed, stations, *density_halos, *basis]
     out = pl.pallas_call(
-        functools.partial(forward_kernel, xs, ys, tile, layers),
-        out_shape=[array(tile, tile)] * (2 + len(xs)),
-        in_specs=[vmem] * (6 + len(ys)),
-        out_specs=[vmem] * (2 + len(xs)),
+        functools.partial(forward_kernel, xs, ys, early, tile, layers),
+        out_shape=[array(tile, tile)] * 2
+        + [array(2 * RADIUS, RADIUS)] * (2 * len(xs))
+        + [array(tile - RADIUS, RADIUS)] * early,
+        in_specs=[vmem] * len(operands),
+        out_specs=[vmem] * (2 + 2 * len(xs) + early),
         scratch_shapes=[pltpu.VMEM((layers * tile, tile), F32), pltpu.VMEM((2 * tile, 2 * tile), F32)],
         compiler_params=PARAMS,
         cost_estimate=cost(18, tile),
         name="forward",
-    )(density, spectra, *density_halos, *basis)
-    own, spill, sends = out[0], out[1], out[2:]
-    received = [swap(value, "gx", phase) for value, phase in zip(sends, xs)]
-    tall = tile + RADIUS * len(xs)
-    out = pl.pallas_call(
-        functools.partial(residual_kernel, xs, ys, tile),
-        out_shape=[array(tile, tile)] * 3 + [array(tall, RADIUS)] * len(ys),
-        in_specs=[vmem] * (4 + 2 * len(xs)),
-        out_specs=[vmem] * (3 + len(ys)),
-        compiler_params=PARAMS,
-        cost_estimate=cost(1, tile),
-        name="residual",
-    )(own, spill, observed, stations, *received, *strips)
-    predicted, residual, behind, sends = out[0], out[1], out[2], out[3:]
-    received = [swap(value, "gy", phase) for value, phase in zip(sends, ys)]
+    )(*operands)
+    own, spill, sends, firsts = out[0], out[1], out[2 : 2 + 2 * len(xs)], out[2 + 2 * len(xs) :]
+    sums = {other: [] for other in (1, 0)}
+    for value, (phase, other) in zip(sends, itertools.product(xs, (1, 0))):
+        sums[other].append(swap(value, "gx", phase))
+    firsts = [swap(value, "gy", 1) for value in firsts]
+    halves, received = [], []
+    for other in (1, 0):
+        operands = [own, spill, observed, stations, *sums[other], *strips]
+        there = int(other in ys)
+        tall = RADIUS * len(xs) + (RADIUS if early and other else tile)
+        out = pl.pallas_call(
+            functools.partial(side_kernel, xs, early, other, tile),
+            out_shape=[array(tile, RADIUS)] * 3 + [array(tall, RADIUS)] * there,
+            in_specs=[vmem] * len(operands),
+            out_specs=[vmem] * (3 + there),
+            compiler_params=PARAMS,
+            cost_estimate=cost(1, tile),
+        )(*operands)
+        halves += out[:3]
+        received += [swap(value, "gy", other) for value in out[3:]]
+    operands = [spectra, *halves, *firsts, *received, *basis]
     return pl.pallas_call(
-        functools.partial(adjoint_kernel, xs, ys, tile, layers),
+        functools.partial(adjoint_kernel, xs, ys, early, tile, layers),
         out_shape=[array(tile, tile), array(tile, tile), array(layers, tile, tile)],
-        in_specs=[vmem] * (8 + len(ys)),
+        in_specs=[vmem] * len(operands),
         out_specs=[hbm] * 3,
-        scratch_shapes=[
-            pltpu.VMEM((tile, tile), F32),
-            pltpu.VMEM((tile, tile), F32),
+        scratch_shapes=[pltpu.VMEM((tile, tile), F32)] * 4
+        + [
             pltpu.VMEM((2 * tile, 2 * tile), F32),
             pltpu.VMEM((layers, tile, tile), F32),
-            pltpu.SemaphoreType.DMA((2 + layers,)),
+            pltpu.SemaphoreType.DMA((4 + 2 * layers,)),
         ],
         compiler_params=PARAMS,
         cost_estimate=cost(20, tile),
         name="adjoint",
-    )(predicted, residual, behind, spectra, *received, *basis)
+    )(*operands)
 
 
 def solution(mesh):

time: 35.5 us -> 36.8 us (1.037)
  the two profiles are of different devices: /device:TPU:17 before, /device:TPU:1 now
where the time goes in v2:
time: 36.8 us; the launch traced here: 36.6 us
  starting transfers between devices  15.5 us (42%)
  waiting for transfers between devices  9.67 us (26%)
  Pallas kernels  9.42 us (26%)
  other arithmetic  1.18 us (3%)
  between operations  0.81 us (2%)
    ppermute x8, starting transfers between devices, swap(): lax.ppermute(value, axis, [link for link in links if 0 <= link[1] < count])  15.5 us
    ppermute x8, waiting for transfers between devices, swap(): lax.ppermute(value, axis, [link for link in links if 0 <= link[1] < count])  9.67 us
    pallas_call x1, Pallas kernels, body(): pl.pallas_call(functools.partial(adjoint_kernel, xs, ys, early, tile, lay...  4.42 us
    pallas_call x1, Pallas kernels, body(): pl.pallas_call(functools.partial(forward_kernel, xs, ys, early, tile, lay...  2.63 us
    pallas_call x1, Pallas kernels, body(): pl.pallas_call(functools.partial(spectrum_kernel, tile, layers), out_shap...  2.21 us
    select_n x1, other arithmetic, cols_of(): return jnp.where(upper, density[..., tile - RADIUS:], density[..., :RADIUS])  1.12 us
  transfers between devices with their start and end apart: 8, of which 4 were waited for; matrix products, arithmetic and copies ran while one was open for 0% of the time, Pallas kernels for 14%

profile of v2, /device:TPU:1, one launch (start us, length us, event | category | flops | bytes accessed | tf_op | source)
XLA Modules:
  0.0 36.6 jit_solution(17564439612517346957)
XLA Ops:
  0.6 0.0 copy-start
  0.6 0.0 copy-start.1
  0.7 1.1 %slice_select_fusion = (f32[2,256,128]{2,1,0:T(8,128)S(1)}, f32[2,256,128]{2,1,0:T(8,128)S(1)}) fusion(f32[2,256,256]{2,1,0:T(8,128)} %density.1, pred[]{:T(512)S(6)} %eq.10, pred[]{:T(512)S(6)} %eq.9), kind=kLoop, calls=%fused_computation.6 | loop fusion | flops 131072 | bytes 1048578 | tf_op jit(solution)/shard_map/jit(_where)/select_n | solution.py:287
  1.8 0.1 collective-permute-start.1
  1.9 4.5 %collective-permute-start = (f32[2,256,128]{2,1,0:T(8,128)S(1)}, f32[2,256,128]{2,1,0:T(8,128)S(1)}, u32[]{:S(2)}, u32[]{:S(2)}) collective-permute-start(f32[2,256,128]{2,1,0:T(8,128)S(1)} %get-tuple-element.30), channel_id=1, source_target_pairs={{1,2},{2,1},{3,4},{4,3},{5,6},{6,5},{7,8},{8,7},{9,10},{10,9},{11,... | collective-permute-start | bytes 786440 | tf_op jit(solution)/shard_map/ppermute | solution.py:257
  6.4 0.0 copy-done
  6.4 0.0 copy-done.1
  6.5 0.0 copy-start.2
  6.5 0.0 copy-start.3
  6.5 0.0 copy-start.4
  6.5 0.0 copy-start.5
  6.5 0.0 copy-start.6
  6.5 1.3 %collective-permute-start.3 = (f32[2,128,256]{2,1,0:T(8,128)S(1)}, f32[2,128,256]{2,1,0:T(8,128)S(1)}, u32[]{:S(2)}, u32[]{:S(2)}) collective-permute-start(f32[2,128,256]{2,1,0:T(8,128)S(1)} %fusion.1), channel_id=1, source_target_pairs={{0,16},{16,0},{1,17},{17,1},{2,18},{18,2},{3,19},{19,3},{4,20},{20... | collective-permute-start | bytes 786440 | tf_op jit(solution)/shard_map/ppermute | solution.py:257
  7.8 2.2 %spectrum.1.spectra = f32[2,384,384]{2,1,0:T(8,128)S(1)} custom-call(s32[2]{0:T(128)} %index_source.1, bf16[384,256]{1,0:T(8,128)(2,1)} %constant.33.clone.refs_0_, bf16[384,256]{1,0:T(8,128)(2,1)} %constant.34.clone.refs_1_, bf16[256,384]{1,0:T(8,128)(2,1)} %constant.35.clone.refs_2_, bf16[256,384]{1,0:T(8,128)(2,1)} %constant.36.clone.refs_3_), custom_call_target="tpu_custom_call" | custom-call | flops 805306368 | bytes 1048576 | tf_op jit(solution)/shard_map/spectrum/pallas_call | solution.py:296
  10.1 0.0 collective-permute-done.1.refs_1_
  10.1 2.4 %collective-permute-done.refs_0_ = f32[2,256,128]{2,1,0:T(8,128)S(1)} collective-permute-done((f32[2,256,128]{2,1,0:T(8,128)S(1)}, f32[2,256,128]{2,1,0:T(8,128)S(1)}, u32[]{:S(2)}, u32[]{:S(2)}) %collective-permute-start) | collective-permute-done | bytes 262176 | tf_op jit(solution)/shard_map/ppermute | solution.py:257
  12.5 0.0 copy-done.2
  12.5 0.0 copy-done.3
  12.5 0.0 copy-done.4
  12.5 0.0 copy-done.5
  12.5 0.0 copy-done.6
  12.5 2.6 %forward.1 = (f32[256,256]{1,0:T(8,128)S(1)}, f32[256,256]{1,0:T(8,128)S(1)}, f32[256,128]{1,0:T(8,128)S(1)}, f32[256,128]{1,0:T(8,128)S(1)}, f32[128,128]{1,0:T(8,128)S(1)}) custom-call(f32[2,256,256]{2,1,0:T(8,128)S(1)} %copy-done.2, f32[2,384,384]{2,1,0:T(8,128)S(1)} %spectrum.1.spectra, f32[256,256]{1,0:T(8,128)S(1)} %copy-done.1, ...), custom_call_target="tpu_custom_call" | custom-call | flops 1811939328 | bytes 1048576 | tf_op jit(solution)/shard_map/forward/pallas_call | solution.py:309
  15.1 1.3 %collective-permute-start.4 = (f32[256,128]{1,0:T(8,128)S(1)}, f32[256,128]{1,0:T(8,128)S(1)}, u32[]{:S(2)}, u32[]{:S(2)}) collective-permute-start(f32[256,128]{1,0:T(8,128)S(1)} %get-tuple-element.22), channel_id=1, source_target_pairs={{0,16},{16,0},{1,17},{17,1},{2,18},{18,2},{3,19},{19,3},{4,20},{20... | collective-permute-start | bytes 393224 | tf_op jit(solution)/shard_map/ppermute | solution.py:257
  16.4 0.2 collective-permute-start.2
  16.7 0.0 collective-permute-done.3.refs_1_
  16.7 2.3 %collective-permute-done.4.refs_0_ = f32[256,128]{1,0:T(8,128)S(1)} collective-permute-done((f32[256,128]{1,0:T(8,128)S(1)}, f32[256,128]{1,0:T(8,128)S(1)}, u32[]{:S(2)}, u32[]{:S(2)}) %collective-permute-start.4) | collective-permute-done | bytes 131104 | tf_op jit(solution)/shard_map/ppermute | solution.py:257
  19.0 0.1 shard_map.140
  19.1 0.1 collective-permute-start.7
  19.2 1.2 %collective-permute-done.2.refs_0_ = f32[256,128]{1,0:T(8,128)S(1)} collective-permute-done((f32[256,128]{1,0:T(8,128)S(1)}, f32[256,128]{1,0:T(8,128)S(1)}, u32[]{:S(2)}, u32[]{:S(2)}) %collective-permute-start.2) | collective-permute-done | bytes 131104 | tf_op jit(solution)/shard_map/ppermute | solution.py:257
  20.4 0.1 shard_map.139
  20.5 6.1 %collective-permute-start.6 = (f32[256,128]{1,0:T(8,128)S(1)}, f32[256,128]{1,0:T(8,128)S(1)}, u32[]{:S(2)}, u32[]{:S(2)}) collective-permute-start(f32[256,128]{1,0:T(8,128)S(1)} %get-tuple-element.27), channel_id=1, source_target_pairs={{1,2},{2,1},{3,4},{4,3},{5,6},{6,5},{7,8},{8,7},{9,10},{10,9},{11,... | collective-permute-start | bytes 393224 | tf_op jit(solution)/shard_map/ppermute | solution.py:257
  26.6 1.9 %collective-permute-start.5 = (f32[128,128]{1,0:T(8,128)S(1)}, f32[128,128]{1,0:T(8,128)S(1)}, u32[]{:S(2)}, u32[]{:S(2)}) collective-permute-start(f32[128,128]{1,0:T(8,128)S(1)} %get-tuple-element.26), channel_id=1, source_target_pairs={{1,2},{2,1},{3,4},{4,3},{5,6},{6,5},{7,8},{8,7},{9,10},{10,9},{11,... | collective-permute-start | bytes 196616 | tf_op jit(solution)/shard_map/ppermute | solution.py:257
  28.5 3.7 %collective-permute-done.5.refs_6_ = f32[128,128]{1,0:T(8,128)S(1)} collective-permute-done((f32[128,128]{1,0:T(8,128)S(1)}, f32[128,128]{1,0:T(8,128)S(1)}, u32[]{:S(2)}, u32[]{:S(2)}) %collective-permute-start.5) | collective-permute-done | bytes 65568 | tf_op jit(solution)/shard_map/ppermute | solution.py:257
  32.1 0.0 collective-permute-done.6.refs_7_
  32.1 0.0 collective-permute-done.7.refs_8_
  32.2 4.4 %adjoint.1 = (f32[256,256]{1,0:T(8,128)}, f32[256,256]{1,0:T(8,128)}, f32[2,256,256]{2,1,0:T(8,128)}) custom-call(f32[2,384,384]{2,1,0:T(8,128)S(1)} %spectrum.1.spectra, f32[256,128]{1,0:T(8,128)S(1)} %get-tuple-element.19.refs_0_, f32[256,128]{1,0:T(8,128)S(1)} %get-tuple-element.20.refs_1_, f32[256,128]{1,0:T(8,128)S(1)} %get-tuple-element.21.refs_2_, ...), custom_call_target="tpu_custom_call" | custom-call | flops 2013265920 | bytes 1048576 | tf_op jit(solution)/shard_map/adjoint/pallas_call | solution.py:342
  (2 shorter events, 0.1 us)
Async XLA Ops:
  0.6 5.7 %copy-start = (s32[256,256]{1,0:T(8,128)S(1)}, s32[256,256]{1,0:T(8,128)}, u32[]{:S(2)}) copy-start(s32[256,256]{1,0:T(8,128)} %stations.5) | copy-start | bytes 786436
  0.6 5.8 %copy-start.1 = (f32[256,256]{1,0:T(8,128)S(1)}, f32[256,256]{1,0:T(8,128)}, u32[]{:S(2)}) copy-start(f32[256,256]{1,0:T(8,128)} %observed.5) | copy-start | bytes 786436
  1.8 8.3 %collective-permute-start.1 = (f32[2,256,128]{2,1,0:T(8,128)S(1)}, f32[2,256,128]{2,1,0:T(8,128)S(1)}, u32[]{:S(2)}, u32[]{:S(2)}) collective-permute-start(f32[2,256,128]{2,1,0:T(8,128)S(1)} %get-tuple-element.29), channel_id=1, source_target_pairs={{0,1},{1,0},{2,3},{3,2},{4,5},{5,4},{6,7},{7,6},{8,9},{9,8},{10,11... | collective-permute-start | bytes 786440 | tf_op jit(solution)/shard_map/ppermute | solution.py:257
  1.9 10.6 %collective-permute-start = (f32[2,256,128]{2,1,0:T(8,128)S(1)}, f32[2,256,128]{2,1,0:T(8,128)S(1)}, u32[]{:S(2)}, u32[]{:S(2)}) collective-permute-start(f32[2,256,128]{2,1,0:T(8,128)S(1)} %get-tuple-element.30), channel_id=1, source_target_pairs={{1,2},{2,1},{3,4},{4,3},{5,6},{6,5},{7,8},{8,7},{9,10},{10,9},{11,... | collective-permute-start | bytes 786440 | tf_op jit(solution)/shard_map/ppermute | solution.py:257
  6.5 6.0 %copy-start.2 = (f32[2,256,256]{2,1,0:T(8,128)S(1)}, f32[2,256,256]{2,1,0:T(8,128)}, u32[]{:S(2)}) copy-start(f32[2,256,256]{2,1,0:T(8,128)} %density.1) | copy-start | bytes 1572868
  6.5 6.0 %copy-start.3 = (bf16[256,512]{1,0:T(8,128)(2,1)S(1)}, bf16[256,512]{1,0:T(8,128)(2,1)}, u32[]{:S(2)}) copy-start(bf16[256,512]{1,0:T(8,128)(2,1)} %constant.32.clone.refs_5_.refs_12_) | copy-start | bytes 786436
  6.5 6.0 %copy-start.4 = (bf16[256,512]{1,0:T(8,128)(2,1)S(1)}, bf16[256,512]{1,0:T(8,128)(2,1)}, u32[]{:S(2)}) copy-start(bf16[256,512]{1,0:T(8,128)(2,1)} %constant.31.clone.refs_4_.refs_11_) | copy-start | bytes 786436
  6.5 6.0 %copy-start.5 = (bf16[512,256]{1,0:T(8,128)(2,1)S(1)}, bf16[512,256]{1,0:T(8,128)(2,1)}, u32[]{:S(2)}) copy-start(bf16[512,256]{1,0:T(8,128)(2,1)} %constant.30.clone.refs_3_.refs_10_) | copy-start | bytes 786436
  6.5 6.0 %copy-start.6 = (bf16[512,256]{1,0:T(8,128)(2,1)S(1)}, bf16[512,256]{1,0:T(8,128)(2,1)}, u32[]{:S(2)}) copy-start(bf16[512,256]{1,0:T(8,128)(2,1)} %constant.29.clone.refs_2_.refs_9_) | copy-start | bytes 786436
  6.5 10.1 %collective-permute-start.3 = (f32[2,128,256]{2,1,0:T(8,128)S(1)}, f32[2,128,256]{2,1,0:T(8,128)S(1)}, u32[]{:S(2)}, u32[]{:S(2)}) collective-permute-start(f32[2,128,256]{2,1,0:T(8,128)S(1)} %fusion.1), channel_id=1, source_target_pairs={{0,16},{16,0},{1,17},{17,1},{2,18},{18,2},{3,19},{19,3},{4,20},{20... | collective-permute-start | bytes 786440 | tf_op jit(solution)/shard_map/ppermute | solution.py:257
  15.1 3.9 %collective-permute-start.4 = (f32[256,128]{1,0:T(8,128)S(1)}, f32[256,128]{1,0:T(8,128)S(1)}, u32[]{:S(2)}, u32[]{:S(2)}) collective-permute-start(f32[256,128]{1,0:T(8,128)S(1)} %get-tuple-element.22), channel_id=1, source_target_pairs={{0,16},{16,0},{1,17},{17,1},{2,18},{18,2},{3,19},{19,3},{4,20},{20... | collective-permute-start | bytes 393224 | tf_op jit(solution)/shard_map/ppermute | solution.py:257
  16.4 4.0 %collective-permute-start.2 = (f32[256,128]{1,0:T(8,128)S(1)}, f32[256,128]{1,0:T(8,128)S(1)}, u32[]{:S(2)}, u32[]{:S(2)}) collective-permute-start(f32[256,128]{1,0:T(8,128)S(1)} %get-tuple-element.18), channel_id=1, source_target_pairs={{0,16},{16,0},{1,17},{17,1},{2,18},{18,2},{3,19},{19,3},{4,20},{20... | collective-permute-start | bytes 393224 | tf_op jit(solution)/shard_map/ppermute | solution.py:257
  19.1 13.1 %collective-permute-start.7 = (f32[384,128]{1,0:T(8,128)S(1)}, f32[384,128]{1,0:T(8,128)S(1)}, u32[]{:S(2)}, u32[]{:S(2)}) collective-permute-start(f32[384,128]{1,0:T(8,128)S(1)} %get-tuple-element.28), channel_id=1, source_target_pairs={{0,1},{1,0},{2,3},{3,2},{4,5},{5,4},{6,7},{7,6},{8,9},{9,8},{10,11... | collective-permute-start | bytes 589832 | tf_op jit(solution)/shard_map/ppermute | solution.py:257
  20.5 11.7 %collective-permute-start.6 = (f32[256,128]{1,0:T(8,128)S(1)}, f32[256,128]{1,0:T(8,128)S(1)}, u32[]{:S(2)}, u32[]{:S(2)}) collective-permute-start(f32[256,128]{1,0:T(8,128)S(1)} %get-tuple-element.27), channel_id=1, source_target_pairs={{1,2},{2,1},{3,4},{4,3},{5,6},{6,5},{7,8},{8,7},{9,10},{10,9},{11,... | collective-permute-start | bytes 393224 | tf_op jit(solution)/shard_map/ppermute | solution.py:257
  26.6 5.6 %collective-permute-start.5 = (f32[128,128]{1,0:T(8,128)S(1)}, f32[128,128]{1,0:T(8,128)S(1)}, u32[]{:S(2)}, u32[]{:S(2)}) collective-permute-start(f32[128,128]{1,0:T(8,128)S(1)} %get-tuple-element.26), channel_id=1, source_target_pairs={{1,2},{2,1},{3,4},{4,3},{5,6},{6,5},{7,8},{8,7},{9,10},{10,9},{11,... | collective-permute-start | bytes 196616 | tf_op jit(solution)/shard_map/ppermute | solution.py:257

commit v3 on v2

--- a/solution.py
+++ b/solution.py
@@ -174,12 +174,40 @@
             ref[start : start + RADIUS] = behind[halo("gx", phase)]
 
 
-def adjoint_kernel(xs, ys, early, tile, layers, spectra, *refs):
-    halves, firsts, refs = (refs[:3], refs[3:6]), refs[6 : 6 + early], refs[6 + early :]
-    strips, basis, basis_t, refs = refs[: len(ys)], refs[len(ys) :][:2], refs[len(ys) :][2:4], refs[len(ys) + 4 :]
-    predicted_out, residual_out, gradient = refs[:3]
-    residual, behind, across, corner, held, result, sems = refs[3:]
-    half = tile // 2
+def scaled(spectra, layer, value, half):
+    rows = []
+    for a in range(4):
+        blocks = [
+            spectra[layer, group(a, half), group(b, half)]
+            * value[a * half : (a + 1) * half, b * half : (b + 1) * half]
+            for b in range(4)
+        ]
+        rows.append(jnp.concatenate(blocks, axis=1))
+    return jnp.concatenate(rows, axis=0)
+
+
+def wide_product(left, right):
+    width = right[0].shape[1]
+    both = jnp.dot(left[0], jnp.concatenate(right, axis=1), preferred_element_type=F32)
+    return both[:, :width] + (both[:, width:] + jnp.dot(left[1], right[0], preferred_element_type=F32))
+
+
+def gradient_half(spectra, value, basis, basis_t, other, tile, layers):
+    low, high = slice(0, tile), slice(tile, 2 * tile)
+    table = pair(basis, ALL, edge("gy", other))
+    mixed = [wide_product(parts(scaled(spectra, layer, value, tile // 2)), table) for layer in range(layers)]
+    mixed = jnp.concatenate(mixed, axis=1)
+    return product(pair(basis_t, ALL, low), parts(mixed[low])) + product(
+        pair(basis_t, ALL, high), parts(mixed[high])
+    )
+
+
+def far_kernel(xs, paired, tile, layers, spectra, *refs):
+    halves, refs = (refs[:3], refs[3:6]), refs[6:]
+    strips, basis, basis_t = refs[: len(paired)], refs[len(paired) :][:2], refs[len(paired) :][2:4]
+    refs = refs[len(paired) + 4 :]
+    predicted_out, residual_out, field, result = refs[:4]
+    residual, behind, across, corner, sems = refs[4:]
     low, high = slice(0, tile), slice(tile, 2 * tile)
     copies = []
     for k, other in enumerate((1, 0)):
@@ -191,19 +219,13 @@
     for k, other in enumerate((1, 0)):
         residual[:, edge("gy", other)] = halves[k][1][...]
         behind[:, edge("gy", other)] = halves[k][2][...]
-    if len(ys) < 2:
-        across[...] = jnp.zeros_like(across)
-    if len(ys) < 2 or len(xs) < 2:
-        corner[...] = jnp.zeros_like(corner)
-    for ref, phase in zip(strips, ys):
+    across[...] = jnp.zeros_like(across)
+    corner[...] = jnp.zeros_like(corner)
+    for ref, phase in zip(strips, paired):
         cols = halo("gy", phase)
-        if early and phase:
-            across[halo("gx", xs[0]), cols] = firsts[0][...]
-            across[edge("gx", xs[0]), cols] = ref[:RADIUS]
-        else:
-            across[:, cols] = ref[:tile]
+        across[:, cols] = ref[:tile]
         for k, other in enumerate(xs):
-            start = ref.shape[0] + (k - len(xs)) * RADIUS
+            start = tile + k * RADIUS
             corner[halo("gx", other), cols] = ref[start : start + RADIUS]
     up_even, up_odd = residual[...] + across[...], residual[...] - across[...]
     down_even, down_odd = behind[...] + corner[...], behind[...] - corner[...]
@@ -213,36 +235,48 @@
     odd = product(parts(odd), pair(basis_t, ALL, high))
     for rows in (low, high):
         both = jnp.concatenate([even[rows], odd[rows]], axis=1)
-        held[rows] = product(pair(basis, rows, ALL), parts(both))
-    for layer in range(layers):
-
-        def scaled(a):
-            rows = slice(a * half, (a + 1) * half)
-            return jnp.concatenate(
-                [
-                    spectra[layer, group(a, half), group(b, half)] * held[rows, b * half : (b + 1) * half]
-                    for b in range(4)
-                ],
-                axis=1,
-            )
-
-        scaled_rows = [scaled(a) for a in range(4)]
-        whole = jnp.concatenate(scaled_rows, axis=0)
-        mixed = product(parts(whole[:, low]), pair(basis, low, ALL)) + product(
-            parts(whole[:, high]), pair(basis, high, ALL)
-        )
-        upper, lower = parts(mixed[low]), parts(mixed[high])
-        for k in range(2):
-            rows = slice(k * half, (k + 1) * half)
-            result[layer, rows] = product(pair(basis_t, rows, low), upper) + product(
-                pair(basis_t, rows, high), lower
-            )
-            copies.append(
-                pltpu.make_async_copy(
-                    result.at[layer, rows], gradient.at[layer, rows], sems.at[4 + 2 * layer + k]
-                )
-            )
+        field[rows] = product(pair(basis, rows, ALL), parts(both))
+    result[...] = gradient_half(spectra, field, basis, basis_t, 0, tile, layers)
+    for copy in copies:
+        copy.wait()
+
+
+def adjoint_kernel(xs, crossing, early, tile, layers, spectra, field, far, *refs):
+    firsts, refs = refs[:early], refs[early:]
+    strips, basis, basis_t = refs[: len(crossing)], refs[len(crossing) :][:2], refs[len(crossing) :][2:4]
+    gradient, across, corner, held, result, sems = refs[len(crossing) + 4 :]
+    low, high = slice(0, tile), slice(tile, 2 * tile)
+    copies = []
+
+    def put(source, first, other):
+        for layer in range(layers):
+            here = source.at[:, layer * RADIUS : (layer + 1) * RADIUS]
+            there = gradient.at[layer, :, edge("gy", other)]
+            copies.append(pltpu.make_async_copy(here, there, sems.at[first + layer]))
             copies[-1].start()
+
+    put(far, 0, 0)
+    for ref, phase in zip(strips, crossing):
+        if len(xs) < 2:
+            corner[...] = jnp.zeros_like(corner)
+        if early:
+            across[halo("gx", xs[0])] = firsts[0][...]
+            across[edge("gx", xs[0])] = ref[:RADIUS]
+        else:
+            across[...] = ref[:tile]
+        for k, other in enumerate(xs):
+            start = ref.shape[0] + (k - len(xs)) * RADIUS
+            corner[halo("gx", other)] = ref[start : start + RADIUS]
+        up = wide_product(pair(basis, low, ALL), parts(across[...] + corner[...]))
+        down = wide_product(pair(basis, high, ALL), parts(across[...] - corner[...]))
+        both = jnp.concatenate(parts(jnp.concatenate([up, down], axis=0)), axis=1)
+        ticks = halo("gy", phase)
+        upper, lower = (jnp.concatenate([table[ticks, :]] * 2, axis=0) for table in basis_t)
+        value = jnp.dot(both, upper, preferred_element_type=F32) + jnp.dot(both, lower, preferred_element_type=F32)
+        held[:, low] = field[:, low] + value[:, low]
+        held[:, high] = field[:, high] - value[:, high]
+    result[...] = gradient_half(spectra, held if crossing else field, basis, basis_t, 1, tile, layers)
+    put(result, layers, 1)
     for copy in copies:
         copy.wait()
 
@@ -338,22 +372,36 @@
         )(*operands)
         halves += out[:3]
         received += [swap(value, "gy", other) for value in out[3:]]
-    operands = [spectra, *halves, *firsts, *received, *basis]
-    return pl.pallas_call(
-        functools.partial(adjoint_kernel, xs, ys, early, tile, layers),
-        out_shape=[array(tile, tile), array(tile, tile), array(layers, tile, tile)],
+    crossing = [phase for phase in ys if phase]
+    paired = [phase for phase in ys if not phase]
+    operands = [spectra, *halves, *received[len(crossing) :], *basis]
+    predicted, residual, field, far = pl.pallas_call(
+        functools.partial(far_kernel, xs, paired, tile, layers),
+        out_shape=[array(tile, tile)] * 2 + [array(2 * tile, 2 * tile), array(tile, layers * RADIUS)],
         in_specs=[vmem] * len(operands),
-        out_specs=[hbm] * 3,
-        scratch_shapes=[pltpu.VMEM((tile, tile), F32)] * 4
+        out_specs=[hbm] * 2 + [vmem] * 2,
+        scratch_shapes=[pltpu.VMEM((tile, tile), F32)] * 4 + [pltpu.SemaphoreType.DMA((4,))],
+        compiler_params=PARAMS,
+        cost_estimate=cost(16, tile),
+        name="far",
+    )(*operands)
+    operands = [spectra, field, far, *firsts, *received[: len(crossing)], *basis]
+    gradient = pl.pallas_call(
+        functools.partial(adjoint_kernel, xs, crossing, early, tile, layers),
+        out_shape=array(layers, tile, tile),
+        in_specs=[vmem] * len(operands),
+        out_specs=hbm,
+        scratch_shapes=[pltpu.VMEM((tile, RADIUS), F32)] * 2
         + [
             pltpu.VMEM((2 * tile, 2 * tile), F32),
-            pltpu.VMEM((layers, tile, tile), F32),
-            pltpu.SemaphoreType.DMA((4 + 2 * layers,)),
+            pltpu.VMEM((tile, layers * RADIUS), F32),
+            pltpu.SemaphoreType.DMA((2 * layers,)),
         ],
         compiler_params=PARAMS,
-        cost_estimate=cost(20, tile),
+        cost_estimate=cost(12, tile),
         name="adjoint",
     )(*operands)
+    return predicted, residual, gradient
 
 
 def solution(mesh):

time: 36.8 us -> 36.7 us (level)
  the two profiles are of different devices: /device:TPU:1 before, /device:TPU:17 now
where the time goes in v3:
time: 36.7 us; the launch traced here: 36.5 us
  starting transfers between devices  16.2 us (44%)
  Pallas kernels  10.5 us (29%)
  waiting for transfers between devices  7.73 us (21%)
  other arithmetic  1.18 us (3%)
  between operations  0.85 us (2%)
    ppermute x8, starting transfers between devices, swap(): lax.ppermute(value, axis, [link for link in links if 0 <= link[1] < count])  16.2 us
    ppermute x8, waiting for transfers between devices, swap(): lax.ppermute(value, axis, [link for link in links if 0 <= link[1] < count])  7.73 us
    pallas_call x1, Pallas kernels, body(): pl.pallas_call(functools.partial(far_kernel, xs, paired, tile, layers), o...  2.93 us
    pallas_call x1, Pallas kernels, body(): pl.pallas_call(functools.partial(forward_kernel, xs, ys, early, tile, lay...  2.63 us
    pallas_call x1, Pallas kernels, body(): pl.pallas_call(functools.partial(adjoint_kernel, xs, crossing, early, til...  2.54 us
    pallas_call x1, Pallas kernels, body(): pl.pallas_call(functools.partial(spectrum_kernel, tile, layers), out_shap...  2.21 us
    select_n x1, other arithmetic, cols_of(): return jnp.where(upper, density[..., tile - RADIUS:], density[..., :RADIUS])  1.12 us
  transfers between devices with their start and end apart: 8, of which 3 were waited for; matrix products, arithmetic and copies ran while one was open for 0% of the time, Pallas kernels for 22%

profile of v3, /device:TPU:17, one launch (start us, length us, event | category | flops | bytes accessed | tf_op | source)
XLA Modules:
  0.0 36.5 jit_solution(7446799348985682480)
XLA Ops:
  0.6 0.0 copy-start
  0.6 0.0 copy-start.1
  0.7 1.1 %slice_select_fusion = (f32[2,256,128]{2,1,0:T(8,128)S(1)}, f32[2,256,128]{2,1,0:T(8,128)S(1)}) fusion(f32[2,256,256]{2,1,0:T(8,128)} %density.1, pred[]{:T(512)S(6)} %eq.10, pred[]{:T(512)S(6)} %eq.9), kind=kLoop, calls=%fused_computation.6 | loop fusion | flops 131072 | bytes 1048578 | tf_op jit(solution)/shard_map/jit(_where)/select_n | solution.py:321
  1.8 0.7 %collective-permute-start.1 = (f32[2,256,128]{2,1,0:T(8,128)S(1)}, f32[2,256,128]{2,1,0:T(8,128)S(1)}, u32[]{:S(2)}, u32[]{:S(2)}) collective-permute-start(f32[2,256,128]{2,1,0:T(8,128)S(1)} %get-tuple-element.37), channel_id=1, source_target_pairs={{0,1},{1,0},{2,3},{3,2},{4,5},{5,4},{6,7},{7,6},{8,9},{9,8},{10,11... | collective-permute-start | bytes 786440 | tf_op jit(solution)/shard_map/ppermute | solution.py:291
  2.5 3.0 %collective-permute-start = (f32[2,256,128]{2,1,0:T(8,128)S(1)}, f32[2,256,128]{2,1,0:T(8,128)S(1)}, u32[]{:S(2)}, u32[]{:S(2)}) collective-permute-start(f32[2,256,128]{2,1,0:T(8,128)S(1)} %get-tuple-element.38), channel_id=1, source_target_pairs={{1,2},{2,1},{3,4},{4,3},{5,6},{6,5},{7,8},{8,7},{9,10},{10,9},{11,... | collective-permute-start | bytes 786440 | tf_op jit(solution)/shard_map/ppermute | solution.py:291
  5.5 0.0 copy-done
  5.6 0.0 copy-done.1
  5.6 0.0 copy-start.2
  5.7 0.0 copy-start.3
  5.7 0.0 copy-start.4
  5.7 0.0 copy-start.5
  5.7 0.0 copy-start.6
  5.7 1.3 %collective-permute-start.3 = (f32[2,128,256]{2,1,0:T(8,128)S(1)}, f32[2,128,256]{2,1,0:T(8,128)S(1)}, u32[]{:S(2)}, u32[]{:S(2)}) collective-permute-start(f32[2,128,256]{2,1,0:T(8,128)S(1)} %fusion.1), channel_id=1, source_target_pairs={{0,16},{16,0},{1,17},{17,1},{2,18},{18,2},{3,19},{19,3},{4,20},{20... | collective-permute-start | bytes 786440 | tf_op jit(solution)/shard_map/ppermute | solution.py:291
  7.0 2.2 %spectrum.1.spectra = f32[2,384,384]{2,1,0:T(8,128)S(1)} custom-call(s32[2]{0:T(128)} %index_source.1, bf16[384,256]{1,0:T(8,128)(2,1)} %constant.33.clone.refs_0_, bf16[384,256]{1,0:T(8,128)(2,1)} %constant.34.clone.refs_1_, bf16[256,384]{1,0:T(8,128)(2,1)} %constant.35.clone.refs_2_, bf16[256,384]{1,0:T(8,128)(2,1)} %constant.36.clone.refs_3_), custom_call_target="tpu_custom_call" | custom-call | flops 805306368 | bytes 1048576 | tf_op jit(solution)/shard_map/spectrum/pallas_call | solution.py:330
  9.2 0.0 collective-permute-done.1.refs_1_
  9.2 4.1 %collective-permute-done.refs_0_ = f32[2,256,128]{2,1,0:T(8,128)S(1)} collective-permute-done((f32[2,256,128]{2,1,0:T(8,128)S(1)}, f32[2,256,128]{2,1,0:T(8,128)S(1)}, u32[]{:S(2)}, u32[]{:S(2)}) %collective-permute-start) | collective-permute-done | bytes 262176 | tf_op jit(solution)/shard_map/ppermute | solution.py:291
  13.3 0.0 copy-done.2
  13.3 0.0 copy-done.3
  13.3 0.0 copy-done.4
  13.3 0.0 copy-done.5
  13.3 0.0 copy-done.6
  13.3 2.6 %forward.1 = (f32[256,256]{1,0:T(8,128)S(1)}, f32[256,256]{1,0:T(8,128)S(1)}, f32[256,128]{1,0:T(8,128)S(1)}, f32[256,128]{1,0:T(8,128)S(1)}, f32[128,128]{1,0:T(8,128)S(1)}) custom-call(f32[2,256,256]{2,1,0:T(8,128)S(1)} %copy-done.2, f32[2,384,384]{2,1,0:T(8,128)S(1)} %spectrum.1.spectra, f32[256,256]{1,0:T(8,128)S(1)} %copy-done.1, ...), custom_call_target="tpu_custom_call" | custom-call | flops 1811939328 | bytes 1048576 | tf_op jit(solution)/shard_map/forward/pallas_call | solution.py:343
  16.0 1.3 %collective-permute-start.4 = (f32[256,128]{1,0:T(8,128)S(1)}, f32[256,128]{1,0:T(8,128)S(1)}, u32[]{:S(2)}, u32[]{:S(2)}) collective-permute-start(f32[256,128]{1,0:T(8,128)S(1)} %get-tuple-element.26), channel_id=1, source_target_pairs={{0,16},{16,0},{1,17},{17,1},{2,18},{18,2},{3,19},{19,3},{4,20},{20... | collective-permute-start | bytes 393224 | tf_op jit(solution)/shard_map/ppermute | solution.py:291
  17.3 0.0 collective-permute-done.3.refs_1_
  17.3 2.6 %collective-permute-done.4.refs_0_ = f32[256,128]{1,0:T(8,128)S(1)} collective-permute-done((f32[256,128]{1,0:T(8,128)S(1)}, f32[256,128]{1,0:T(8,128)S(1)}, u32[]{:S(2)}, u32[]{:S(2)}) %collective-permute-start.4) | collective-permute-done | bytes 131104 | tf_op jit(solution)/shard_map/ppermute | solution.py:291
  19.9 0.1 shard_map.140
  19.9 0.1 collective-permute-start.5
  20.0 1.3 %collective-permute-start.2 = (f32[256,128]{1,0:T(8,128)S(1)}, f32[256,128]{1,0:T(8,128)S(1)}, u32[]{:S(2)}, u32[]{:S(2)}) collective-permute-start(f32[256,128]{1,0:T(8,128)S(1)} %get-tuple-element.22), channel_id=1, source_target_pairs={{0,16},{16,0},{1,17},{17,1},{2,18},{18,2},{3,19},{19,3},{4,20},{20... | collective-permute-start | bytes 393224 | tf_op jit(solution)/shard_map/ppermute | solution.py:291
  21.3 4.2 %collective-permute-start.6 = (f32[128,128]{1,0:T(8,128)S(1)}, f32[128,128]{1,0:T(8,128)S(1)}, u32[]{:S(2)}, u32[]{:S(2)}) collective-permute-start(f32[128,128]{1,0:T(8,128)S(1)} %get-tuple-element.35), channel_id=1, source_target_pairs={{1,2},{2,1},{3,4},{4,3},{5,6},{6,5},{7,8},{8,7},{9,10},{10,9},{11,... | collective-permute-start | bytes 196616 | tf_op jit(solution)/shard_map/ppermute | solution.py:291
  25.5 0.0 collective-permute-done.2.refs_0_
  25.5 0.1 shard_map.139
  25.6 4.3 %collective-permute-start.7 = (f32[256,128]{1,0:T(8,128)S(1)}, f32[256,128]{1,0:T(8,128)S(1)}, u32[]{:S(2)}, u32[]{:S(2)}) collective-permute-start(f32[256,128]{1,0:T(8,128)S(1)} %get-tuple-element.36), channel_id=1, source_target_pairs={{1,2},{2,1},{3,4},{4,3},{5,6},{6,5},{7,8},{8,7},{9,10},{10,9},{11,... | collective-permute-start | bytes 393224 | tf_op jit(solution)/shard_map/ppermute | solution.py:291
  29.9 0.0 collective-permute-done.5.refs_6_
  29.9 2.9 %far.1 = (f32[256,256]{1,0:T(8,128)}, f32[256,256]{1,0:T(8,128)}, f32[512,512]{1,0:T(8,128)S(1)}, f32[256,256]{1,0:T(8,128)S(1)}) custom-call(f32[2,384,384]{2,1,0:T(8,128)S(1)} %spectrum.1.spectra, f32[256,128]{1,0:T(8,128)S(1)} %get-tuple-element.23.refs_0_, f32[256,128]{1,0:T(8,128)S(1)} %get-tuple-element.24.refs_1_, ...), custom_call_target="tpu_custom_call" | custom-call | flops 1610612736 | bytes 1048576 | tf_op jit(solution)/shard_map/far/pallas_call | solution.py:378
  32.8 0.0 collective-permute-done.6.refs_0_
  32.8 1.1 %collective-permute-done.7.refs_1_ = f32[256,128]{1,0:T(8,128)S(1)} collective-permute-done((f32[256,128]{1,0:T(8,128)S(1)}, f32[256,128]{1,0:T(8,128)S(1)}, u32[]{:S(2)}, u32[]{:S(2)}) %collective-permute-start.7) | collective-permute-done | bytes 131104 | tf_op jit(solution)/shard_map/ppermute | solution.py:291
  33.9 2.5 %adjoint.1 = f32[2,256,256]{2,1,0:T(8,128)} custom-call(f32[2,384,384]{2,1,0:T(8,128)S(1)} %spectrum.1.spectra, f32[512,512]{1,0:T(8,128)S(1)} %get-tuple-element.33.field, f32[256,256]{1,0:T(8,128)S(1)} %get-tuple-element.34.far, f32[128,128]{1,0:T(8,128)S(1)} %collective-permute-done.6.refs_0_, f32[256,128]{1,0:T(8,128)S(1)} %collective-permute-done.7.refs_1_, ...), custom_call_target="tpu_custom_call" | custom-call | flops 1207959552 | bytes 1048576 | tf_op jit(solution)/shard_map/adjoint/pallas_call | solution.py:389
  (2 shorter events, 0.1 us)
Async XLA Ops:
  0.6 4.9 %copy-start = (s32[256,256]{1,0:T(8,128)S(1)}, s32[256,256]{1,0:T(8,128)}, u32[]{:S(2)}) copy-start(s32[256,256]{1,0:T(8,128)} %stations.5) | copy-start | bytes 786436
  0.6 5.0 %copy-start.1 = (f32[256,256]{1,0:T(8,128)S(1)}, f32[256,256]{1,0:T(8,128)}, u32[]{:S(2)}) copy-start(f32[256,256]{1,0:T(8,128)} %observed.5) | copy-start | bytes 786436
  1.8 7.5 %collective-permute-start.1 = (f32[2,256,128]{2,1,0:T(8,128)S(1)}, f32[2,256,128]{2,1,0:T(8,128)S(1)}, u32[]{:S(2)}, u32[]{:S(2)}) collective-permute-start(f32[2,256,128]{2,1,0:T(8,128)S(1)} %get-tuple-element.37), channel_id=1, source_target_pairs={{0,1},{1,0},{2,3},{3,2},{4,5},{5,4},{6,7},{7,6},{8,9},{9,8},{10,11... | collective-permute-start | bytes 786440 | tf_op jit(solution)/shard_map/ppermute | solution.py:291
  2.5 10.8 %collective-permute-start = (f32[2,256,128]{2,1,0:T(8,128)S(1)}, f32[2,256,128]{2,1,0:T(8,128)S(1)}, u32[]{:S(2)}, u32[]{:S(2)}) collective-permute-start(f32[2,256,128]{2,1,0:T(8,128)S(1)} %get-tuple-element.38), channel_id=1, source_target_pairs={{1,2},{2,1},{3,4},{4,3},{5,6},{6,5},{7,8},{8,7},{9,10},{10,9},{11,... | collective-permute-start | bytes 786440 | tf_op jit(solution)/shard_map/ppermute | solution.py:291
  5.6 7.7 %copy-start.2 = (f32[2,256,256]{2,1,0:T(8,128)S(1)}, f32[2,256,256]{2,1,0:T(8,128)}, u32[]{:S(2)}) copy-start(f32[2,256,256]{2,1,0:T(8,128)} %density.1) | copy-start | bytes 1572868
  5.7 7.7 %copy-start.3 = (bf16[256,512]{1,0:T(8,128)(2,1)S(1)}, bf16[256,512]{1,0:T(8,128)(2,1)}, u32[]{:S(2)}) copy-start(bf16[256,512]{1,0:T(8,128)(2,1)} %constant.32.clone.refs_5_.refs_10_) | copy-start | bytes 786436
  5.7 7.6 %copy-start.4 = (bf16[256,512]{1,0:T(8,128)(2,1)S(1)}, bf16[256,512]{1,0:T(8,128)(2,1)}, u32[]{:S(2)}) copy-start(bf16[256,512]{1,0:T(8,128)(2,1)} %constant.31.clone.refs_4_.refs_9_) | copy-start | bytes 786436
  5.7 7.6 %copy-start.5 = (bf16[512,256]{1,0:T(8,128)(2,1)S(1)}, bf16[512,256]{1,0:T(8,128)(2,1)}, u32[]{:S(2)}) copy-start(bf16[512,256]{1,0:T(8,128)(2,1)} %constant.30.clone.refs_3_.refs_8_) | copy-start | bytes 786436
  5.7 7.6 %copy-start.6 = (bf16[512,256]{1,0:T(8,128)(2,1)S(1)}, bf16[512,256]{1,0:T(8,128)(2,1)}, u32[]{:S(2)}) copy-start(bf16[512,256]{1,0:T(8,128)(2,1)} %constant.29.clone.refs_2_.refs_7_) | copy-start | bytes 786436
  5.7 11.6 %collective-permute-start.3 = (f32[2,128,256]{2,1,0:T(8,128)S(1)}, f32[2,128,256]{2,1,0:T(8,128)S(1)}, u32[]{:S(2)}, u32[]{:S(2)}) collective-permute-start(f32[2,128,256]{2,1,0:T(8,128)S(1)} %fusion.1), channel_id=1, source_target_pairs={{0,16},{16,0},{1,17},{17,1},{2,18},{18,2},{3,19},{19,3},{4,20},{20... | collective-permute-start | bytes 786440 | tf_op jit(solution)/shard_map/ppermute | solution.py:291
  16.0 3.9 %collective-permute-start.4 = (f32[256,128]{1,0:T(8,128)S(1)}, f32[256,128]{1,0:T(8,128)S(1)}, u32[]{:S(2)}, u32[]{:S(2)}) collective-permute-start(f32[256,128]{1,0:T(8,128)S(1)} %get-tuple-element.26), channel_id=1, source_target_pairs={{0,16},{16,0},{1,17},{17,1},{2,18},{18,2},{3,19},{19,3},{4,20},{20... | collective-permute-start | bytes 393224 | tf_op jit(solution)/shard_map/ppermute | solution.py:291
  19.9 10.0 %collective-permute-start.5 = (f32[384,128]{1,0:T(8,128)S(1)}, f32[384,128]{1,0:T(8,128)S(1)}, u32[]{:S(2)}, u32[]{:S(2)}) collective-permute-start(f32[384,128]{1,0:T(8,128)S(1)} %get-tuple-element.30), channel_id=1, source_target_pairs={{0,1},{1,0},{2,3},{3,2},{4,5},{5,4},{6,7},{7,6},{8,9},{9,8},{10,11... | collective-permute-start | bytes 589832 | tf_op jit(solution)/shard_map/ppermute | solution.py:291
  20.0 5.5 %collective-permute-start.2 = (f32[256,128]{1,0:T(8,128)S(1)}, f32[256,128]{1,0:T(8,128)S(1)}, u32[]{:S(2)}, u32[]{:S(2)}) collective-permute-start(f32[256,128]{1,0:T(8,128)S(1)} %get-tuple-element.22), channel_id=1, source_target_pairs={{0,16},{16,0},{1,17},{17,1},{2,18},{18,2},{3,19},{19,3},{4,20},{20... | collective-permute-start | bytes 393224 | tf_op jit(solution)/shard_map/ppermute | solution.py:291
  21.3 11.5 %collective-permute-start.6 = (f32[128,128]{1,0:T(8,128)S(1)}, f32[128,128]{1,0:T(8,128)S(1)}, u32[]{:S(2)}, u32[]{:S(2)}) collective-permute-start(f32[128,128]{1,0:T(8,128)S(1)} %get-tuple-element.35), channel_id=1, source_target_pairs={{1,2},{2,1},{3,4},{4,3},{5,6},{6,5},{7,8},{8,7},{9,10},{10,9},{11,... | collective-permute-start | bytes 196616 | tf_op jit(solution)/shard_map/ppermute | solution.py:291
  25.6 8.3 %collective-permute-start.7 = (f32[256,128]{1,0:T(8,128)S(1)}, f32[256,128]{1,0:T(8,128)S(1)}, u32[]{:S(2)}, u32[]{:S(2)}) collective-permute-start(f32[256,128]{1,0:T(8,128)S(1)} %get-tuple-element.36), channel_id=1, source_target_pairs={{1,2},{2,1},{3,4},{4,3},{5,6},{6,5},{7,8},{8,7},{9,10},{10,9},{11,... | collective-permute-start | bytes 393224 | tf_op jit(solution)/shard_map/ppermute | solution.py:291

commit v4 on v3

--- a/solution.py
+++ b/solution.py
@@ -202,12 +202,9 @@
     )
 
 
-def far_kernel(xs, paired, tile, layers, spectra, *refs):
-    halves, refs = (refs[:3], refs[3:6]), refs[6:]
-    strips, basis, basis_t = refs[: len(paired)], refs[len(paired) :][:2], refs[len(paired) :][2:4]
-    refs = refs[len(paired) + 4 :]
-    predicted_out, residual_out, field, result = refs[:4]
-    residual, behind, across, corner, sems = refs[4:]
+def own_kernel(tile, *refs):
+    halves, basis = (refs[:3], refs[3:6]), refs[6:8]
+    predicted_out, residual_out, rows_done, residual, behind, sems = refs[8:]
     low, high = slice(0, tile), slice(tile, 2 * tile)
     copies = []
     for k, other in enumerate((1, 0)):
@@ -219,26 +216,33 @@
     for k, other in enumerate((1, 0)):
         residual[:, edge("gy", other)] = halves[k][1][...]
         behind[:, edge("gy", other)] = halves[k][2][...]
-    across[...] = jnp.zeros_like(across)
-    corner[...] = jnp.zeros_like(corner)
+    rows_done[low] = product(pair(basis, low, ALL), parts(residual[...] + behind[...]))
+    rows_done[high] = product(pair(basis, high, ALL), parts(residual[...] - behind[...]))
+    for copy in copies:
+        copy.wait()
+
+
+def strip_rows(top, bottom, basis, tile):
+    up = wide_product(pair(basis, slice(0, tile), ALL), parts(top + bottom))
+    down = wide_product(pair(basis, slice(tile, 2 * tile), ALL), parts(top - bottom))
+    return jnp.concatenate([up, down], axis=0)
+
+
+def far_kernel(xs, paired, tile, layers, spectra, rows_done, *refs):
+    strips, refs = refs[: len(paired)], refs[len(paired) :]
+    basis, basis_t, (field, result, corner, wrapped) = refs[:2], refs[2:4], refs[4:]
+    low, high = slice(0, tile), slice(tile, 2 * tile)
+    wrapped[...] = jnp.zeros_like(wrapped)
     for ref, phase in zip(strips, paired):
-        cols = halo("gy", phase)
-        across[:, cols] = ref[:tile]
+        if len(xs) < 2:
+            corner[...] = jnp.zeros_like(corner)
         for k, other in enumerate(xs):
             start = tile + k * RADIUS
-            corner[halo("gx", other), cols] = ref[start : start + RADIUS]
-    up_even, up_odd = residual[...] + across[...], residual[...] - across[...]
-    down_even, down_odd = behind[...] + corner[...], behind[...] - corner[...]
-    even = jnp.concatenate([up_even + down_even, up_even - down_even], axis=0)
-    odd = jnp.concatenate([up_odd + down_odd, up_odd - down_odd], axis=0)
-    even = product(parts(even), pair(basis_t, ALL, low))
-    odd = product(parts(odd), pair(basis_t, ALL, high))
-    for rows in (low, high):
-        both = jnp.concatenate([even[rows], odd[rows]], axis=1)
-        field[rows] = product(pair(basis, rows, ALL), parts(both))
+            corner[halo("gx", other)] = ref[start : start + RADIUS]
+        wrapped[:, halo("gy", phase)] = strip_rows(ref[:tile], corner[...], basis, tile)
+    field[:, low] = product(parts(rows_done[...] + wrapped[...]), pair(basis_t, ALL, low))
+    field[:, high] = product(parts(rows_done[...] - wrapped[...]), pair(basis_t, ALL, high))
     result[...] = gradient_half(spectra, field, basis, basis_t, 0, tile, layers)
-    for copy in copies:
-        copy.wait()
 
 
 def adjoint_kernel(xs, crossing, early, tile, layers, spectra, field, far, *refs):
@@ -267,9 +271,7 @@
         for k, other in enumerate(xs):
             start = ref.shape[0] + (k - len(xs)) * RADIUS
             corner[halo("gx", other)] = ref[start : start + RADIUS]
-        up = wide_product(pair(basis, low, ALL), parts(across[...] + corner[...]))
-        down = wide_product(pair(basis, high, ALL), parts(across[...] - corner[...]))
-        both = jnp.concatenate(parts(jnp.concatenate([up, down], axis=0)), axis=1)
+        both = jnp.concatenate(parts(strip_rows(across[...], corner[...], basis, tile)), axis=1)
         ticks = halo("gy", phase)
         upper, lower = (jnp.concatenate([table[ticks, :]] * 2, axis=0) for table in basis_t)
         value = jnp.dot(both, upper, preferred_element_type=F32) + jnp.dot(both, lower, preferred_element_type=F32)
@@ -374,15 +376,26 @@
         received += [swap(value, "gy", other) for value in out[3:]]
     crossing = [phase for phase in ys if phase]
     paired = [phase for phase in ys if not phase]
-    operands = [spectra, *halves, *received[len(crossing) :], *basis]
-    predicted, residual, field, far = pl.pallas_call(
+    operands = [*halves, *basis[:2]]
+    predicted, residual, rows_done = pl.pallas_call(
+        functools.partial(own_kernel, tile),
+        out_shape=[array(tile, tile)] * 2 + [array(2 * tile, tile)],
+        in_specs=[vmem] * len(operands),
+        out_specs=[hbm] * 2 + [vmem],
+        scratch_shapes=[pltpu.VMEM((tile, tile), F32)] * 2 + [pltpu.SemaphoreType.DMA((4,))],
+        compiler_params=PARAMS,
+        cost_estimate=cost(2, tile),
+        name="own",
+    )(*operands)
+    operands = [spectra, rows_done, *received[len(crossing) :], *basis]
+    field, far = pl.pallas_call(
         functools.partial(far_kernel, xs, paired, tile, layers),
-        out_shape=[array(tile, tile)] * 2 + [array(2 * tile, 2 * tile), array(tile, layers * RADIUS)],
+        out_shape=[array(2 * tile, 2 * tile), array(tile, layers * RADIUS)],
         in_specs=[vmem] * len(operands),
-        out_specs=[hbm] * 2 + [vmem] * 2,
-        scratch_shapes=[pltpu.VMEM((tile, tile), F32)] * 4 + [pltpu.SemaphoreType.DMA((4,))],
+        out_specs=[vmem] * 2,
+        scratch_shapes=[pltpu.VMEM((tile, RADIUS), F32), pltpu.VMEM((2 * tile, tile), F32)],
         compiler_params=PARAMS,
-        cost_estimate=cost(16, tile),
+        cost_estimate=cost(14, tile),
         name="far",
     )(*operands)
     operands = [spectra, field, far, *firsts, *received[: len(crossing)], *basis]

time: 36.7 us -> 36.7 us (level)
    pallas_call x0 -> x1, Pallas kernels: none -> 1.06 us  [body(): pl.pallas_call(functools.partial(own_kernel, tile), out_shape=[array(tile...]
    pallas_call x1, Pallas kernels: 2.93 us -> 2.06 us  [body(): pl.pallas_call(functools.partial(far_kernel, xs, paired, tile, layers), o...]
where the time goes in v4:
time: 36.7 us; the launch traced here: 36.5 us
  starting transfers between devices  16.2 us (44%)
  Pallas kernels  10.7 us (29%)
  waiting for transfers between devices  7.53 us (21%)
  other arithmetic  1.18 us (3%)
  between operations  0.85 us (2%)
    ppermute x8, starting transfers between devices, swap(): lax.ppermute(value, axis, [link for link in links if 0 <= link[1] < count])  16.2 us
    ppermute x8, waiting for transfers between devices, swap(): lax.ppermute(value, axis, [link for link in links if 0 <= link[1] < count])  7.53 us
    pallas_call x1, Pallas kernels, body(): pl.pallas_call(functools.partial(forward_kernel, xs, ys, early, tile, lay...  2.63 us
    pallas_call x1, Pallas kernels, body(): pl.pallas_call(functools.partial(adjoint_kernel, xs, crossing, early, til...  2.54 us
    pallas_call x1, Pallas kernels, body(): pl.pallas_call(functools.partial(spectrum_kernel, tile, layers), out_shap...  2.21 us
    pallas_call x1, Pallas kernels, body(): pl.pallas_call(functools.partial(far_kernel, xs, paired, tile, layers), o...  2.06 us
    select_n x1, other arithmetic, cols_of(): return jnp.where(upper, density[..., tile - RADIUS:], density[..., :RADIUS])  1.12 us
    pallas_call x1, Pallas kernels, body(): pl.pallas_call(functools.partial(own_kernel, tile), out_shape=[array(tile...  1.06 us
  transfers between devices with their start and end apart: 8, of which 3 were waited for; matrix products, arithmetic and copies ran while one was open for 0% of the time, Pallas kernels for 22%

profile of v4, /device:TPU:17, one launch (start us, length us, event | category | flops | bytes accessed | tf_op | source)
XLA Modules:
  0.0 36.5 jit_solution(2068349323470328049)
XLA Ops:
  0.6 0.0 copy-start
  0.6 0.0 copy-start.1
  0.7 1.1 %slice_select_fusion = (f32[2,256,128]{2,1,0:T(8,128)S(1)}, f32[2,256,128]{2,1,0:T(8,128)S(1)}) fusion(f32[2,256,256]{2,1,0:T(8,128)} %density.1, pred[]{:T(512)S(6)} %eq.10, pred[]{:T(512)S(6)} %eq.9), kind=kLoop, calls=%fused_computation.6 | loop fusion | flops 131072 | bytes 1048578 | tf_op jit(solution)/shard_map/jit(_where)/select_n | solution.py:323
  1.8 0.7 %collective-permute-start.1 = (f32[2,256,128]{2,1,0:T(8,128)S(1)}, f32[2,256,128]{2,1,0:T(8,128)S(1)}, u32[]{:S(2)}, u32[]{:S(2)}) collective-permute-start(f32[2,256,128]{2,1,0:T(8,128)S(1)} %get-tuple-element.39), channel_id=1, source_target_pairs={{0,1},{1,0},{2,3},{3,2},{4,5},{5,4},{6,7},{7,6},{8,9},{9,8},{10,11... | collective-permute-start | bytes 786440 | tf_op jit(solution)/shard_map/ppermute | solution.py:293
  2.5 3.0 %collective-permute-start = (f32[2,256,128]{2,1,0:T(8,128)S(1)}, f32[2,256,128]{2,1,0:T(8,128)S(1)}, u32[]{:S(2)}, u32[]{:S(2)}) collective-permute-start(f32[2,256,128]{2,1,0:T(8,128)S(1)} %get-tuple-element.40), channel_id=1, source_target_pairs={{1,2},{2,1},{3,4},{4,3},{5,6},{6,5},{7,8},{8,7},{9,10},{10,9},{11,... | collective-permute-start | bytes 786440 | tf_op jit(solution)/shard_map/ppermute | solution.py:293
  5.5 0.0 copy-done
  5.6 0.0 copy-done.1
  5.6 0.0 copy-start.2
  5.7 0.0 copy-start.3
  5.7 0.0 copy-start.4
  5.7 0.0 copy-start.5
  5.7 0.0 copy-start.6
  5.7 1.3 %collective-permute-start.3 = (f32[2,128,256]{2,1,0:T(8,128)S(1)}, f32[2,128,256]{2,1,0:T(8,128)S(1)}, u32[]{:S(2)}, u32[]{:S(2)}) collective-permute-start(f32[2,128,256]{2,1,0:T(8,128)S(1)} %fusion.1), channel_id=1, source_target_pairs={{0,16},{16,0},{1,17},{17,1},{2,18},{18,2},{3,19},{19,3},{4,20},{20... | collective-permute-start | bytes 786440 | tf_op jit(solution)/shard_map/ppermute | solution.py:293
  7.0 2.2 %spectrum.1.spectra = f32[2,384,384]{2,1,0:T(8,128)S(1)} custom-call(s32[2]{0:T(128)} %index_source.1, bf16[384,256]{1,0:T(8,128)(2,1)} %constant.33.clone.refs_0_, bf16[384,256]{1,0:T(8,128)(2,1)} %constant.34.clone.refs_1_, bf16[256,384]{1,0:T(8,128)(2,1)} %constant.35.clone.refs_2_, bf16[256,384]{1,0:T(8,128)(2,1)} %constant.36.clone.refs_3_), custom_call_target="tpu_custom_call" | custom-call | flops 805306368 | bytes 1048576 | tf_op jit(solution)/shard_map/spectrum/pallas_call | solution.py:332
  9.2 0.0 collective-permute-done.1.refs_1_
  9.2 4.1 %collective-permute-done.refs_0_ = f32[2,256,128]{2,1,0:T(8,128)S(1)} collective-permute-done((f32[2,256,128]{2,1,0:T(8,128)S(1)}, f32[2,256,128]{2,1,0:T(8,128)S(1)}, u32[]{:S(2)}, u32[]{:S(2)}) %collective-permute-start) | collective-permute-done | bytes 262176 | tf_op jit(solution)/shard_map/ppermute | solution.py:293
  13.3 0.0 copy-done.2
  13.3 0.0 copy-done.3
  13.3 0.0 copy-done.4
  13.3 0.0 copy-done.5
  13.3 0.0 copy-done.6
  13.3 2.6 %forward.1 = (f32[256,256]{1,0:T(8,128)S(1)}, f32[256,256]{1,0:T(8,128)S(1)}, f32[256,128]{1,0:T(8,128)S(1)}, f32[256,128]{1,0:T(8,128)S(1)}, f32[128,128]{1,0:T(8,128)S(1)}) custom-call(f32[2,256,256]{2,1,0:T(8,128)S(1)} %copy-done.2, f32[2,384,384]{2,1,0:T(8,128)S(1)} %spectrum.1.spectra, f32[256,256]{1,0:T(8,128)S(1)} %copy-done.1, ...), custom_call_target="tpu_custom_call" | custom-call | flops 1811939328 | bytes 1048576 | tf_op jit(solution)/shard_map/forward/pallas_call | solution.py:345
  16.0 1.3 %collective-permute-start.4 = (f32[256,128]{1,0:T(8,128)S(1)}, f32[256,128]{1,0:T(8,128)S(1)}, u32[]{:S(2)}, u32[]{:S(2)}) collective-permute-start(f32[256,128]{1,0:T(8,128)S(1)} %get-tuple-element.27), channel_id=1, source_target_pairs={{0,16},{16,0},{1,17},{17,1},{2,18},{18,2},{3,19},{19,3},{4,20},{20... | collective-permute-start | bytes 393224 | tf_op jit(solution)/shard_map/ppermute | solution.py:293
  17.3 0.0 collective-permute-done.3.refs_1_
  17.3 2.6 %collective-permute-done.4.refs_0_ = f32[256,128]{1,0:T(8,128)S(1)} collective-permute-done((f32[256,128]{1,0:T(8,128)S(1)}, f32[256,128]{1,0:T(8,128)S(1)}, u32[]{:S(2)}, u32[]{:S(2)}) %collective-permute-start.4) | collective-permute-done | bytes 131104 | tf_op jit(solution)/shard_map/ppermute | solution.py:293
  19.9 0.1 shard_map.140
  19.9 0.1 collective-permute-start.5
  20.0 1.3 %collective-permute-start.2 = (f32[256,128]{1,0:T(8,128)S(1)}, f32[256,128]{1,0:T(8,128)S(1)}, u32[]{:S(2)}, u32[]{:S(2)}) collective-permute-start(f32[256,128]{1,0:T(8,128)S(1)} %get-tuple-element.23), channel_id=1, source_target_pairs={{0,16},{16,0},{1,17},{17,1},{2,18},{18,2},{3,19},{19,3},{4,20},{20... | collective-permute-start | bytes 393224 | tf_op jit(solution)/shard_map/ppermute | solution.py:293
  21.3 4.2 %collective-permute-start.6 = (f32[128,128]{1,0:T(8,128)S(1)}, f32[128,128]{1,0:T(8,128)S(1)}, u32[]{:S(2)}, u32[]{:S(2)}) collective-permute-start(f32[128,128]{1,0:T(8,128)S(1)} %get-tuple-element.37), channel_id=1, source_target_pairs={{1,2},{2,1},{3,4},{4,3},{5,6},{6,5},{7,8},{8,7},{9,10},{10,9},{11,... | collective-permute-start | bytes 196616 | tf_op jit(solution)/shard_map/ppermute | solution.py:293
  25.5 0.0 collective-permute-done.2.refs_0_
  25.5 0.1 shard_map.139
  25.6 4.3 %collective-permute-start.7 = (f32[256,128]{1,0:T(8,128)S(1)}, f32[256,128]{1,0:T(8,128)S(1)}, u32[]{:S(2)}, u32[]{:S(2)}) collective-permute-start(f32[256,128]{1,0:T(8,128)S(1)} %get-tuple-element.38), channel_id=1, source_target_pairs={{1,2},{2,1},{3,4},{4,3},{5,6},{6,5},{7,8},{8,7},{9,10},{10,9},{11,... | collective-permute-start | bytes 393224 | tf_op jit(solution)/shard_map/ppermute | solution.py:293
  29.9 1.1 %own.1 = (f32[256,256]{1,0:T(8,128)}, f32[256,256]{1,0:T(8,128)}, f32[512,256]{1,0:T(8,128)S(1)}) custom-call(f32[256,128]{1,0:T(8,128)S(1)} %get-tuple-element.24.refs_0_, f32[256,128]{1,0:T(8,128)S(1)} %get-tuple-element.25.refs_1_, f32[256,128]{1,0:T(8,128)S(1)} %get-tuple-element.26.refs_2_, f32[256,128]{1,0:T(8,128)S(1)} %get-tuple-element.28.refs_3_, ...), custom_call_target="tpu_custom_call" | custom-call | flops 201326592 | bytes 1048576 | tf_op jit(solution)/shard_map/own/pallas_call | solution.py:380
  31.0 0.0 collective-permute-done.5.refs_0_
  31.0 2.1 %far.1 = (f32[512,512]{1,0:T(8,128)S(1)}, f32[256,256]{1,0:T(8,128)S(1)}) custom-call(f32[2,384,384]{2,1,0:T(8,128)S(1)} %spectrum.1.spectra, f32[512,256]{1,0:T(8,128)S(1)} %get-tuple-element.33.rows_done, f32[384,128]{1,0:T(8,128)S(1)} %collective-permute-done.5.refs_0_, bf16[512,256]{1,0:T(8,128)(2,1)S(1)} %copy-done.4, bf16[512,256]{1,0:T(8,128)(2,1)S(1)} %copy-done.3, ...), custom_call_target="tpu_custom_call" | custom-call | flops 1409286144 | bytes 1048576 | tf_op jit(solution)/shard_map/far/pallas_call | solution.py:391
  33.0 0.0 collective-permute-done.6.refs_0_
  33.0 0.9 %collective-permute-done.7.refs_1_ = f32[256,128]{1,0:T(8,128)S(1)} collective-permute-done((f32[256,128]{1,0:T(8,128)S(1)}, f32[256,128]{1,0:T(8,128)S(1)}, u32[]{:S(2)}, u32[]{:S(2)}) %collective-permute-start.7) | collective-permute-done | bytes 131104 | tf_op jit(solution)/shard_map/ppermute | solution.py:293
  33.9 2.5 %adjoint.1 = f32[2,256,256]{2,1,0:T(8,128)} custom-call(f32[2,384,384]{2,1,0:T(8,128)S(1)} %spectrum.1.spectra, f32[512,512]{1,0:T(8,128)S(1)} %get-tuple-element.35.field, f32[256,256]{1,0:T(8,128)S(1)} %get-tuple-element.36.far, f32[128,128]{1,0:T(8,128)S(1)} %collective-permute-done.6.refs_0_, f32[256,128]{1,0:T(8,128)S(1)} %collective-permute-done.7.refs_1_, ...), custom_call_target="tpu_custom_call" | custom-call | flops 1207959552 | bytes 1048576 | tf_op jit(solution)/shard_map/adjoint/pallas_call | solution.py:402
  (2 shorter events, 0.1 us)
Async XLA Ops:
  0.6 4.9 %copy-start = (s32[256,256]{1,0:T(8,128)S(1)}, s32[256,256]{1,0:T(8,128)}, u32[]{:S(2)}) copy-start(s32[256,256]{1,0:T(8,128)} %stations.5) | copy-start | bytes 786436
  0.6 5.0 %copy-start.1 = (f32[256,256]{1,0:T(8,128)S(1)}, f32[256,256]{1,0:T(8,128)}, u32[]{:S(2)}) copy-start(f32[256,256]{1,0:T(8,128)} %observed.5) | copy-start | bytes 786436
  1.8 7.5 %collective-permute-start.1 = (f32[2,256,128]{2,1,0:T(8,128)S(1)}, f32[2,256,128]{2,1,0:T(8,128)S(1)}, u32[]{:S(2)}, u32[]{:S(2)}) collective-permute-start(f32[2,256,128]{2,1,0:T(8,128)S(1)} %get-tuple-element.39), channel_id=1, source_target_pairs={{0,1},{1,0},{2,3},{3,2},{4,5},{5,4},{6,7},{7,6},{8,9},{9,8},{10,11... | collective-permute-start | bytes 786440 | tf_op jit(solution)/shard_map/ppermute | solution.py:293
  2.5 10.8 %collective-permute-start = (f32[2,256,128]{2,1,0:T(8,128)S(1)}, f32[2,256,128]{2,1,0:T(8,128)S(1)}, u32[]{:S(2)}, u32[]{:S(2)}) collective-permute-start(f32[2,256,128]{2,1,0:T(8,128)S(1)} %get-tuple-element.40), channel_id=1, source_target_pairs={{1,2},{2,1},{3,4},{4,3},{5,6},{6,5},{7,8},{8,7},{9,10},{10,9},{11,... | collective-permute-start | bytes 786440 | tf_op jit(solution)/shard_map/ppermute | solution.py:293
  5.6 7.7 %copy-start.2 = (f32[2,256,256]{2,1,0:T(8,128)S(1)}, f32[2,256,256]{2,1,0:T(8,128)}, u32[]{:S(2)}) copy-start(f32[2,256,256]{2,1,0:T(8,128)} %density.1) | copy-start | bytes 1572868
  5.7 7.7 %copy-start.3 = (bf16[512,256]{1,0:T(8,128)(2,1)S(1)}, bf16[512,256]{1,0:T(8,128)(2,1)}, u32[]{:S(2)}) copy-start(bf16[512,256]{1,0:T(8,128)(2,1)} %constant.30.clone.refs_3_.refs_7_.refs_2_) | copy-start | bytes 786436
  5.7 7.6 %copy-start.4 = (bf16[512,256]{1,0:T(8,128)(2,1)S(1)}, bf16[512,256]{1,0:T(8,128)(2,1)}, u32[]{:S(2)}) copy-start(bf16[512,256]{1,0:T(8,128)(2,1)} %constant.29.clone.refs_2_.refs_6_.refs_1_) | copy-start | bytes 786436
  5.7 7.6 %copy-start.5 = (bf16[256,512]{1,0:T(8,128)(2,1)S(1)}, bf16[256,512]{1,0:T(8,128)(2,1)}, u32[]{:S(2)}) copy-start(bf16[256,512]{1,0:T(8,128)(2,1)} %constant.32.clone.refs_5_.refs_4_) | copy-start | bytes 786436
  5.7 7.6 %copy-start.6 = (bf16[256,512]{1,0:T(8,128)(2,1)S(1)}, bf16[256,512]{1,0:T(8,128)(2,1)}, u32[]{:S(2)}) copy-start(bf16[256,512]{1,0:T(8,128)(2,1)} %constant.31.clone.refs_4_.refs_3_) | copy-start | bytes 786436
  5.7 11.6 %collective-permute-start.3 = (f32[2,128,256]{2,1,0:T(8,128)S(1)}, f32[2,128,256]{2,1,0:T(8,128)S(1)}, u32[]{:S(2)}, u32[]{:S(2)}) collective-permute-start(f32[2,128,256]{2,1,0:T(8,128)S(1)} %fusion.1), channel_id=1, source_target_pairs={{0,16},{16,0},{1,17},{17,1},{2,18},{18,2},{3,19},{19,3},{4,20},{20... | collective-permute-start | bytes 786440 | tf_op jit(solution)/shard_map/ppermute | solution.py:293
  16.0 3.9 %collective-permute-start.4 = (f32[256,128]{1,0:T(8,128)S(1)}, f32[256,128]{1,0:T(8,128)S(1)}, u32[]{:S(2)}, u32[]{:S(2)}) collective-permute-start(f32[256,128]{1,0:T(8,128)S(1)} %get-tuple-element.27), channel_id=1, source_target_pairs={{0,16},{16,0},{1,17},{17,1},{2,18},{18,2},{3,19},{19,3},{4,20},{20... | collective-permute-start | bytes 393224 | tf_op jit(solution)/shard_map/ppermute | solution.py:293
  19.9 11.0 %collective-permute-start.5 = (f32[384,128]{1,0:T(8,128)S(1)}, f32[384,128]{1,0:T(8,128)S(1)}, u32[]{:S(2)}, u32[]{:S(2)}) collective-permute-start(f32[384,128]{1,0:T(8,128)S(1)} %get-tuple-element.34), channel_id=1, source_target_pairs={{0,1},{1,0},{2,3},{3,2},{4,5},{5,4},{6,7},{7,6},{8,9},{9,8},{10,11... | collective-permute-start | bytes 589832 | tf_op jit(solution)/shard_map/ppermute | solution.py:293
  20.0 5.5 %collective-permute-start.2 = (f32[256,128]{1,0:T(8,128)S(1)}, f32[256,128]{1,0:T(8,128)S(1)}, u32[]{:S(2)}, u32[]{:S(2)}) collective-permute-start(f32[256,128]{1,0:T(8,128)S(1)} %get-tuple-element.23), channel_id=1, source_target_pairs={{0,16},{16,0},{1,17},{17,1},{2,18},{18,2},{3,19},{19,3},{4,20},{20... | collective-permute-start | bytes 393224 | tf_op jit(solution)/shard_map/ppermute | solution.py:293
  21.3 11.7 %collective-permute-start.6 = (f32[128,128]{1,0:T(8,128)S(1)}, f32[128,128]{1,0:T(8,128)S(1)}, u32[]{:S(2)}, u32[]{:S(2)}) collective-permute-start(f32[128,128]{1,0:T(8,128)S(1)} %get-tuple-element.37), channel_id=1, source_target_pairs={{1,2},{2,1},{3,4},{4,3},{5,6},{6,5},{7,8},{8,7},{9,10},{10,9},{11,... | collective-permute-start | bytes 196616 | tf_op jit(solution)/shard_map/ppermute | solution.py:293
  25.6 8.3 %collective-permute-start.7 = (f32[256,128]{1,0:T(8,128)S(1)}, f32[256,128]{1,0:T(8,128)S(1)}, u32[]{:S(2)}, u32[]{:S(2)}) collective-permute-start(f32[256,128]{1,0:T(8,128)S(1)} %get-tuple-element.38), channel_id=1, source_target_pairs={{1,2},{2,1},{3,4},{4,3},{5,6},{6,5},{7,8},{8,7},{9,10},{10,9},{11,... | collective-permute-start | bytes 393224 | tf_op jit(solution)/shard_map/ppermute | solution.py:293

commit v5 on v4

--- a/solution.py
+++ b/solution.py
@@ -1,5 +1,4 @@
 import functools
-import itertools
 import math
 
 import jax
@@ -62,6 +61,12 @@
     return dot(left[0], right[0]) + (dot(left[0], right[1]) + dot(left[1], right[0]))
 
 
+def wide_product(left, right):
+    width = right[0].shape[1]
+    both = jnp.dot(left[0], jnp.concatenate(right, axis=1), preferred_element_type=F32)
+    return both[:, :width] + (both[:, width:] + jnp.dot(left[1], right[0], preferred_element_type=F32))
+
+
 def pair(refs, *index):
     return refs[0][index], refs[1][index]
 
@@ -85,12 +90,59 @@
 ALL = slice(None)
 
 
-def spectrum_kernel(tile, layers, index_source, *refs):
-    sources, spectra, held, index, sems = refs[:4], refs[4], refs[5:9], refs[9], refs[10]
+def columns_half(total, basis, basis_t, other, tile):
+    low, high = slice(0, tile), slice(tile, 2 * tile)
+    mixed = wide_product(parts(total), pair(basis, ALL, edge("gy", other)))
+    even = wide_product(pair(basis_t, ALL, low), parts(mixed[low]))
+    odd = wide_product(pair(basis_t, ALL, high), parts(mixed[high]))
+    return even + odd, even - odd
+
+
+def send_half(xs, sends, own, spill):
+    for ref, phase in zip(sends, xs):
+        ref[:RADIUS] = spill[halo("gx", phase)]
+        ref[RADIUS:] = own[edge("gx", phase)]
+
+
+def summed(spectra, values, half, before=None):
+    rows = []
+    for a in range(4):
+        blocks = []
+        for b in range(4):
+            place = slice(a * half, (a + 1) * half), slice(b * half, (b + 1) * half)
+            block = None
+            for layer, value in enumerate(values):
+                term = spectra[layer, group(a, half), group(b, half)] * value[place]
+                block = term if block is None else block + term
+            if before is not None:
+                block = before[place] + block if b < 2 else before[place] - block
+            blocks.append(block)
+        rows.append(jnp.concatenate(blocks, axis=1))
+    return jnp.concatenate(rows, axis=0)
+
+
+def prepare_kernel(xs, paired, tile, layers, index_source, *refs):
+    sources, density, refs = refs[:4], refs[4], refs[5:]
+    received, refs = refs[: len(paired)], refs[len(paired) :]
+    basis, basis_t, (spectra, total, own, spill), refs = refs[:2], refs[2:4], refs[4:8], refs[8:]
+    sends, held, (index, wrapped, fields, sems) = refs[: len(xs)], refs[len(xs) : len(xs) + 4], refs[len(xs) + 4 :]
     copies = [pltpu.make_async_copy(sources[k], held[k], sems.at[k]) for k in range(4)]
     copies.append(pltpu.make_async_copy(index_source, index, sems.at[4]))
     for copy in reversed(copies):
         copy.start()
+    low, high = slice(0, tile), slice(tile, 2 * tile)
+    wrapped[...] = jnp.zeros_like(wrapped)
+    for ref, phase in zip(received, paired):
+        for layer in range(layers):
+            wrapped[layer * tile : (layer + 1) * tile, halo("gy", phase)] = ref[layer]
+    field = jnp.concatenate([density[layer] for layer in range(layers)], axis=0)
+    behind = wrapped[...]
+    even = product(parts(field + behind), pair(basis_t, ALL, low))
+    odd = product(parts(field - behind), pair(basis_t, ALL, high))
+    for layer in range(layers):
+        rows = slice(layer * tile, (layer + 1) * tile)
+        both = jnp.concatenate([even[rows], odd[rows]], axis=1)
+        fields[layer] = product(pair(basis, ALL, ALL), parts(both))
     span = RADIUS + 8
     rows = lax.broadcasted_iota(jnp.int32, (span, tile), 0)
     cols = lax.broadcasted_iota(jnp.int32, (span, tile), 1)
@@ -108,47 +160,35 @@
     copies[1].wait()
     rest = jnp.zeros((tile - span, first.shape[1]), F32)
     for layer in range(layers):
-        own = jnp.concatenate([first[layer * span : (layer + 1) * span], rest], axis=0)
-        spectra[layer] = product(pair(held[:2], ALL, ALL), parts(own))
-
-
-def forward_kernel(xs, ys, early, tile, layers, density, spectra, observed, stations, *refs):
-    received, refs = refs[: len(ys)], refs[len(ys) :]
+        whole = jnp.concatenate([first[layer * span : (layer + 1) * span], rest], axis=0)
+        spectra[layer] = product(pair(held[:2], ALL, ALL), parts(whole))
+    total[...] = summed(spectra, [fields.at[layer] for layer in range(layers)], tile // 2)
+    own[...], spill[...] = columns_half(total[...], basis, basis_t, 0, tile)
+    send_half(xs, sends, own, spill)
+
+
+def forward_kernel(xs, crossing, early, tile, layers, spectra, before, observed, stations, *refs):
+    received, refs = refs[: len(crossing)], refs[len(crossing) :]
     basis, basis_t, (own, spill), refs = refs[:2], refs[2:4], refs[4:6], refs[6:]
-    sends, firsts, (wrapped, total) = refs[: 2 * len(xs)], refs[2 * len(xs) : -2], refs[-2:]
-    half = tile // 2
-    low, high = slice(0, tile), slice(tile, 2 * tile)
-    if len(ys) < 2:
-        wrapped[...] = jnp.zeros_like(wrapped)
-    for ref, phase in zip(received, ys):
+    sends, firsts = refs[: len(xs)], refs[len(xs) :]
+    total = before[...]
+    for ref, phase in zip(received, crossing):
+        strips = jnp.concatenate([ref[layer] for layer in range(layers)], axis=1)
+        rows_done = product(pair(basis, ALL, ALL), parts(strips))
+        ticks = halo("gy", phase)
+        upper, lower = (jnp.concatenate([table[ticks, :]] * 2, axis=0) for table in basis_t)
+        values = []
         for layer in range(layers):
-            wrapped[layer * tile : (layer + 1) * tile, halo("gy", phase)] = ref[layer]
-    field = jnp.concatenate([density[layer] for layer in range(layers)], axis=0)
-    behind = wrapped[...]
-    even = product(parts(field + behind), pair(basis_t, ALL, low))
-    odd = product(parts(field - behind), pair(basis_t, ALL, high))
-    for layer in range(layers):
-        rows = slice(layer * tile, (layer + 1) * tile)
-        both = jnp.concatenate([even[rows], odd[rows]], axis=1)
-        value = product(pair(basis, ALL, ALL), parts(both))
-        for a in range(4):
-            for b in range(4):
-                place = slice(a * half, (a + 1) * half), slice(b * half, (b + 1) * half)
-                term = spectra[layer, group(a, half), group(b, half)] * value[place]
-                total[place] = term if layer == 0 else total[place] + term
-    mixed = product(parts(total[:, low]), pair(basis, low, ALL)) + product(
-        parts(total[:, high]), pair(basis, high, ALL)
-    )
-    even = product(pair(basis_t, ALL, low), parts(mixed[low]))
-    odd = product(pair(basis_t, ALL, high), parts(mixed[high]))
-    own[...] = even + odd
-    spill[...] = even - odd
-    for k, (phase, other) in enumerate(itertools.product(xs, (1, 0))):
-        sends[k][:RADIUS] = spill[halo("gx", phase), edge("gy", other)]
-        sends[k][RADIUS:] = own[edge("gx", phase), edge("gy", other)]
+            both = jnp.concatenate(parts(rows_done[:, layer * RADIUS : (layer + 1) * RADIUS]), axis=1)
+            values.append(
+                jnp.dot(both, upper, preferred_element_type=F32) + jnp.dot(both, lower, preferred_element_type=F32)
+            )
+        total = summed(spectra, values, tile // 2, before)
+    own[...], spill[...] = columns_half(total, basis, basis_t, 1, tile)
+    send_half(xs, sends, own, spill)
     if early:
         place = halo("gx", xs[0]), edge("gy", 1)
-        firsts[0][...] = stations[place].astype(F32) * (own[place] - observed[place])
+        firsts[0][...] = stations[place].astype(F32) * (own[place[0], :] - observed[place])
 
 
 def side_kernel(xs, early, other, tile, own, spill, observed, stations, *refs):
@@ -156,13 +196,13 @@
     received, strips, refs = refs[:count], refs[count : 2 * count], refs[2 * count :]
     (predicted, residual, behind), sends = refs[:3], refs[3:]
     cols = edge("gy", other)
-    predicted[...] = own[:, cols]
+    predicted[...] = own[...]
     if count < 2:
         behind[...] = jnp.zeros_like(behind)
     for ref, strip, phase in zip(received, strips, xs):
         predicted[edge("gx", phase)] += ref[:RADIUS]
         rows = halo("gx", phase)
-        behind[rows] = strip[1, :, cols] * (spill[rows, cols] + ref[RADIUS:] - strip[0, :, cols])
+        behind[rows] = strip[1, :, cols] * (spill[rows] + ref[RADIUS:] - strip[0, :, cols])
     residual[...] = stations[:, cols].astype(F32) * (predicted[...] - observed[:, cols])
     for ref in sends:
         if early and other:
@@ -184,12 +224,6 @@
         ]
         rows.append(jnp.concatenate(blocks, axis=1))
     return jnp.concatenate(rows, axis=0)
-
-
-def wide_product(left, right):
-    width = right[0].shape[1]
-    both = jnp.dot(left[0], jnp.concatenate(right, axis=1), preferred_element_type=F32)
-    return both[:, :width] + (both[:, width:] + jnp.dot(left[1], right[0], preferred_element_type=F32))
 
 
 def gradient_half(spectra, value, basis, basis_t, other, tile, layers):
@@ -329,39 +363,46 @@
 
     density_halos = [swap(cols_of(phase), "gy", phase) for phase in ys]
     strips = [swap(rows_of(phase), "gx", phase) for phase in xs]
-    spectra = pl.pallas_call(
-        functools.partial(spectrum_kernel, tile, layers),
-        out_shape=array(layers, groups, groups),
-        in_specs=[hbm] * 5,
-        out_specs=vmem,
+    paired = [phase for phase in ys if not phase]
+    crossing = [phase for phase in ys if phase]
+    early = int(len(xs) == 1 and 1 in ys)
+    part = array(tile, RADIUS)
+    operands = [in_hbm(value) for value in (layer_index, *sides)]
+    operands += [density, *density_halos[len(crossing) :], *basis]
+    spectra, before, *out = pl.pallas_call(
+        functools.partial(prepare_kernel, xs, paired, tile, layers),
+        out_shape=[array(layers, groups, groups), array(2 * tile, 2 * tile), part, part]
+        + [array(2 * RADIUS, RADIUS)] * len(xs),
+        in_specs=[hbm] * 5 + [vmem] * (len(operands) - 5),
+        out_specs=[vmem] * (4 + len(xs)),
         scratch_shapes=[pltpu.VMEM(table.shape, BF16) for table in sides]
-        + [pltpu.SMEM((layers,), jnp.int32), pltpu.SemaphoreType.DMA((5,))],
+        + [
+            pltpu.SMEM((layers,), jnp.int32),
+            pltpu.VMEM((layers * tile, tile), F32),
+            pltpu.VMEM((layers, 2 * tile, 2 * tile), F32),
+            pltpu.SemaphoreType.DMA((5,)),
+        ],
         compiler_params=PARAMS,
-        cost_estimate=cost(8, tile),
-        name="spectrum",
-    )(*[in_hbm(value) for value in (layer_index, *sides)])
-    early = int(len(xs) == 1 and 1 in ys)
-    operands = [density, spectra, observed, stations, *density_halos, *basis]
+        cost_estimate=cost(24, tile),
+        name="prepare",
+    )(*operands)
+    values, sends = {0: out[:2]}, {0: out[2:]}
+    operands = [spectra, before, observed, stations, *density_halos[: len(crossing)], *basis]
     out = pl.pallas_call(
-        functools.partial(forward_kernel, xs, ys, early, tile, layers),
-        out_shape=[array(tile, tile)] * 2
-        + [array(2 * RADIUS, RADIUS)] * (2 * len(xs))
-        + [array(tile - RADIUS, RADIUS)] * early,
+        functools.partial(forward_kernel, xs, crossing, early, tile, layers),
+        out_shape=[part, part] + [array(2 * RADIUS, RADIUS)] * len(xs) + [array(tile - RADIUS, RADIUS)] * early,
         in_specs=[vmem] * len(operands),
-        out_specs=[vmem] * (2 + 2 * len(xs) + early),
-        scratch_shapes=[pltpu.VMEM((layers * tile, tile), F32), pltpu.VMEM((2 * tile, 2 * tile), F32)],
+        out_specs=[vmem] * (2 + len(xs) + early),
         compiler_params=PARAMS,
-        cost_estimate=cost(18, tile),
+        cost_estimate=cost(12, tile),
         name="forward",
     )(*operands)
-    own, spill, sends, firsts = out[0], out[1], out[2 : 2 + 2 * len(xs)], out[2 + 2 * len(xs) :]
-    sums = {other: [] for other in (1, 0)}
-    for value, (phase, other) in zip(sends, itertools.product(xs, (1, 0))):
-        sums[other].append(swap(value, "gx", phase))
+    values[1], sends[1], firsts = out[:2], out[2 : 2 + len(xs)], out[2 + len(xs) :]
+    sums = {other: [swap(value, "gx", phase) for value, phase in zip(sends[other], xs)] for other in (1, 0)}
     firsts = [swap(value, "gy", 1) for value in firsts]
     halves, received = [], []
     for other in (1, 0):
-        operands = [own, spill, observed, stations, *sums[other], *strips]
+        operands = [*values[other], observed, stations, *sums[other], *strips]
         there = int(other in ys)
         tall = RADIUS * len(xs) + (RADIUS if early and other else tile)
         out = pl.pallas_call(

time: 36.7 us -> 34.6 us (0.943)
  starting transfers between devices: 16.2 us -> 13 us
  waiting for transfers between devices: 7.53 us -> 8.09 us
  Pallas kernels: 10.7 us -> 11.2 us
    ppermute x8, starting transfers between devices: 16.2 us -> 13 us  [swap(): lax.ppermute(value, axis, [link for link in links if 0 <= link[1] < count])]
    pallas_call x2, Pallas kernels: 4.84 us -> 5.41 us  [the longest x1 3.47 us: body(): pl.pallas_call(functools.partial(prepare_kernel, xs, paired, tile, layers...]
    ppermute x8, waiting for transfers between devices: 7.53 us -> 8.09 us  [swap(): lax.ppermute(value, axis, [link for link in links if 0 <= link[1] < count])]
  transfers between devices with their start and end apart: 8 -> 8, of which waited for: 3 -> 3; matrix products, arithmetic and copies ran while one was open for 0% -> 0% of each run, Pallas kernels for 22% -> 25%
where the time goes in v5:
time: 34.6 us; the launch traced here: 34.4 us
  starting transfers between devices  13 us (38%)
  Pallas kernels  11.2 us (32%)
  waiting for transfers between devices  8.09 us (23%)
  other arithmetic  1.26 us (4%)
  between operations  0.84 us (2%)
    ppermute x8, starting transfers between devices, swap(): lax.ppermute(value, axis, [link for link in links if 0 <= link[1] < count])  13 us
    ppermute x8, waiting for transfers between devices, swap(): lax.ppermute(value, axis, [link for link in links if 0 <= link[1] < count])  8.09 us
    pallas_call x1, Pallas kernels, body(): pl.pallas_call(functools.partial(prepare_kernel, xs, paired, tile, layers...  3.47 us
    pallas_call x1, Pallas kernels, body(): pl.pallas_call(functools.partial(adjoint_kernel, xs, crossing, early, til...  2.54 us
    pallas_call x1, Pallas kernels, body(): pl.pallas_call(functools.partial(far_kernel, xs, paired, tile, layers), o...  2.06 us
    pallas_call x1, Pallas kernels, body(): pl.pallas_call(functools.partial(forward_kernel, xs, crossing, early, til...  1.94 us
    select_n x1, other arithmetic, cols_of(): return jnp.where(upper, density[..., tile - RADIUS:], density[..., :RADIUS])  1.2 us
    pallas_call x1, Pallas kernels, body(): pl.pallas_call(functools.partial(own_kernel, tile), out_shape=[array(tile...  1.06 us
  transfers between devices with their start and end apart: 8, of which 3 were waited for; matrix products, arithmetic and copies ran while one was open for 0% of the time, Pallas kernels for 25%

profile of v5, /device:TPU:17, one launch (start us, length us, event | category | flops | bytes accessed | tf_op | source)
XLA Modules:
  0.0 34.4 jit_solution(2531097076824689745)
XLA Ops:
  0.6 0.0 copy-start
  0.6 0.0 copy-start.1
  0.7 0.0 copy-start.2
  0.7 0.0 copy-start.3
  0.7 0.0 copy-start.4
  0.7 0.0 copy-start.5
  0.7 0.0 copy-start.6
  0.7 1.2 %slice_select_fusion = (f32[2,256,128]{2,1,0:T(8,128)S(1)}, f32[2,256,128]{2,1,0:T(8,128)S(1)}) fusion(f32[2,256,256]{2,1,0:T(8,128)} %refs_4_.4, pred[]{:T(512)S(6)} %eq.10, pred[]{:T(512)S(6)} %eq.9), kind=kLoop, calls=%fused_computation.6 | loop fusion | flops 131072 | bytes 1048578 | tf_op jit(solution)/shard_map/jit(_where)/select_n | solution.py:357
  1.9 0.7 %collective-permute-start = (f32[2,256,128]{2,1,0:T(8,128)S(1)}, f32[2,256,128]{2,1,0:T(8,128)S(1)}, u32[]{:S(2)}, u32[]{:S(2)}) collective-permute-start(f32[2,256,128]{2,1,0:T(8,128)S(1)} %get-tuple-element.48), channel_id=1, source_target_pairs={{0,1},{1,0},{2,3},{3,2},{4,5},{5,4},{6,7},{7,6},{8,9},{9,8},{10,11... | collective-permute-start | bytes 786440 | tf_op jit(solution)/shard_map/ppermute | solution.py:327
  2.7 0.0 copy-done
  2.7 0.0 copy-done.1
  2.7 1.3 %collective-permute-start.3 = (f32[2,128,256]{2,1,0:T(8,128)S(1)}, f32[2,128,256]{2,1,0:T(8,128)S(1)}, u32[]{:S(2)}, u32[]{:S(2)}) collective-permute-start(f32[2,128,256]{2,1,0:T(8,128)S(1)} %fusion.1), channel_id=1, source_target_pairs={{0,16},{16,0},{1,17},{17,1},{2,18},{18,2},{3,19},{19,3},{4,20},{20... | collective-permute-start | bytes 786440 | tf_op jit(solution)/shard_map/ppermute | solution.py:327
  4.0 3.3 %collective-permute-start.1 = (f32[2,256,128]{2,1,0:T(8,128)S(1)}, f32[2,256,128]{2,1,0:T(8,128)S(1)}, u32[]{:S(2)}, u32[]{:S(2)}) collective-permute-start(f32[2,256,128]{2,1,0:T(8,128)S(1)} %get-tuple-element.47), channel_id=1, source_target_pairs={{1,2},{2,1},{3,4},{4,3},{5,6},{6,5},{7,8},{8,7},{9,10},{10,9},{11,... | collective-permute-start | bytes 786440 | tf_op jit(solution)/shard_map/ppermute | solution.py:327
  7.4 0.0 collective-permute-done.refs_5_
  7.4 0.0 copy-done.2
  7.4 0.0 copy-done.3
  7.4 0.0 copy-done.4
  7.4 0.0 copy-done.5
  7.4 0.0 copy-done.6
  7.4 3.5 %prepare.1 = (f32[2,384,384]{2,1,0:T(8,128)S(1)}, f32[512,512]{1,0:T(8,128)S(1)}, f32[256,128]{1,0:T(8,128)S(1)}, f32[256,128]{1,0:T(8,128)S(1)}, f32[256,128]{1,0:T(8,128)S(1)}) custom-call(s32[2]{0:T(128)} %index_source.1, bf16[384,256]{1,0:T(8,128)(2,1)} %constant.33.clone.refs_0_, bf16[384,256]{1,0:T(8,128)(2,1)} %constant.34.clone.refs_1_, ...), custom_call_target="tpu_custom_call" | custom-call | flops 2415919104 | bytes 1048576 | tf_op jit(solution)/shard_map/prepare/pallas_call | solution.py:372
  10.9 0.3 collective-permute-start.4
  11.2 0.0 collective-permute-done.3.refs_1_
  11.2 4.7 %collective-permute-done.4.refs_0_ = f32[256,128]{1,0:T(8,128)S(1)} collective-permute-done((f32[256,128]{1,0:T(8,128)S(1)}, f32[256,128]{1,0:T(8,128)S(1)}, u32[]{:S(2)}, u32[]{:S(2)}) %collective-permute-start.4) | collective-permute-done | bytes 131104 | tf_op jit(solution)/shard_map/ppermute | solution.py:327
  15.9 0.1 shard_map.140
  16.0 1.0 %collective-permute-start.5 = (f32[384,128]{1,0:T(8,128)S(1)}, f32[384,128]{1,0:T(8,128)S(1)}, u32[]{:S(2)}, u32[]{:S(2)}) collective-permute-start(f32[384,128]{1,0:T(8,128)S(1)} %get-tuple-element.42), channel_id=1, source_target_pairs={{0,1},{1,0},{2,3},{3,2},{4,5},{5,4},{6,7},{7,6},{8,9},{9,8},{10,11... | collective-permute-start | bytes 589832 | tf_op jit(solution)/shard_map/ppermute | solution.py:327
  17.0 0.0 collective-permute-done.1.refs_0_
  17.0 1.9 %forward.1 = (f32[256,128]{1,0:T(8,128)S(1)}, f32[256,128]{1,0:T(8,128)S(1)}, f32[256,128]{1,0:T(8,128)S(1)}, f32[128,128]{1,0:T(8,128)S(1)}) custom-call(f32[2,384,384]{2,1,0:T(8,128)S(1)} %get-tuple-element.25.spectra, f32[512,512]{1,0:T(8,128)S(1)} %get-tuple-element.26.before, f32[256,256]{1,0:T(8,128)S(1)} %copy-done.1, s32[256,256]{1,0:T(8,128)S(1)} %copy-done, ...), custom_call_target="tpu_custom_call" | custom-call | flops 1207959552 | bytes 1048576 | tf_op jit(solution)/shard_map/forward/pallas_call | solution.py:391
  19.0 0.3 collective-permute-start.2
  19.3 2.8 %collective-permute-start.6 = (f32[128,128]{1,0:T(8,128)S(1)}, f32[128,128]{1,0:T(8,128)S(1)}, u32[]{:S(2)}, u32[]{:S(2)}) collective-permute-start(f32[128,128]{1,0:T(8,128)S(1)} %get-tuple-element.45), channel_id=1, source_target_pairs={{1,2},{2,1},{3,4},{4,3},{5,6},{6,5},{7,8},{8,7},{9,10},{10,9},{11,... | collective-permute-start | bytes 196616 | tf_op jit(solution)/shard_map/ppermute | solution.py:327
  22.1 2.0 %collective-permute-done.2.refs_0_ = f32[256,128]{1,0:T(8,128)S(1)} collective-permute-done((f32[256,128]{1,0:T(8,128)S(1)}, f32[256,128]{1,0:T(8,128)S(1)}, u32[]{:S(2)}, u32[]{:S(2)}) %collective-permute-start.2) | collective-permute-done | bytes 131104 | tf_op jit(solution)/shard_map/ppermute | solution.py:327
  24.1 0.1 shard_map.139
  24.2 3.2 %collective-permute-start.7 = (f32[256,128]{1,0:T(8,128)S(1)}, f32[256,128]{1,0:T(8,128)S(1)}, u32[]{:S(2)}, u32[]{:S(2)}) collective-permute-start(f32[256,128]{1,0:T(8,128)S(1)} %get-tuple-element.46), channel_id=1, source_target_pairs={{1,2},{2,1},{3,4},{4,3},{5,6},{6,5},{7,8},{8,7},{9,10},{10,9},{11,... | collective-permute-start | bytes 393224 | tf_op jit(solution)/shard_map/ppermute | solution.py:327
  27.4 1.1 %own.1 = (f32[256,256]{1,0:T(8,128)}, f32[256,256]{1,0:T(8,128)}, f32[512,256]{1,0:T(8,128)S(1)}) custom-call(f32[256,128]{1,0:T(8,128)S(1)} %get-tuple-element.30.refs_0_, f32[256,128]{1,0:T(8,128)S(1)} %get-tuple-element.31.refs_1_, f32[256,128]{1,0:T(8,128)S(1)} %get-tuple-element.32.refs_2_, f32[256,128]{1,0:T(8,128)S(1)} %get-tuple-element.36.refs_3_, ...), custom_call_target="tpu_custom_call" | custom-call | flops 201326592 | bytes 1048576 | tf_op jit(solution)/shard_map/own/pallas_call | solution.py:421
  28.4 0.0 collective-permute-done.5.refs_0_
  28.4 2.1 %far.1 = (f32[512,512]{1,0:T(8,128)S(1)}, f32[256,256]{1,0:T(8,128)S(1)}) custom-call(f32[2,384,384]{2,1,0:T(8,128)S(1)} %get-tuple-element.25.spectra, f32[512,256]{1,0:T(8,128)S(1)} %get-tuple-element.41.rows_done, f32[384,128]{1,0:T(8,128)S(1)} %collective-permute-done.5.refs_0_, bf16[512,256]{1,0:T(8,128)(2,1)S(1)} %copy-done.4, ...), custom_call_target="tpu_custom_call" | custom-call | flops 1409286144 | bytes 1048576 | tf_op jit(solution)/shard_map/far/pallas_call | solution.py:432
  30.5 0.0 collective-permute-done.6.refs_0_
  30.5 1.3 %collective-permute-done.7.refs_1_ = f32[256,128]{1,0:T(8,128)S(1)} collective-permute-done((f32[256,128]{1,0:T(8,128)S(1)}, f32[256,128]{1,0:T(8,128)S(1)}, u32[]{:S(2)}, u32[]{:S(2)}) %collective-permute-start.7) | collective-permute-done | bytes 131104 | tf_op jit(solution)/shard_map/ppermute | solution.py:327
  31.9 2.5 %adjoint.1 = f32[2,256,256]{2,1,0:T(8,128)} custom-call(f32[2,384,384]{2,1,0:T(8,128)S(1)} %get-tuple-element.25.spectra, f32[512,512]{1,0:T(8,128)S(1)} %get-tuple-element.43.field, f32[256,256]{1,0:T(8,128)S(1)} %get-tuple-element.44.far, f32[128,128]{1,0:T(8,128)S(1)} %collective-permute-done.6.refs_0_, f32[256,128]{1,0:T(8,128)S(1)} %collective-permute-done.7.refs_1_, ...), custom_call_target="tpu_custom_call" | custom-call | flops 1207959552 | bytes 1048576 | tf_op jit(solution)/shard_map/adjoint/pallas_call | solution.py:443
  (2 shorter events, 0.1 us)
Async XLA Ops:
  0.6 2.0 %copy-start = (s32[256,256]{1,0:T(8,128)S(1)}, s32[256,256]{1,0:T(8,128)}, u32[]{:S(2)}) copy-start(s32[256,256]{1,0:T(8,128)} %stations.5) | copy-start | bytes 786436
  0.6 2.0 %copy-start.1 = (f32[256,256]{1,0:T(8,128)S(1)}, f32[256,256]{1,0:T(8,128)}, u32[]{:S(2)}) copy-start(f32[256,256]{1,0:T(8,128)} %observed.5) | copy-start | bytes 786436
  0.7 6.7 %copy-start.2 = (f32[2,256,256]{2,1,0:T(8,128)S(1)}, f32[2,256,256]{2,1,0:T(8,128)}, u32[]{:S(2)}) copy-start(f32[2,256,256]{2,1,0:T(8,128)} %refs_4_.4) | copy-start | bytes 1572868
  0.7 6.7 %copy-start.3 = (bf16[512,256]{1,0:T(8,128)(2,1)S(1)}, bf16[512,256]{1,0:T(8,128)(2,1)}, u32[]{:S(2)}) copy-start(bf16[512,256]{1,0:T(8,128)(2,1)} %constant.30.clone.refs_7_.refs_2_.refs_3_) | copy-start | bytes 786436
  0.7 6.7 %copy-start.4 = (bf16[512,256]{1,0:T(8,128)(2,1)S(1)}, bf16[512,256]{1,0:T(8,128)(2,1)}, u32[]{:S(2)}) copy-start(bf16[512,256]{1,0:T(8,128)(2,1)} %constant.29.clone.refs_6_.refs_1_.refs_2_) | copy-start | bytes 786436
  0.7 6.7 %copy-start.5 = (bf16[256,512]{1,0:T(8,128)(2,1)S(1)}, bf16[256,512]{1,0:T(8,128)(2,1)}, u32[]{:S(2)}) copy-start(bf16[256,512]{1,0:T(8,128)(2,1)} %constant.32.clone.refs_9_.refs_4_.refs_5_) | copy-start | bytes 786436
  0.7 6.7 %copy-start.6 = (bf16[256,512]{1,0:T(8,128)(2,1)S(1)}, bf16[256,512]{1,0:T(8,128)(2,1)}, u32[]{:S(2)}) copy-start(bf16[256,512]{1,0:T(8,128)(2,1)} %constant.31.clone.refs_8_.refs_3_.refs_4_) | copy-start | bytes 786436
  1.9 5.4 %collective-permute-start = (f32[2,256,128]{2,1,0:T(8,128)S(1)}, f32[2,256,128]{2,1,0:T(8,128)S(1)}, u32[]{:S(2)}, u32[]{:S(2)}) collective-permute-start(f32[2,256,128]{2,1,0:T(8,128)S(1)} %get-tuple-element.48), channel_id=1, source_target_pairs={{0,1},{1,0},{2,3},{3,2},{4,5},{5,4},{6,7},{7,6},{8,9},{9,8},{10,11... | collective-permute-start | bytes 786440 | tf_op jit(solution)/shard_map/ppermute | solution.py:327
  2.7 8.5 %collective-permute-start.3 = (f32[2,128,256]{2,1,0:T(8,128)S(1)}, f32[2,128,256]{2,1,0:T(8,128)S(1)}, u32[]{:S(2)}, u32[]{:S(2)}) collective-permute-start(f32[2,128,256]{2,1,0:T(8,128)S(1)} %fusion.1), channel_id=1, source_target_pairs={{0,16},{16,0},{1,17},{17,1},{2,18},{18,2},{3,19},{19,3},{4,20},{20... | collective-permute-start | bytes 786440 | tf_op jit(solution)/shard_map/ppermute | solution.py:327
  4.0 13.0 %collective-permute-start.1 = (f32[2,256,128]{2,1,0:T(8,128)S(1)}, f32[2,256,128]{2,1,0:T(8,128)S(1)}, u32[]{:S(2)}, u32[]{:S(2)}) collective-permute-start(f32[2,256,128]{2,1,0:T(8,128)S(1)} %get-tuple-element.47), channel_id=1, source_target_pairs={{1,2},{2,1},{3,4},{4,3},{5,6},{6,5},{7,8},{8,7},{9,10},{10,9},{11,... | collective-permute-start | bytes 786440 | tf_op jit(solution)/shard_map/ppermute | solution.py:327
  10.9 5.0 %collective-permute-start.4 = (f32[256,128]{1,0:T(8,128)S(1)}, f32[256,128]{1,0:T(8,128)S(1)}, u32[]{:S(2)}, u32[]{:S(2)}) collective-permute-start(f32[256,128]{1,0:T(8,128)S(1)} %get-tuple-element.35), channel_id=1, source_target_pairs={{0,16},{16,0},{1,17},{17,1},{2,18},{18,2},{3,19},{19,3},{4,20},{20... | collective-permute-start | bytes 393224 | tf_op jit(solution)/shard_map/ppermute | solution.py:327
  16.0 12.4 %collective-permute-start.5 = (f32[384,128]{1,0:T(8,128)S(1)}, f32[384,128]{1,0:T(8,128)S(1)}, u32[]{:S(2)}, u32[]{:S(2)}) collective-permute-start(f32[384,128]{1,0:T(8,128)S(1)} %get-tuple-element.42), channel_id=1, source_target_pairs={{0,1},{1,0},{2,3},{3,2},{4,5},{5,4},{6,7},{7,6},{8,9},{9,8},{10,11... | collective-permute-start | bytes 589832 | tf_op jit(solution)/shard_map/ppermute | solution.py:327
  19.0 5.1 %collective-permute-start.2 = (f32[256,128]{1,0:T(8,128)S(1)}, f32[256,128]{1,0:T(8,128)S(1)}, u32[]{:S(2)}, u32[]{:S(2)}) collective-permute-start(f32[256,128]{1,0:T(8,128)S(1)} %get-tuple-element.29), channel_id=1, source_target_pairs={{0,16},{16,0},{1,17},{17,1},{2,18},{18,2},{3,19},{19,3},{4,20},{20... | collective-permute-start | bytes 393224 | tf_op jit(solution)/shard_map/ppermute | solution.py:327
  19.3 11.3 %collective-permute-start.6 = (f32[128,128]{1,0:T(8,128)S(1)}, f32[128,128]{1,0:T(8,128)S(1)}, u32[]{:S(2)}, u32[]{:S(2)}) collective-permute-start(f32[128,128]{1,0:T(8,128)S(1)} %get-tuple-element.45), channel_id=1, source_target_pairs={{1,2},{2,1},{3,4},{4,3},{5,6},{6,5},{7,8},{8,7},{9,10},{10,9},{11,... | collective-permute-start | bytes 196616 | tf_op jit(solution)/shard_map/ppermute | solution.py:327
  24.2 7.7 %collective-permute-start.7 = (f32[256,128]{1,0:T(8,128)S(1)}, f32[256,128]{1,0:T(8,128)S(1)}, u32[]{:S(2)}, u32[]{:S(2)}) collective-permute-start(f32[256,128]{1,0:T(8,128)S(1)} %get-tuple-element.46), channel_id=1, source_target_pairs={{1,2},{2,1},{3,4},{4,3},{5,6},{6,5},{7,8},{8,7},{9,10},{10,9},{11,... | collective-permute-start | bytes 393224 | tf_op jit(solution)/shard_map/ppermute | solution.py:327

commit v6 on v5

--- a/solution.py
+++ b/solution.py
@@ -226,14 +226,14 @@
     return jnp.concatenate(rows, axis=0)
 
 
-def gradient_half(spectra, value, basis, basis_t, other, tile, layers):
+def gradient_half(spectra, value, basis, basis_t, other, tile, layers, pieces=(ALL,)):
     low, high = slice(0, tile), slice(tile, 2 * tile)
     table = pair(basis, ALL, edge("gy", other))
     mixed = [wide_product(parts(scaled(spectra, layer, value, tile // 2)), table) for layer in range(layers)]
     mixed = jnp.concatenate(mixed, axis=1)
-    return product(pair(basis_t, ALL, low), parts(mixed[low])) + product(
-        pair(basis_t, ALL, high), parts(mixed[high])
-    )
+    even, odd = parts(mixed[low]), parts(mixed[high])
+    for rows in pieces:
+        yield rows, product(pair(basis_t, rows, low), even) + product(pair(basis_t, rows, high), odd)
 
 
 def own_kernel(tile, *refs):
@@ -276,7 +276,8 @@
         wrapped[:, halo("gy", phase)] = strip_rows(ref[:tile], corner[...], basis, tile)
     field[:, low] = product(parts(rows_done[...] + wrapped[...]), pair(basis_t, ALL, low))
     field[:, high] = product(parts(rows_done[...] - wrapped[...]), pair(basis_t, ALL, high))
-    result[...] = gradient_half(spectra, field, basis, basis_t, 0, tile, layers)
+    for rows, value in gradient_half(spectra, field, basis, basis_t, 0, tile, layers):
+        result[rows] = value
 
 
 def adjoint_kernel(xs, crossing, early, tile, layers, spectra, field, far, *refs):
@@ -286,14 +287,14 @@
     low, high = slice(0, tile), slice(tile, 2 * tile)
     copies = []
 
-    def put(source, first, other):
+    def put(source, rows, other):
         for layer in range(layers):
-            here = source.at[:, layer * RADIUS : (layer + 1) * RADIUS]
-            there = gradient.at[layer, :, edge("gy", other)]
-            copies.append(pltpu.make_async_copy(here, there, sems.at[first + layer]))
+            here = source.at[rows, layer * RADIUS : (layer + 1) * RADIUS]
+            there = gradient.at[layer, rows, edge("gy", other)]
+            copies.append(pltpu.make_async_copy(here, there, sems.at[len(copies)]))
             copies[-1].start()
 
-    put(far, 0, 0)
+    put(far, slice(0, tile), 0)
     for ref, phase in zip(strips, crossing):
         if len(xs) < 2:
             corner[...] = jnp.zeros_like(corner)
@@ -311,8 +312,11 @@
         value = jnp.dot(both, upper, preferred_element_type=F32) + jnp.dot(both, lower, preferred_element_type=F32)
         held[:, low] = field[:, low] + value[:, low]
         held[:, high] = field[:, high] - value[:, high]
-    result[...] = gradient_half(spectra, held if crossing else field, basis, basis_t, 1, tile, layers)
-    put(result, layers, 1)
+    total = held if crossing else field
+    pieces = [slice(start, start + tile // 2) for start in range(0, tile, tile // 2)]
+    for rows, value in gradient_half(spectra, total, basis, basis_t, 1, tile, layers, pieces):
+        result[rows] = value
+        put(result, rows, 1)
     for copy in copies:
         copy.wait()
 
@@ -449,7 +453,7 @@
         + [
             pltpu.VMEM((2 * tile, 2 * tile), F32),
             pltpu.VMEM((tile, layers * RADIUS), F32),
-            pltpu.SemaphoreType.DMA((2 * layers,)),
+            pltpu.SemaphoreType.DMA((3 * layers,)),
         ],
         compiler_params=PARAMS,
         cost_estimate=cost(12, tile),

time: 34.6 us -> 34.2 us (0.988)
    pallas_call x1, Pallas kernels: 2.54 us -> 2.19 us  [body(): pl.pallas_call(functools.partial(adjoint_kernel, xs, crossing, early, til...]
  transfers between devices with their start and end apart: 8 -> 8, of which waited for: 3 -> 3; matrix products, arithmetic and copies ran while one was open for 0% -> 0% of each run, Pallas kernels for 25% -> 26%
where the time goes in v6:
time: 34.2 us; the launch traced here: 34 us
  starting transfers between devices  13 us (38%)
  Pallas kernels  10.9 us (32%)
  waiting for transfers between devices  8.09 us (24%)
  other arithmetic  1.26 us (4%)
  between operations  0.84 us (2%)
    ppermute x8, starting transfers between devices, swap(): lax.ppermute(value, axis, [link for link in links if 0 <= link[1] < count])  13 us
    ppermute x8, waiting for transfers between devices, swap(): lax.ppermute(value, axis, [link for link in links if 0 <= link[1] < count])  8.09 us
    pallas_call x1, Pallas kernels, body(): pl.pallas_call(functools.partial(prepare_kernel, xs, paired, tile, layers...  3.47 us
    pallas_call x1, Pallas kernels, body(): pl.pallas_call(functools.partial(adjoint_kernel, xs, crossing, early, til...  2.19 us
    pallas_call x1, Pallas kernels, body(): pl.pallas_call(functools.partial(far_kernel, xs, paired, tile, layers), o...  2.06 us
    pallas_call x1, Pallas kernels, body(): pl.pallas_call(functools.partial(forward_kernel, xs, crossing, early, til...  1.94 us
    select_n x1, other arithmetic, cols_of(): return jnp.where(upper, density[..., tile - RADIUS:], density[..., :RADIUS])  1.2 us
    pallas_call x1, Pallas kernels, body(): pl.pallas_call(functools.partial(own_kernel, tile), out_shape=[array(tile...  1.06 us
  transfers between devices with their start and end apart: 8, of which 3 were waited for; matrix products, arithmetic and copies ran while one was open for 0% of the time, Pallas kernels for 26%

profile of v6, /device:TPU:17, one launch (start us, length us, event | category | flops | bytes accessed | tf_op | source)
XLA Modules:
  0.0 34.0 jit_solution(5466527956106931973)
XLA Ops:
  0.6 0.0 copy-start
  0.6 0.0 copy-start.1
  0.7 0.0 copy-start.2
  0.7 0.0 copy-start.3
  0.7 0.0 copy-start.4
  0.7 0.0 copy-start.5
  0.7 0.0 copy-start.6
  0.7 1.2 %slice_select_fusion = (f32[2,256,128]{2,1,0:T(8,128)S(1)}, f32[2,256,128]{2,1,0:T(8,128)S(1)}) fusion(f32[2,256,256]{2,1,0:T(8,128)} %refs_4_.4, pred[]{:T(512)S(6)} %eq.10, pred[]{:T(512)S(6)} %eq.9), kind=kLoop, calls=%fused_computation.6 | loop fusion | flops 131072 | bytes 1048578 | tf_op jit(solution)/shard_map/jit(_where)/select_n | solution.py:361
  1.9 0.7 %collective-permute-start = (f32[2,256,128]{2,1,0:T(8,128)S(1)}, f32[2,256,128]{2,1,0:T(8,128)S(1)}, u32[]{:S(2)}, u32[]{:S(2)}) collective-permute-start(f32[2,256,128]{2,1,0:T(8,128)S(1)} %get-tuple-element.48), channel_id=1, source_target_pairs={{0,1},{1,0},{2,3},{3,2},{4,5},{5,4},{6,7},{7,6},{8,9},{9,8},{10,11... | collective-permute-start | bytes 786440 | tf_op jit(solution)/shard_map/ppermute | solution.py:331
  2.7 0.0 copy-done
  2.7 0.0 copy-done.1
  2.7 1.3 %collective-permute-start.3 = (f32[2,128,256]{2,1,0:T(8,128)S(1)}, f32[2,128,256]{2,1,0:T(8,128)S(1)}, u32[]{:S(2)}, u32[]{:S(2)}) collective-permute-start(f32[2,128,256]{2,1,0:T(8,128)S(1)} %fusion.1), channel_id=1, source_target_pairs={{0,16},{16,0},{1,17},{17,1},{2,18},{18,2},{3,19},{19,3},{4,20},{20... | collective-permute-start | bytes 786440 | tf_op jit(solution)/shard_map/ppermute | solution.py:331
  4.0 3.3 %collective-permute-start.1 = (f32[2,256,128]{2,1,0:T(8,128)S(1)}, f32[2,256,128]{2,1,0:T(8,128)S(1)}, u32[]{:S(2)}, u32[]{:S(2)}) collective-permute-start(f32[2,256,128]{2,1,0:T(8,128)S(1)} %get-tuple-element.47), channel_id=1, source_target_pairs={{1,2},{2,1},{3,4},{4,3},{5,6},{6,5},{7,8},{8,7},{9,10},{10,9},{11,... | collective-permute-start | bytes 786440 | tf_op jit(solution)/shard_map/ppermute | solution.py:331
  7.4 0.0 collective-permute-done.refs_5_
  7.4 0.0 copy-done.2
  7.4 0.0 copy-done.3
  7.4 0.0 copy-done.4
  7.4 0.0 copy-done.5
  7.4 0.0 copy-done.6
  7.4 3.5 %prepare.1 = (f32[2,384,384]{2,1,0:T(8,128)S(1)}, f32[512,512]{1,0:T(8,128)S(1)}, f32[256,128]{1,0:T(8,128)S(1)}, f32[256,128]{1,0:T(8,128)S(1)}, f32[256,128]{1,0:T(8,128)S(1)}) custom-call(s32[2]{0:T(128)} %index_source.1, bf16[384,256]{1,0:T(8,128)(2,1)} %constant.33.clone.refs_0_, bf16[384,256]{1,0:T(8,128)(2,1)} %constant.34.clone.refs_1_, ...), custom_call_target="tpu_custom_call" | custom-call | flops 2415919104 | bytes 1048576 | tf_op jit(solution)/shard_map/prepare/pallas_call | solution.py:376
  10.9 0.3 collective-permute-start.4
  11.2 0.0 collective-permute-done.3.refs_1_
  11.2 4.7 %collective-permute-done.4.refs_0_ = f32[256,128]{1,0:T(8,128)S(1)} collective-permute-done((f32[256,128]{1,0:T(8,128)S(1)}, f32[256,128]{1,0:T(8,128)S(1)}, u32[]{:S(2)}, u32[]{:S(2)}) %collective-permute-start.4) | collective-permute-done | bytes 131104 | tf_op jit(solution)/shard_map/ppermute | solution.py:331
  15.9 0.1 shard_map.140
  16.0 1.0 %collective-permute-start.5 = (f32[384,128]{1,0:T(8,128)S(1)}, f32[384,128]{1,0:T(8,128)S(1)}, u32[]{:S(2)}, u32[]{:S(2)}) collective-permute-start(f32[384,128]{1,0:T(8,128)S(1)} %get-tuple-element.42), channel_id=1, source_target_pairs={{0,1},{1,0},{2,3},{3,2},{4,5},{5,4},{6,7},{7,6},{8,9},{9,8},{10,11... | collective-permute-start | bytes 589832 | tf_op jit(solution)/shard_map/ppermute | solution.py:331
  17.0 0.0 collective-permute-done.1.refs_0_
  17.0 1.9 %forward.1 = (f32[256,128]{1,0:T(8,128)S(1)}, f32[256,128]{1,0:T(8,128)S(1)}, f32[256,128]{1,0:T(8,128)S(1)}, f32[128,128]{1,0:T(8,128)S(1)}) custom-call(f32[2,384,384]{2,1,0:T(8,128)S(1)} %get-tuple-element.25.spectra, f32[512,512]{1,0:T(8,128)S(1)} %get-tuple-element.26.before, f32[256,256]{1,0:T(8,128)S(1)} %copy-done.1, s32[256,256]{1,0:T(8,128)S(1)} %copy-done, ...), custom_call_target="tpu_custom_call" | custom-call | flops 1207959552 | bytes 1048576 | tf_op jit(solution)/shard_map/forward/pallas_call | solution.py:395
  19.0 0.3 collective-permute-start.2
  19.3 2.8 %collective-permute-start.6 = (f32[128,128]{1,0:T(8,128)S(1)}, f32[128,128]{1,0:T(8,128)S(1)}, u32[]{:S(2)}, u32[]{:S(2)}) collective-permute-start(f32[128,128]{1,0:T(8,128)S(1)} %get-tuple-element.45), channel_id=1, source_target_pairs={{1,2},{2,1},{3,4},{4,3},{5,6},{6,5},{7,8},{8,7},{9,10},{10,9},{11,... | collective-permute-start | bytes 196616 | tf_op jit(solution)/shard_map/ppermute | solution.py:331
  22.1 2.0 %collective-permute-done.2.refs_0_ = f32[256,128]{1,0:T(8,128)S(1)} collective-permute-done((f32[256,128]{1,0:T(8,128)S(1)}, f32[256,128]{1,0:T(8,128)S(1)}, u32[]{:S(2)}, u32[]{:S(2)}) %collective-permute-start.2) | collective-permute-done | bytes 131104 | tf_op jit(solution)/shard_map/ppermute | solution.py:331
  24.1 0.1 shard_map.139
  24.2 3.2 %collective-permute-start.7 = (f32[256,128]{1,0:T(8,128)S(1)}, f32[256,128]{1,0:T(8,128)S(1)}, u32[]{:S(2)}, u32[]{:S(2)}) collective-permute-start(f32[256,128]{1,0:T(8,128)S(1)} %get-tuple-element.46), channel_id=1, source_target_pairs={{1,2},{2,1},{3,4},{4,3},{5,6},{6,5},{7,8},{8,7},{9,10},{10,9},{11,... | collective-permute-start | bytes 393224 | tf_op jit(solution)/shard_map/ppermute | solution.py:331
  27.4 1.1 %own.1 = (f32[256,256]{1,0:T(8,128)}, f32[256,256]{1,0:T(8,128)}, f32[512,256]{1,0:T(8,128)S(1)}) custom-call(f32[256,128]{1,0:T(8,128)S(1)} %get-tuple-element.30.refs_0_, f32[256,128]{1,0:T(8,128)S(1)} %get-tuple-element.31.refs_1_, f32[256,128]{1,0:T(8,128)S(1)} %get-tuple-element.32.refs_2_, f32[256,128]{1,0:T(8,128)S(1)} %get-tuple-element.36.refs_3_, ...), custom_call_target="tpu_custom_call" | custom-call | flops 201326592 | bytes 1048576 | tf_op jit(solution)/shard_map/own/pallas_call | solution.py:425
  28.4 0.0 collective-permute-done.5.refs_0_
  28.4 2.1 %far.1 = (f32[512,512]{1,0:T(8,128)S(1)}, f32[256,256]{1,0:T(8,128)S(1)}) custom-call(f32[2,384,384]{2,1,0:T(8,128)S(1)} %get-tuple-element.25.spectra, f32[512,256]{1,0:T(8,128)S(1)} %get-tuple-element.41.rows_done, f32[384,128]{1,0:T(8,128)S(1)} %collective-permute-done.5.refs_0_, bf16[512,256]{1,0:T(8,128)(2,1)S(1)} %copy-done.4, ...), custom_call_target="tpu_custom_call" | custom-call | flops 1409286144 | bytes 1048576 | tf_op jit(solution)/shard_map/far/pallas_call | solution.py:436
  30.5 0.0 collective-permute-done.6.refs_0_
  30.5 1.3 %collective-permute-done.7.refs_1_ = f32[256,128]{1,0:T(8,128)S(1)} collective-permute-done((f32[256,128]{1,0:T(8,128)S(1)}, f32[256,128]{1,0:T(8,128)S(1)}, u32[]{:S(2)}, u32[]{:S(2)}) %collective-permute-start.7) | collective-permute-done | bytes 131104 | tf_op jit(solution)/shard_map/ppermute | solution.py:331
  31.9 2.2 %adjoint.1 = f32[2,256,256]{2,1,0:T(8,128)} custom-call(f32[2,384,384]{2,1,0:T(8,128)S(1)} %get-tuple-element.25.spectra, f32[512,512]{1,0:T(8,128)S(1)} %get-tuple-element.43.field, f32[256,256]{1,0:T(8,128)S(1)} %get-tuple-element.44.far, f32[128,128]{1,0:T(8,128)S(1)} %collective-permute-done.6.refs_0_, f32[256,128]{1,0:T(8,128)S(1)} %collective-permute-done.7.refs_1_, ...), custom_call_target="tpu_custom_call" | custom-call | flops 1207959552 | bytes 1048576 | tf_op jit(solution)/shard_map/adjoint/pallas_call | solution.py:447
  (2 shorter events, 0.1 us)
Async XLA Ops:
  0.6 2.0 %copy-start = (s32[256,256]{1,0:T(8,128)S(1)}, s32[256,256]{1,0:T(8,128)}, u32[]{:S(2)}) copy-start(s32[256,256]{1,0:T(8,128)} %stations.5) | copy-start | bytes 786436
  0.6 2.0 %copy-start.1 = (f32[256,256]{1,0:T(8,128)S(1)}, f32[256,256]{1,0:T(8,128)}, u32[]{:S(2)}) copy-start(f32[256,256]{1,0:T(8,128)} %observed.5) | copy-start | bytes 786436
  0.7 6.7 %copy-start.2 = (f32[2,256,256]{2,1,0:T(8,128)S(1)}, f32[2,256,256]{2,1,0:T(8,128)}, u32[]{:S(2)}) copy-start(f32[2,256,256]{2,1,0:T(8,128)} %refs_4_.4) | copy-start | bytes 1572868
  0.7 6.7 %copy-start.3 = (bf16[512,256]{1,0:T(8,128)(2,1)S(1)}, bf16[512,256]{1,0:T(8,128)(2,1)}, u32[]{:S(2)}) copy-start(bf16[512,256]{1,0:T(8,128)(2,1)} %constant.30.clone.refs_7_.refs_2_.refs_3_) | copy-start | bytes 786436
  0.7 6.7 %copy-start.4 = (bf16[512,256]{1,0:T(8,128)(2,1)S(1)}, bf16[512,256]{1,0:T(8,128)(2,1)}, u32[]{:S(2)}) copy-start(bf16[512,256]{1,0:T(8,128)(2,1)} %constant.29.clone.refs_6_.refs_1_.refs_2_) | copy-start | bytes 786436
  0.7 6.7 %copy-start.5 = (bf16[256,512]{1,0:T(8,128)(2,1)S(1)}, bf16[256,512]{1,0:T(8,128)(2,1)}, u32[]{:S(2)}) copy-start(bf16[256,512]{1,0:T(8,128)(2,1)} %constant.32.clone.refs_9_.refs_4_.refs_5_) | copy-start | bytes 786436
  0.7 6.7 %copy-start.6 = (bf16[256,512]{1,0:T(8,128)(2,1)S(1)}, bf16[256,512]{1,0:T(8,128)(2,1)}, u32[]{:S(2)}) copy-start(bf16[256,512]{1,0:T(8,128)(2,1)} %constant.31.clone.refs_8_.refs_3_.refs_4_) | copy-start | bytes 786436
  1.9 5.4 %collective-permute-start = (f32[2,256,128]{2,1,0:T(8,128)S(1)}, f32[2,256,128]{2,1,0:T(8,128)S(1)}, u32[]{:S(2)}, u32[]{:S(2)}) collective-permute-start(f32[2,256,128]{2,1,0:T(8,128)S(1)} %get-tuple-element.48), channel_id=1, source_target_pairs={{0,1},{1,0},{2,3},{3,2},{4,5},{5,4},{6,7},{7,6},{8,9},{9,8},{10,11... | collective-permute-start | bytes 786440 | tf_op jit(solution)/shard_map/ppermute | solution.py:331
  2.7 8.5 %collective-permute-start.3 = (f32[2,128,256]{2,1,0:T(8,128)S(1)}, f32[2,128,256]{2,1,0:T(8,128)S(1)}, u32[]{:S(2)}, u32[]{:S(2)}) collective-permute-start(f32[2,128,256]{2,1,0:T(8,128)S(1)} %fusion.1), channel_id=1, source_target_pairs={{0,16},{16,0},{1,17},{17,1},{2,18},{18,2},{3,19},{19,3},{4,20},{20... | collective-permute-start | bytes 786440 | tf_op jit(solution)/shard_map/ppermute | solution.py:331
  4.0 13.0 %collective-permute-start.1 = (f32[2,256,128]{2,1,0:T(8,128)S(1)}, f32[2,256,128]{2,1,0:T(8,128)S(1)}, u32[]{:S(2)}, u32[]{:S(2)}) collective-permute-start(f32[2,256,128]{2,1,0:T(8,128)S(1)} %get-tuple-element.47), channel_id=1, source_target_pairs={{1,2},{2,1},{3,4},{4,3},{5,6},{6,5},{7,8},{8,7},{9,10},{10,9},{11,... | collective-permute-start | bytes 786440 | tf_op jit(solution)/shard_map/ppermute | solution.py:331
  10.9 5.0 %collective-permute-start.4 = (f32[256,128]{1,0:T(8,128)S(1)}, f32[256,128]{1,0:T(8,128)S(1)}, u32[]{:S(2)}, u32[]{:S(2)}) collective-permute-start(f32[256,128]{1,0:T(8,128)S(1)} %get-tuple-element.35), channel_id=1, source_target_pairs={{0,16},{16,0},{1,17},{17,1},{2,18},{18,2},{3,19},{19,3},{4,20},{20... | collective-permute-start | bytes 393224 | tf_op jit(solution)/shard_map/ppermute | solution.py:331
  16.0 12.4 %collective-permute-start.5 = (f32[384,128]{1,0:T(8,128)S(1)}, f32[384,128]{1,0:T(8,128)S(1)}, u32[]{:S(2)}, u32[]{:S(2)}) collective-permute-start(f32[384,128]{1,0:T(8,128)S(1)} %get-tuple-element.42), channel_id=1, source_target_pairs={{0,1},{1,0},{2,3},{3,2},{4,5},{5,4},{6,7},{7,6},{8,9},{9,8},{10,11... | collective-permute-start | bytes 589832 | tf_op jit(solution)/shard_map/ppermute | solution.py:331
  19.0 5.1 %collective-permute-start.2 = (f32[256,128]{1,0:T(8,128)S(1)}, f32[256,128]{1,0:T(8,128)S(1)}, u32[]{:S(2)}, u32[]{:S(2)}) collective-permute-start(f32[256,128]{1,0:T(8,128)S(1)} %get-tuple-element.29), channel_id=1, source_target_pairs={{0,16},{16,0},{1,17},{17,1},{2,18},{18,2},{3,19},{19,3},{4,20},{20... | collective-permute-start | bytes 393224 | tf_op jit(solution)/shard_map/ppermute | solution.py:331
  19.3 11.3 %collective-permute-start.6 = (f32[128,128]{1,0:T(8,128)S(1)}, f32[128,128]{1,0:T(8,128)S(1)}, u32[]{:S(2)}, u32[]{:S(2)}) collective-permute-start(f32[128,128]{1,0:T(8,128)S(1)} %get-tuple-element.45), channel_id=1, source_target_pairs={{1,2},{2,1},{3,4},{4,3},{5,6},{6,5},{7,8},{8,7},{9,10},{10,9},{11,... | collective-permute-start | bytes 196616 | tf_op jit(solution)/shard_map/ppermute | solution.py:331
  24.2 7.7 %collective-permute-start.7 = (f32[256,128]{1,0:T(8,128)S(1)}, f32[256,128]{1,0:T(8,128)S(1)}, u32[]{:S(2)}, u32[]{:S(2)}) collective-permute-start(f32[256,128]{1,0:T(8,128)S(1)} %get-tuple-element.46), channel_id=1, source_target_pairs={{1,2},{2,1},{3,4},{4,3},{5,6},{6,5},{7,8},{8,7},{9,10},{10,9},{11,... | collective-permute-start | bytes 393224 | tf_op jit(solution)/shard_map/ppermute | solution.py:331
